TPU v7x, 32 devices: a 4x4x1 block of a 4x4x8 slice. The times are simulated.
32 devices in a mesh: dp: 1 (over z), ing: 4 (over y), grp: 8 (over x, core).
Axes of the slice: x: 4, y: 4, z: 1, core: 2. Of those that a mesh axis runs over, the one named last changes fastest.
The devices are a block of a 4x4x8 slice.
Arguments:
- x_tokens: bfloat16 [32768, 1024], P(('dp', 'grp', 'ing'))
- expert_ids: int32 [32768, 8], P(('dp', 'grp', 'ing'))
- gate_vals: float32 [32768, 8], P(('dp', 'grp', 'ing'))
- y_grad: bfloat16 [32768, 1024], P(('dp', 'grp', 'ing'))
- w_gate: bfloat16 [32, 1024, 512], P(('grp', 'ing'))
- w_up: bfloat16 [32, 1024, 512], P(('grp', 'ing'))
- w_down: bfloat16 [32, 512, 1024], P(('grp', 'ing'))
Outputs:
- output 1: bfloat16 [32768, 1024], P(('dp', 'grp', 'ing'))
- output 2: bfloat16 [32768, 1024], P(('dp', 'grp', 'ing'))
- output 3: float32 [32, 1024, 512], P(('dp', 'grp', 'ing'))
- output 4: float32 [32, 1024, 512], P(('dp', 'grp', 'ing'))
- output 5: float32 [32, 512, 1024], P(('dp', 'grp', 'ing'))
All inputs are finite; a program needn't handle non-finite values.
Results may differ from a plain program's by a relative error of at most 0.00889638.
Values are sent between devices in bfloat16 or wider.
A program may use at most 768 MiB of HBM per device.

v0:
```python
import jax
import jax.numpy as jnp
from jax import lax
from jax.sharding import PartitionSpec as P


def source_tables(ids_loc, groups, per_group, grp_cap):
    tokens, top_k = ids_loc.shape
    tok_group = ids_loc // per_group
    earlier = jnp.tril(jnp.ones((top_k, top_k), dtype=bool), -1)
    is_first = ~jnp.any((tok_group[:, :, None] == tok_group[:, None, :]) & earlier[None], axis=2)
    member = jnp.any(tok_group[:, :, None] == jnp.arange(groups)[None, None, :], axis=1).astype(jnp.int32)
    grp_pos = jnp.cumsum(member, axis=0) - 1
    grp_count = grp_pos[-1] + 1
    send_slot = jnp.where(member > 0, jnp.arange(groups)[None, :] * grp_cap + grp_pos, groups * grp_cap)
    tok_index = jnp.broadcast_to(jnp.arange(tokens, dtype=jnp.int32)[:, None], (tokens, groups))
    send_tok = jnp.zeros((groups * grp_cap,), jnp.int32).at[send_slot.reshape(-1)].set(tok_index.reshape(-1), mode='drop')
    send_valid = (jnp.arange(grp_cap)[None, :] < grp_count[:, None]).reshape(-1)
    ret_row = tok_group * grp_cap + jnp.take_along_axis(grp_pos, tok_group, axis=1)
    return send_tok, send_valid, is_first, ret_row


def expert_stage(recv_x, recv_dy, recv_ids, recv_gates, weights, my_group, inner, in_cap):
    wg_loc, wu_loc, wd_loc = weights
    local_exp = wg_loc.shape[0]
    hidden = wg_loc.shape[1]
    per_group = local_exp * inner
    recv_rows, top_k = recv_ids.shape
    in_group = (recv_ids // per_group) == my_group
    loc_exp = jnp.where(in_group, recv_ids - my_group * per_group, per_group)
    exp_hit = jnp.any(loc_exp[:, :, None] == jnp.arange(per_group)[None, None, :], axis=1).astype(jnp.int32)
    exp_pos = jnp.cumsum(exp_hit, axis=0) - 1
    pick_pos = jnp.take_along_axis(exp_pos, jnp.minimum(loc_exp, per_group - 1), axis=1)
    fwd_slot = jnp.where(in_group, loc_exp * in_cap + pick_pos, per_group * in_cap)
    row_index = jnp.broadcast_to(jnp.arange(recv_rows, dtype=jnp.int32)[:, None], (recv_rows, top_k))
    fwd_src = jnp.zeros((per_group * in_cap,), jnp.int32).at[fwd_slot.reshape(-1)].set(row_index.reshape(-1), mode='drop')
    fwd_gate = jnp.zeros((per_group * in_cap,), jnp.float32).at[fwd_slot.reshape(-1)].set(recv_gates.reshape(-1), mode='drop')
    buf_shape = (inner, local_exp, in_cap, hidden)
    fwd_x = recv_x[fwd_src].reshape(buf_shape)
    fwd_do = (fwd_gate[:, None] * recv_dy[fwd_src].astype(jnp.float32)).astype(jnp.bfloat16).reshape(buf_shape)
    exp_x = lax.all_to_all(fwd_x, 'ing', 0, 0, tiled=True)
    exp_do = lax.all_to_all(fwd_do, 'ing', 0, 0, tiled=True)
    h_gate = jnp.einsum('blcd,ldf->blcf', exp_x, wg_loc, preferred_element_type=jnp.float32)
    h_up = jnp.einsum('blcd,ldf->blcf', exp_x, wu_loc, preferred_element_type=jnp.float32)
    sig_gate = jax.nn.sigmoid(h_gate)
    silu_gate = h_gate * sig_gate
    act_bf = (silu_gate * h_up).astype(jnp.bfloat16)
    out_bf = jnp.einsum('blcf,lfd->blcd', act_bf, wd_loc, preferred_element_type=jnp.float32).astype(jnp.bfloat16)
    d_act = jnp.einsum('blcd,lfd->blcf', exp_do, wd_loc, preferred_element_type=jnp.float32)
    d_hgate = (d_act * h_up * sig_gate * (1.0 + h_gate * (1.0 - sig_gate))).astype(jnp.bfloat16)
    d_hup = (d_act * silu_gate).astype(jnp.bfloat16)
    dx_bf = (jnp.einsum('blcf,ldf->blcd', d_hgate, wg_loc, preferred_element_type=jnp.float32) + jnp.einsum('blcf,ldf->blcd', d_hup, wu_loc, preferred_element_type=jnp.float32)).astype(jnp.bfloat16)
    grad_gate = jnp.einsum('blcd,blcf->ldf', exp_x, d_hgate, preferred_element_type=jnp.float32)
    grad_up = jnp.einsum('blcd,blcf->ldf', exp_x, d_hup, preferred_element_type=jnp.float32)
    grad_down = jnp.einsum('blcf,blcd->lfd', act_bf, exp_do, preferred_element_type=jnp.float32)
    back_out = lax.all_to_all(out_bf, 'ing', 0, 0, tiled=True).reshape(per_group * in_cap, hidden)
    back_dx = lax.all_to_all(dx_bf, 'ing', 0, 0, tiled=True).reshape(per_group * in_cap, hidden)
    take_slot = jnp.minimum(fwd_slot, per_group * in_cap - 1)
    mix_gate = jnp.where(in_group, recv_gates, 0.0)
    grp_y = jnp.sum(mix_gate[:, :, None] * back_out[take_slot].astype(jnp.float32), axis=1).astype(jnp.bfloat16)
    grp_dx = jnp.sum(jnp.where(in_group[:, :, None], back_dx[take_slot].astype(jnp.float32), 0.0), axis=1).astype(jnp.bfloat16)
    return grp_y, grp_dx, (grad_gate, grad_up, grad_down)


def solution(mesh):
    groups = mesh.shape['grp']
    inner = mesh.shape['ing']
    tok_spec = P(('dp', 'grp', 'ing'), None)
    weight_spec = P(('grp', 'ing'), None, None)
    grad_spec = P(('dp', 'grp', 'ing'), None, None)

    def device_fn(x_loc, ids_loc, gates_loc, dy_loc, wg_loc, wu_loc, wd_loc):
        tokens, hidden = x_loc.shape
        top_k = ids_loc.shape[1]
        per_group = wg_loc.shape[0] * inner
        num_exp = per_group * groups
        group_limit = min(max(1, groups // 2), top_k // 2)
        grp_cap = tokens * group_limit // groups
        in_cap = groups * (3 * tokens * top_k // (2 * num_exp))
        my_group = lax.axis_index('grp')
        send_tok, send_valid, is_first, ret_row = source_tables(ids_loc, groups, per_group, grp_cap)
        send_x = x_loc[send_tok].reshape(groups, grp_cap, hidden)
        send_dy = dy_loc[send_tok].reshape(groups, grp_cap, hidden)
        send_ids = jnp.where(send_valid[:, None], ids_loc[send_tok], -1).reshape(groups, grp_cap, top_k)
        send_gates = gates_loc[send_tok].reshape(groups, grp_cap, top_k)
        recv_x = lax.all_to_all(send_x, 'grp', 0, 0, tiled=True).reshape(groups * grp_cap, hidden)
        recv_dy = lax.all_to_all(send_dy, 'grp', 0, 0, tiled=True).reshape(groups * grp_cap, hidden)
        recv_ids = lax.all_to_all(send_ids, 'grp', 0, 0, tiled=True).reshape(groups * grp_cap, top_k)
        recv_gates = lax.all_to_all(send_gates, 'grp', 0, 0, tiled=True).reshape(groups * grp_cap, top_k)
        grp_y, grp_dx, grad_list = expert_stage(recv_x, recv_dy, recv_ids, recv_gates, (wg_loc, wu_loc, wd_loc), my_group, inner, in_cap)
        ret_y = lax.all_to_all(grp_y.reshape(groups, grp_cap, hidden), 'grp', 0, 0, tiled=True).reshape(groups * grp_cap, hidden)
        ret_dx = lax.all_to_all(grp_dx.reshape(groups, grp_cap, hidden), 'grp', 0, 0, tiled=True).reshape(groups * grp_cap, hidden)
        y_out = jnp.sum(jnp.where(is_first[:, :, None], ret_y[ret_row].astype(jnp.float32), 0.0), axis=1).astype(jnp.bfloat16)
        dx_out = jnp.sum(jnp.where(is_first[:, :, None], ret_dx[ret_row].astype(jnp.float32), 0.0), axis=1).astype(jnp.bfloat16)
        return y_out, dx_out, grad_list[0], grad_list[1], grad_list[2]

    return jax.shard_map(device_fn, mesh=mesh, in_specs=(tok_spec, tok_spec, tok_spec, tok_spec, weight_spec, weight_spec, weight_spec), out_specs=(tok_spec, tok_spec, grad_spec, grad_spec, grad_spec), check_vma=False)
```

profile of v0, /device:TPU:97, one launch (start us, length us, event | category | flops | bytes accessed | tf_op | source)
XLA Modules:
  0.0 2481.8 jit_solution(3167363668322915598)
XLA Ops:
  7.1 30.5 %scatter_custom_fusion = s32[4096]{0:T(1024)S(1)} fusion(s32[8192]{0:T(1024)S(1)} %bitcast.261, s32[8192]{0:T(1024)S(1)} %reshape.711, s32[]{:T(128)} %constant.42.clone.1), kind=kCustom, calls=%fused_computation.143 | custom fusion | bytes 16388 | tf_op jit(solution)/shard_map/scatter | solution.py:17
  37.6 14.2 gather_fusion.1
  61.1 14.2 gather_fusion
  83.0 18.2 gather_fusion.6
  111.4 18.2 gather_fusion.2
  150.5 273.6 %gather_fusion.10 = s32[32768]{0:T(1024)S(1)} fusion(s32[4096,4]{0,1:T(4,128)S(1)} %bitcast.243, s32[32768]{0:T(1024)S(1)} %reshape.695), kind=kCustom, calls=%fused_computation.10 | custom fusion | bytes 524288 | tf_op jit(solution)/shard_map/jit(take_along_axis)/gather | solution.py:33
  430.6 120.8 %scatter_custom_fusion.2 = f32[12288]{0:T(1024)S(1)} fusion(s32[32768]{0:T(1024)S(1)} %bitcast.259, f32[32768]{0:T(1024)} %reshape.727, f32[]{:T(128)} %constant.60.clone.1), kind=kCustom, calls=%fused_computation.136 | custom fusion | bytes 49664 | tf_op jit(solution)/shard_map/scatter | solution.py:37
  551.4 120.4 %scatter_custom_fusion.1 = s32[12288]{0:T(1024)S(1)} fusion(s32[32768]{0:T(1024)S(1)} %bitcast.260, s32[32768]{0:T(1024)} %reshape.719, s32[]{:T(128)} %constant.42.clone.1), kind=kCustom, calls=%fused_computation.138 | custom fusion | bytes 49664 | tf_op jit(solution)/shard_map/scatter | solution.py:36
  671.9 64.9 %gather_fusion.7 = bf16[12288,1024]{1,0:T(8,128)(2,1)} fusion(bf16[4096,1024]{1,0:T(8,128)(2,1)} %bitcast.44, s32[12288]{0:T(1024)S(1)} %fusion.60), kind=kCustom, calls=%fused_computation.7 | custom fusion | bytes 50380800 | tf_op jit(solution)/shard_map/gather | solution.py:40
  736.7 21.8 fusion.2
  767.1 64.9 %gather_fusion.3 = bf16[12288,1024]{1,0:T(8,128)(2,1)} fusion(bf16[4096,1024]{1,0:T(8,128)(2,1)} %bitcast.9, s32[12288]{0:T(1024)S(1)} %fusion.60), kind=kCustom, calls=%fused_computation.3 | custom fusion | bytes 50380800 | tf_op jit(solution)/shard_map/gather | solution.py:39
  832.0 209.9 %all-to-all-done.7 = bf16[4,1,3072,1024]{3,2,1,0:T(8,128)(2,1)} async-done(((bf16[4,1,3072,1024]{3,2,1,0:T(8,128)(2,1)}), bf16[4,1,3072,1024]{3,2,1,0:T(8,128)(2,1)}, u32[]{:S(2)}, u32[]{:S(2)}) %all-to-all-start.7) | async-done | bytes 25165856 | tf_op jit(solution)/shard_map/all_to_all | solution.py:42
  1050.7 22.7 fusion.12
  1073.3 249.8 %all-to-all-done.3 = bf16[4,1,3072,1024]{3,2,1,0:T(8,128)(2,1)} async-done(((bf16[4,1,3072,1024]{3,2,1,0:T(8,128)(2,1)}), bf16[4,1,3072,1024]{3,2,1,0:T(8,128)(2,1)}, u32[]{:S(2)}, u32[]{:S(2)}) %all-to-all-start.3) | async-done | bytes 25165856 | tf_op jit(solution)/shard_map/all_to_all | solution.py:41
  1323.2 22.7 fusion.22
  1345.8 45.2 %fusion.27 = (bf16[4,3072,512]{2,1,0:T(8,128)(2,1)}, bf16[4,1,3072,512]{3,2,0,1:T(8,128)(2,1)}, bf16[4,3072,512]{2,1,0:T(8,128)(2,1)}) fusion(f32[4,3072,512]{2,1,0:T(8,128)} %fusion.22, f32[4,3072,512]{2,1,0:T(8,128)} %fusion.12, bf16[1,1024,512]{2,1,0:T(8,128)(2,1)S(1)} %copy-done.17, bf16[4,1,3072,1024]{3,2,1,0:T(8,128)(2,1)} %all-to-all-done.3), kind=kOutput, calls=%fused_computation.55 | convolution fusion | flops 12979273728 | bytes 114294784 | tf_op jit(solution)/shard_map/blcd,ldf->blcf/dot_general | solution.py:43
  1391.0 24.7 fusion.30
  1415.7 29.6 %fusion.26 = bf16[4,1,3072,1024]{3,2,1,0:T(8,128)(2,1)} fusion(f32[4,3072,1024]{2,1,0:T(8,128)} %fusion.30, bf16[4,3072,512]{2,1,0:T(8,128)(2,1)} %get-tuple-element.13, bf16[1,1024,512]{2,1,0:T(8,128)(2,1)S(1)} %copy-done.18), kind=kOutput, calls=%fused_computation.54 | convolution fusion | flops 12910067712 | bytes 89128960 | tf_op jit(solution)/shard_map/blcf,ldf->blcd/dot_general | solution.py:52
  1453.8 21.2 convert_bitcast_fusion
  1475.0 250.4 %all-to-all-done.8 = bf16[4,1,3072,1024]{3,2,1,0:T(8,128)(2,1)} async-done(((bf16[4,1,3072,1024]{3,2,1,0:T(8,128)(2,1)}), bf16[4,1,3072,1024]{3,2,1,0:T(8,128)(2,1)}, u32[]{:S(2)}, u32[]{:S(2)}) %all-to-all-start.8) | async-done | bytes 25165856 | tf_op jit(solution)/shard_map/all_to_all | solution.py:57
  1743.9 170.6 %gather_fusion.8 = bf16[32768,1024]{1,0:T(8,128)(2,1)} fusion(bf16[12288,1024]{1,0:T(8,128)(2,1)} %bitcast.61, s32[32768]{0:T(1024)S(1)} %broadcast_clamp_fusion), kind=kCustom, calls=%fused_computation.8 | custom fusion | bytes 134348800 | tf_op jit(solution)/shard_map/gather | solution.py:61
  1914.5 54.0 %fusion = bf16[4096,1024]{1,0:T(8,128)(2,1)} fusion(bf16[32768,1024]{1,0:T(8,128)(2,1)} %gather_fusion.8, pred[4096,8]{1,0:T(8,128)(4,1)S(1)} %copy-done.7), kind=kLoop, calls=%fused_computation.16 | loop fusion | flops 96468992 | bytes 75530240 | tf_op jit(solution)/shard_map/reduce_sum | solution.py:61
  1968.5 36.2 %all-to-all-done.4 = bf16[4,1,3072,1024]{3,2,1,0:T(8,128)(2,1)} async-done(((bf16[4,1,3072,1024]{3,2,1,0:T(8,128)(2,1)}), bf16[4,1,3072,1024]{3,2,1,0:T(8,128)(2,1)}, u32[]{:S(2)}, u32[]{:S(2)}) %all-to-all-start.4) | async-done | bytes 25165856 | tf_op jit(solution)/shard_map/all_to_all | solution.py:56
  2015.6 170.6 %gather_fusion.4 = bf16[32768,1024]{1,0:T(8,128)(2,1)} fusion(bf16[12288,1024]{1,0:T(8,128)(2,1)} %bitcast.37, s32[32768]{0:T(1024)S(1)} %broadcast_clamp_fusion), kind=kCustom, calls=%fused_computation.4 | custom fusion | bytes 134348800 | tf_op jit(solution)/shard_map/gather | solution.py:60
  2186.2 53.3 %fusion.1 = bf16[4096,1024]{1,0:T(8,128)(2,1)} fusion(bf16[32768,1024]{1,0:T(8,128)(2,1)} %gather_fusion.4, f32[4096,8]{1,0:T(8,128)} %copy.84), kind=kLoop, calls=%fused_computation.18 | loop fusion | flops 96468992 | bytes 75628544 | tf_op jit(solution)/shard_map/reduce_sum | solution.py:60
  2246.5 48.5 %gather_fusion.11 = s32[8192]{0:T(1024)S(1)} fusion(s32[1024,8]{0,1:T(8,128)S(1)} %bitcast.245, s32[8192]{0:T(1024)S(1)} %reshape.701), kind=kCustom, calls=%fused_computation.11 | custom fusion | bytes 131072 | tf_op jit(solution)/shard_map/jit(take_along_axis)/gather | solution.py:19
  2296.0 21.1 fusion.45
  2317.2 21.1 fusion.40
  2338.3 21.3 fusion.37
  2359.6 45.1 %gather_fusion.9 = bf16[8192,1024]{1,0:T(8,128)(2,1)} fusion(bf16[4096,1024]{1,0:T(8,128)(2,1)} %bitcast.64, s32[8192]{0:T(1024)S(1)} %broadcast_clamp_fusion.1), kind=kCustom, calls=%fused_computation.9 | custom fusion | bytes 33587200 | tf_op jit(solution)/shard_map/gather | solution.py:94
  2404.7 45.2 %gather_fusion.5 = bf16[8192,1024]{1,0:T(8,128)(2,1)} fusion(bf16[4096,1024]{1,0:T(8,128)(2,1)} %bitcast.40, s32[8192]{0:T(1024)S(1)} %broadcast_clamp_fusion.1), kind=kCustom, calls=%fused_computation.5 | custom fusion | bytes 33587200 | tf_op jit(solution)/shard_map/gather | solution.py:93
  2449.9 31.4 %fusion.3 = (bf16[1024,1024]{1,0:T(8,128)(2,1)}, bf16[1024,1024]{1,0:T(8,128)(2,1)}) fusion(bf16[8192,1024]{1,0:T(8,128)(2,1)} %gather_fusion.9, pred[1024,8]{1,0:T(8,128)(4,1)S(1)} %copy-done.8, bf16[8192,1024]{1,0:T(8,128)(2,1)} %gather_fusion.5), kind=kLoop, calls=%fused_computation.23 | loop fusion | flops 48234496 | bytes 37756928 | tf_op jit(solution)/shard_map/reduce_sum | solution.py:94
  (120 shorter events, 123.8 us)
Async XLA Ops:
  0.6 82.4 %copy-start = (bf16[1024,1024]{1,0:T(8,128)(2,1)S(1)}, bf16[1024,1024]{1,0:T(8,128)(2,1)}, u32[]{:S(2)}) copy-start(bf16[1024,1024]{1,0:T(8,128)(2,1)} %param.10) | copy-start | bytes 6291460
  37.6 23.1 copy-start.10
  54.6 23.6 all-to-all-start.1
  60.6 14.7 copy-start.2
  78.2 23.1 all-to-all-start
  101.2 10.1 copy-start.4
  101.2 322.9 %all-to-all-start.6 = ((bf16[8,512,1024]{2,1,0:T(8,128)(2,1)}), bf16[8,512,1024]{2,1,0:T(8,128)(2,1)}, u32[]{:S(2)}, u32[]{:S(2)}) async-start(bf16[8,512,1024]{2,1,0:T(8,128)(2,1)} %bitcast.250), calls=%async_computation.6 | async-start | bytes 16777216 | tf_op jit(solution)/shard_map/all_to_all | solution.py:87
  130.3 293.8 %copy-start.14 = (pred[4096,8]{0,1:T(8,128)(4,1)}, pred[4096,8]{0,1:T(8,128)(4,1)S(1)}, u32[]{:S(2)}) copy-start(pred[4096,8]{0,1:T(8,128)(4,1)S(1)} %get-tuple-element.10) | copy-start | bytes 98308
  424.1 5.2 copy-start.5
  424.1 5.2 copy-start.9
  424.2 334.4 %all-to-all-start.2 = ((bf16[8,512,1024]{2,1,0:T(8,128)(2,1)}), bf16[8,512,1024]{2,1,0:T(8,128)(2,1)}, u32[]{:S(2)}, u32[]{:S(2)}) async-start(bf16[8,512,1024]{2,1,0:T(8,128)(2,1)} %bitcast.249), calls=%async_computation.2 | async-start | bytes 16777216 | tf_op jit(solution)/shard_map/all_to_all | solution.py:86
  758.6 283.3 %all-to-all-start.7 = ((bf16[4,1,3072,1024]{3,2,1,0:T(8,128)(2,1)}), bf16[4,1,3072,1024]{3,2,1,0:T(8,128)(2,1)}, u32[]{:S(2)}, u32[]{:S(2)}) async-start(bf16[4,1,3072,1024]{3,2,1,0:T(8,128)(2,1)} %fusion.2), calls=%async_computation.7 | async-start | bytes 50331648 | tf_op jit(solution)/shard_map/all_to_all | solution.py:42
  1041.9 8.7 copy-start.19
  1041.9 281.3 %all-to-all-start.3 = ((bf16[4,1,3072,1024]{3,2,1,0:T(8,128)(2,1)}), bf16[4,1,3072,1024]{3,2,1,0:T(8,128)(2,1)}, u32[]{:S(2)}, u32[]{:S(2)}) async-start(bf16[4,1,3072,1024]{3,2,1,0:T(8,128)(2,1)} %bitcast.246), calls=%async_computation.3 | async-start | bytes 50331648 | tf_op jit(solution)/shard_map/all_to_all | solution.py:41
  1050.6 272.5 %copy-start.18 = (bf16[1,1024,512]{2,1,0:T(8,128)(2,1)S(1)}, bf16[1,1024,512]{2,1,0:T(8,128)(2,1)}, u32[]{:S(2)}) copy-start(bf16[1,1024,512]{2,1,0:T(8,128)(2,1)} %param.12) | copy-start | bytes 3145732
  1073.3 272.5 %copy-start.17 = (bf16[1,1024,512]{2,1,0:T(8,128)(2,1)S(1)}, bf16[1,1024,512]{2,1,0:T(8,128)(2,1)}, u32[]{:S(2)}) copy-start(bf16[1,1024,512]{2,1,0:T(8,128)(2,1)} %param.11) | copy-start | bytes 3145732
  1445.4 280.0 %all-to-all-start.8 = ((bf16[4,1,3072,1024]{3,2,1,0:T(8,128)(2,1)}), bf16[4,1,3072,1024]{3,2,1,0:T(8,128)(2,1)}, u32[]{:S(2)}, u32[]{:S(2)}) async-start(bf16[4,1,3072,1024]{3,2,1,0:T(8,128)(2,1)} %fusion.26), calls=%async_computation.8 | async-start | bytes 50331648 | tf_op jit(solution)/shard_map/all_to_all | solution.py:57
  1475.0 259.2 %copy-start.15 = (pred[4096,8]{0,1:T(8,128)(4,1)S(1)}, pred[4096,8]{0,1:T(8,128)(4,1)}, u32[]{:S(2)}) copy-start(pred[4096,8]{0,1:T(8,128)(4,1)} %copy-done.14) | copy-start | bytes 98308
  1475.0 260.6 %copy-start.6 = (s32[32768]{0:T(1024)S(1)}, s32[32768]{0:T(1024)}, u32[]{:S(2)}) copy-start(s32[32768]{0:T(1024)} %copy-done.5) | copy-start | bytes 393220
  1725.4 279.4 %all-to-all-start.4 = ((bf16[4,1,3072,1024]{3,2,1,0:T(8,128)(2,1)}), bf16[4,1,3072,1024]{3,2,1,0:T(8,128)(2,1)}, u32[]{:S(2)}, u32[]{:S(2)}) async-start(bf16[4,1,3072,1024]{3,2,1,0:T(8,128)(2,1)} %convert_bitcast_fusion), calls=%async_computation.4 | async-start | bytes 50331648 | tf_op jit(solution)/shard_map/all_to_all | solution.py:56
  1743.9 170.7 %copy-start.7 = (pred[4096,8]{1,0:T(8,128)(4,1)S(1)}, pred[4096,8]{1,0:T(8,128)(4,1)}, u32[]{:S(2)}) copy-start(pred[4096,8]{1,0:T(8,128)(4,1)} %copy.92) | copy-start | bytes 98308
  2004.8 8.9 copy-start.13
  2004.8 234.7 %all-to-all-start.9 = ((bf16[8,512,1024]{2,1,0:T(8,128)(2,1)}), bf16[8,512,1024]{2,1,0:T(8,128)(2,1)}, u32[]{:S(2)}, u32[]{:S(2)}) async-start(bf16[8,512,1024]{2,1,0:T(8,128)(2,1)} %bitcast.252), calls=%async_computation.9 | async-start | bytes 16777216 | tf_op jit(solution)/shard_map/all_to_all | solution.py:92
  2239.5 5.7 copy-start.16
  2239.5 6.6 copy-start.11
  2239.5 7.1 copy-start.3
  2239.5 165.3 %all-to-all-start.5 = ((bf16[8,512,1024]{2,1,0:T(8,128)(2,1)}), bf16[8,512,1024]{2,1,0:T(8,128)(2,1)}, u32[]{:S(2)}, u32[]{:S(2)}) async-start(bf16[8,512,1024]{2,1,0:T(8,128)(2,1)} %bitcast.251), calls=%async_computation.5 | async-start | bytes 16777216 | tf_op jit(solution)/shard_map/all_to_all | solution.py:91
  2246.5 49.0 %copy-start.12 = (s32[1024,8]{0,1:T(8,128)S(1)}, s32[1024,8]{0,1:T(8,128)}, u32[]{:S(2)}) copy-start(s32[1024,8]{0,1:T(8,128)} %param.8) | copy-start | bytes 98308
  2404.7 45.2 %copy-start.8 = (pred[1024,8]{1,0:T(8,128)(4,1)S(1)}, pred[1024,8]{1,0:T(8,128)(4,1)}, u32[]{:S(2)}) copy-start(pred[1024,8]{1,0:T(8,128)(4,1)} %copy.77) | copy-start | bytes 24580
  2449.9 31.4 %copy-start.1 = (bf16[1024,1024]{1,0:T(8,128)(2,1)S(1)}, bf16[1024,1024]{1,0:T(8,128)(2,1)}, u32[]{:S(2)}) copy-start(bf16[1024,1024]{1,0:T(8,128)(2,1)} %param.10) | copy-start | bytes 6291460
where the time goes:
time: 2490 us; the launch traced here: 2480 us
  local copies, waits for them, and re-layouts  1250 us (50%)
  waiting for transfers between devices  746 us (30%)
  matrix products  230 us (9%)
  other arithmetic  179 us (7%)
  starting transfers between devices  70.5 us (3%)
    gather x3, local copies, waits for them, and re-layouts, expert_stage(): jnp.take_along_axis(exp_pos, jnp.minimum(loc_exp, per_group - 1), axis=1)  279 us
    all_to_all x1, waiting for transfers between devices, expert_stage(): lax.all_to_all(dx_bf, 'ing', 0, 0, tiled=True)  250 us
    all_to_all x1, waiting for transfers between devices, expert_stage(): exp_x = lax.all_to_all(fwd_x, 'ing', 0, 0, tiled=True)  250 us
    all_to_all x1, waiting for transfers between devices, expert_stage(): exp_do = lax.all_to_all(fwd_do, 'ing', 0, 0, tiled=True)  210 us
    gather x1, local copies, waits for them, and re-layouts, expert_stage(): back_dx[take_slot].astype(jnp.float32)  171 us
    gather x1, local copies, waits for them, and re-layouts, expert_stage(): back_out[take_slot].astype(jnp.float32)  171 us
    scatter x1, local copies, waits for them, and re-layouts, expert_stage(): jnp.zeros((per_group * in_cap,), jnp.float32).at[fwd_slot.reshape(-1)]  121 us
    scatter x1, local copies, waits for them, and re-layouts, expert_stage(): jnp.zeros((per_group * in_cap,), jnp.int32).at[fwd_slot.reshape(-1)]  120 us
  transfers between devices with their start and end apart: 10, of which 4 were waited for; matrix products, arithmetic and copies ran while one was open for 57% of the time, Pallas kernels for 0%

commit v1 on v0

v1 whole, which is shorter than its diff:
```python
import functools

import jax
import jax.numpy as jnp
from jax import lax
from jax.experimental import pallas as pl
from jax.experimental.pallas import tpu as pltpu
from jax.sharding import PartitionSpec as P

F32 = jnp.float32
BF16 = jnp.bfloat16
SUB = 128
TILE = 256


def dot(a, b, ca, cb):
    return lax.dot_general(a, b, (((ca,), (cb,)), ((), ())), preferred_element_type=F32)


def split3(v):
    hi = v.astype(BF16)
    rest = v - hi.astype(F32)
    mid = rest.astype(BF16)
    lo = (rest - mid.astype(F32)).astype(BF16)
    return jnp.concatenate([hi.astype(F32), mid.astype(F32), lo.astype(F32)], axis=0).astype(BF16)


def pack_kernel(groups, per_group, cap, ids_ref, gates_ref, x_ref, dy_ref, packed_ref, meta_ref, slot_ref, slots, vals):
    h = pl.program_id(0)
    top_k, tokens = ids_ref.shape
    num_exp = groups * per_group

    @pl.when(h == 0)
    def _():
        exp_iota = lax.broadcasted_iota(jnp.int32, (num_exp, tokens), 0)
        grp_iota = lax.broadcasted_iota(jnp.int32, (groups, tokens), 0)
        mem = jnp.zeros((num_exp, tokens), F32)
        gate = jnp.zeros((num_exp, tokens), F32)
        gmem = jnp.zeros((groups, tokens), F32)
        for j in range(top_k):
            row = ids_ref[j:j + 1, :]
            hit = row == exp_iota
            mem = jnp.where(hit, 1.0, mem)
            gate = jnp.where(hit, gates_ref[j:j + 1, :], gate)
            gmem = jnp.where((row // per_group) == grp_iota, 1.0, gmem)
        upper = (lax.broadcasted_iota(jnp.int32, (tokens, tokens), 0) <= lax.broadcasted_iota(jnp.int32, (tokens, tokens), 1)).astype(F32).astype(BF16)
        rank = jnp.where(mem > 0, dot(mem.astype(BF16), upper, 1, 0), 0.0)
        slot = jnp.where(gmem > 0, dot(gmem.astype(BF16), upper, 1, 0), 0.0)
        slots[...] = slot
        slot_ref[...] = slot
        for g in range(groups):
            vals[g, 0:per_group, :] = rank[g * per_group:(g + 1) * per_group, :]
            vals[g, per_group:2 * per_group, :] = gate[g * per_group:(g + 1) * per_group, :]

    row = slots[pl.ds(h, 1), :]
    pick = (row == (lax.broadcasted_iota(jnp.int32, (cap, tokens), 0) + 1).astype(F32)).astype(F32).astype(BF16)
    hidden = x_ref.shape[1]
    packed_ref[0, :, 0:hidden] = dot(pick, x_ref[...], 1, 0).astype(BF16)
    packed_ref[0, :, hidden:] = dot(pick, dy_ref[...], 1, 0).astype(BF16)
    parts = dot(split3(vals[h]), pick, 1, 1)
    n = 2 * per_group
    meta_ref[0] = (parts[0:n] + parts[n:2 * n]) + parts[2 * n:3 * n]


def pack_rows(ids_t, gates_t, x, dy, groups, per_group, cap):
    top_k, tokens = ids_t.shape
    hidden = x.shape[1]
    whole = lambda shape: pl.BlockSpec(shape, lambda h: (0,) * len(shape))
    return pl.pallas_call(
        functools.partial(pack_kernel, groups, per_group, cap),
        grid=(groups,),
        out_shape=(
            jax.ShapeDtypeStruct((groups, cap, 2 * hidden), BF16),
            jax.ShapeDtypeStruct((groups, 2 * per_group, cap), F32),
            jax.ShapeDtypeStruct((groups, tokens), F32),
        ),
        in_specs=[whole((top_k, tokens)), whole((top_k, tokens)), whole((tokens, hidden)), whole((tokens, hidden))],
        out_specs=(
            pl.BlockSpec((1, cap, 2 * hidden), lambda h: (h, 0, 0)),
            pl.BlockSpec((1, 2 * per_group, cap), lambda h: (h, 0, 0)),
            whole((groups, tokens)),
        ),
        scratch_shapes=[pltpu.VMEM((groups, tokens), F32), pltpu.VMEM((groups, 2 * per_group, tokens), F32)],
        compiler_params=pltpu.CompilerParams(vmem_limit_bytes=48 * 1024 * 1024),
        cost_estimate=pl.CostEstimate(flops=4 * groups * cap * tokens * hidden, bytes_accessed=groups * cap * hidden * 4, transcendentals=0),
        name='pack_rows',
    )(ids_t, gates_t, x, dy)


def expert_kernel(max_tiles, has_prev, cnt_ref, *refs):
    meta_ref, xd_ref, w1_ref, w3_ref, w2_ref = refs[:5]
    refs = refs[5:]
    prev = refs[:3] if has_prev else None
    refs = refs[3:] if has_prev else refs
    pq_ref, g1_ref, g3_ref, g2_ref, buf, pq, acc1, acc3, acc2, stage, in_sem, out_sem, pq_sem = refs
    k = pl.program_id(0)
    per_group = pl.num_programs(0)
    srcs, rows2, cap = meta_ref.shape
    hidden = xd_ref.shape[2] // 2
    accs = (acc1, acc3, acc2)
    outs = (g1_ref, g3_ref, g2_ref)

    @pl.when(k > 0)
    def _():
        for i in range(3):
            pltpu.make_async_copy(accs[i], outs[i].at[k - 1], out_sem.at[i]).wait()

    if has_prev:
        for i in range(3):
            pltpu.make_async_copy(prev[i].at[k], accs[i], in_sem.at[i]).start()
    else:
        for a in accs:
            a[...] = jnp.zeros_like(a)

    @pl.when(k == 0)
    def _():
        pq[...] = jnp.zeros_like(pq)

    def pick(s, m):
        slot = (lax.broadcasted_iota(jnp.int32, (m, cap), 0) + 1).astype(F32)
        return meta_ref[s, pl.ds(k, 1), :] == slot

    offs = []
    off = jnp.int32(0)
    for s in range(srcs):
        tiles = (cnt_ref[s, k] + SUB - 1) // SUB
        offs.append((pl.multiple_of(off, SUB), tiles))
        off = off + tiles * SUB
    total = off

    for s in range(srcs):
        start, tiles = offs[s]
        for t in range(1, max_tiles + 1):
            m = t * SUB

            @pl.when(tiles == t)
            def _(s=s, m=m, start=start):
                hit = pick(s, m)
                sel = hit.astype(F32).astype(BF16)
                buf[pl.ds(start, m), 0:hidden] = dot(sel, xd_ref[s, :, 0:hidden], 1, 0).astype(BF16)
                gate = jnp.sum(jnp.where(hit, meta_ref[s, pl.ds(per_group + k, 1), :], 0.0), axis=1, keepdims=True)
                buf[pl.ds(start, m), hidden:] = (gate * dot(sel, xd_ref[s, :, hidden:], 1, 0)).astype(BF16)

    n_tiles = (total + TILE - 1) // TILE

    @pl.loop(total // SUB, n_tiles * (TILE // SUB))
    def _(i):
        buf[pl.ds(pl.multiple_of(i * SUB, SUB), SUB), :] = jnp.zeros((SUB, 2 * hidden), BF16)

    if has_prev:
        for i in range(3):
            pltpu.make_async_copy(prev[i].at[k], accs[i], in_sem.at[i]).wait()

    @pl.loop(0, n_tiles)
    def _(i):
        r0 = pl.multiple_of(i * TILE, TILE)
        x = buf[pl.ds(r0, TILE), 0:hidden]
        d = buf[pl.ds(r0, TILE), hidden:]
        h1 = dot(x, w1_ref[0], 1, 0)
        h3 = dot(x, w3_ref[0], 1, 0)
        da = dot(d, w2_ref[0], 1, 1)
        sig = jax.nn.sigmoid(h1)
        silu = h1 * sig
        a = (silu * h3).astype(BF16)
        dh1 = (da * h3 * sig * (1.0 + h1 * (1.0 - sig))).astype(BF16)
        dh3 = (da * silu).astype(BF16)
        acc1[...] += dot(x, dh1, 0, 0)
        acc3[...] += dot(x, dh3, 0, 0)
        acc2[...] += dot(a, d, 0, 0)
        buf[pl.ds(r0, TILE), 0:hidden] = dot(a, w2_ref[0], 1, 0).astype(BF16)
        buf[pl.ds(r0, TILE), hidden:] = (dot(dh1, w1_ref[0], 1, 1) + dot(dh3, w3_ref[0], 1, 1)).astype(BF16)

    for i in range(3):
        pltpu.make_async_copy(accs[i], outs[i].at[k], out_sem.at[i]).start()

    for s in range(srcs):
        start, tiles = offs[s]
        for t in range(1, max_tiles + 1):
            m = t * SUB

            @pl.when(tiles == t)
            def _(s=s, m=m, start=start):
                sel = pick(s, m).astype(F32).astype(BF16)
                cols = jnp.transpose(meta_ref[s])
                lane = lax.broadcasted_iota(jnp.int32, (cap, rows2), 1)
                gate = jnp.sum(jnp.where(lane == per_group + k, cols, 0.0), axis=1, keepdims=True)
                pq[s, :, 0:hidden] += gate * dot(sel, buf[pl.ds(start, m), 0:hidden], 0, 0)
                pq[s, :, hidden:] += dot(sel, buf[pl.ds(start, m), hidden:], 0, 0)

    @pl.when(k == per_group - 1)
    def _():
        for s in range(srcs):
            slot = s % 2
            if s >= 2:
                pltpu.make_async_copy(stage.at[slot], pq_ref.at[s - 2], pq_sem.at[slot]).wait()
            stage[slot] = pq[s].astype(BF16)
            pltpu.make_async_copy(stage.at[slot], pq_ref.at[s], pq_sem.at[slot]).start()
        for s in range(max(0, srcs - 2), srcs):
            pltpu.make_async_copy(stage.at[s % 2], pq_ref.at[s], pq_sem.at[s % 2]).wait()
        for i in range(3):
            pltpu.make_async_copy(accs[i], outs[i].at[k], out_sem.at[i]).wait()


def run_experts(counts, meta, xd, w1, w3, w2, prev, exp_cap):
    srcs, rows2, cap = meta.shape
    per_group, hidden, ff = w1.shape
    max_tiles = -(-exp_cap // SUB)
    buf_rows = -(-srcs * max_tiles * SUB // TILE) * TILE
    any_spec = pl.BlockSpec(memory_space=pl.ANY)
    vmem = pl.BlockSpec(memory_space=pltpu.VMEM)
    w_spec = lambda a: pl.BlockSpec((1,) + a.shape[1:], lambda k, *_: (k, 0, 0))
    has_prev = prev is not None
    grads = (
        jax.ShapeDtypeStruct(w1.shape, F32),
        jax.ShapeDtypeStruct(w3.shape, F32),
        jax.ShapeDtypeStruct(w2.shape, F32),
    )
    rows = srcs * exp_cap * per_group * 2 // 3
    return pl.pallas_call(
        functools.partial(expert_kernel, max_tiles, has_prev),
        grid_spec=pltpu.PrefetchScalarGridSpec(
            num_scalar_prefetch=1,
            grid=(per_group,),
            in_specs=[vmem, vmem, w_spec(w1), w_spec(w3), w_spec(w2)] + [any_spec] * (3 if has_prev else 0),
            out_specs=[any_spec] * 4,
            scratch_shapes=[
                pltpu.VMEM((buf_rows, 2 * hidden), BF16),
                pltpu.VMEM((srcs, cap, 2 * hidden), F32),
                pltpu.VMEM((hidden, ff), F32),
                pltpu.VMEM((hidden, ff), F32),
                pltpu.VMEM((ff, hidden), F32),
                pltpu.VMEM((2, cap, 2 * hidden), BF16),
                pltpu.SemaphoreType.DMA((3,)),
                pltpu.SemaphoreType.DMA((3,)),
                pltpu.SemaphoreType.DMA((2,)),
            ],
        ),
        out_shape=(jax.ShapeDtypeStruct(xd.shape, BF16),) + grads,
        input_output_aliases={6: 1, 7: 2, 8: 3} if has_prev else {},
        compiler_params=pltpu.CompilerParams(vmem_limit_bytes=63 * 1024 * 1024, dimension_semantics=('arbitrary',)),
        cost_estimate=pl.CostEstimate(flops=rows * (18 * hidden * ff + 8 * cap * hidden), bytes_accessed=srcs * cap * hidden * 8, transcendentals=0),
        name='run_experts',
    )(counts, meta, xd, w1, w3, w2, *(prev or ()))


def home_kernel(slot_ref, ret_ref, y_ref, dx_ref):
    groups, cap, width = ret_ref.shape
    rows = y_ref.shape[0]
    acc = None
    for g in range(groups):
        pick = (slot_ref[g:g + 1, :] == (lax.broadcasted_iota(jnp.int32, (cap, rows), 0) + 1).astype(F32)).astype(F32).astype(BF16)
        part = dot(pick, ret_ref[g], 0, 0)
        acc = part if acc is None else acc + part
    y_ref[...] = acc[:, :width // 2].astype(BF16)
    dx_ref[...] = acc[:, width // 2:].astype(BF16)


def home_sum(slot, ret, block):
    groups, tokens = slot.shape
    _, cap, width = ret.shape
    out = jax.ShapeDtypeStruct((tokens, width // 2), BF16)
    return pl.pallas_call(
        home_kernel,
        grid=(tokens // block,),
        out_shape=(out, out),
        in_specs=[pl.BlockSpec((groups, block), lambda i: (0, i)), pl.BlockSpec(memory_space=pltpu.VMEM)],
        out_specs=(pl.BlockSpec((block, width // 2), lambda i: (i, 0)),) * 2,
        compiler_params=pltpu.CompilerParams(vmem_limit_bytes=48 * 1024 * 1024),
        cost_estimate=pl.CostEstimate(flops=2 * groups * cap * tokens * width, bytes_accessed=groups * cap * width * 2, transcendentals=0),
        name='home_sum',
    )(slot, ret)


def solution(mesh):
    groups = mesh.shape['grp']
    inner = mesh.shape['ing']
    tok_spec = P(('dp', 'grp', 'ing'), None)
    weight_spec = P(('grp', 'ing'), None, None)
    grad_spec = P(('dp', 'grp', 'ing'), None, None)

    def device_fn(x_loc, ids_loc, gates_loc, dy_loc, wg_loc, wu_loc, wd_loc):
        tokens, hidden = x_loc.shape
        top_k = ids_loc.shape[1]
        per_group = wg_loc.shape[0] * inner
        num_exp = per_group * groups
        group_limit = min(max(1, groups // 2), top_k // 2)
        cap = tokens * group_limit // groups
        exp_cap = 3 * tokens * top_k // (2 * num_exp)
        gather = lambda w: lax.all_gather(w, 'ing', axis=0, tiled=True)
        w1, w3, w2 = gather(wg_loc), gather(wu_loc), gather(wd_loc)
        packed, meta, slot = pack_rows(ids_loc.T, gates_loc.T, x_loc, dy_loc, groups, per_group, cap)
        swap = lambda a: lax.all_to_all(a, 'grp', 0, 0, tiled=True)
        recv_meta = swap(meta)
        recv = swap(packed)
        counts = jnp.max(recv_meta[:, :per_group, :], axis=2).astype(jnp.int32)
        half = groups // 2
        grads = None
        outs = []
        for c in range(2):
            sl = slice(c * half, (c + 1) * half)
            res = run_experts(counts[sl], recv_meta[sl], recv[sl], w1, w3, w2, grads, exp_cap)
            outs.append(res[0])
            grads = res[1:]
        ret = swap(jnp.concatenate(outs, axis=0))
        g1, g3, g2 = [lax.psum_scatter(g, 'ing', scatter_dimension=0, tiled=True) for g in grads]
        y_out, dx_out = home_sum(slot, ret, 256)
        return y_out, dx_out, g1, g3, g2

    return jax.shard_map(device_fn, mesh=mesh, in_specs=(tok_spec, tok_spec, tok_spec, tok_spec, weight_spec, weight_spec, weight_spec), out_specs=(tok_spec, tok_spec, grad_spec, grad_spec, grad_spec), check_vma=False)
```

time: 2490 us -> 688 us (0.28)
  local copies, waits for them, and re-layouts: 1250 us -> 17.9 us
  waiting for transfers between devices: 746 us -> 202 us
  Pallas kernels: 0 us -> 235 us
  matrix products: 230 us -> 0 us
  blocking collectives: 0 us -> 200 us
  other arithmetic: 179 us -> 8.09 us
  starting transfers between devices: 70.5 us -> 6.81 us
    gather x19 -> x0, local copies, waits for them, and re-layouts: 956 us -> none  [the longest x3 279 us: expert_stage(): jnp.take_along_axis(exp_pos, jnp.minimum(loc_exp, per_group - 1), axis=1)]
    all_to_all x10 -> x1, waiting for transfers between devices: 746 us -> 181 us  [device_fn(): swap = lambda a: lax.all_to_all(a, 'grp', 0, 0, tiled=True)]
    scatter x3 -> x0, local copies, waits for them, and re-layouts: 272 us -> none  [the longest x1 121 us: expert_stage(): jnp.zeros((per_group * in_cap,), jnp.float32).at[fwd_slot.reshape(-1)]]
    pallas_call x0 -> x4, Pallas kernels: none -> 235 us  [the longest x2 188 us: run_experts(): pl.pallas_call(functools.partial(expert_kernel, max_tiles, has_prev), gri...]
    dot_general x9 -> x0, matrix products: 230 us -> none  [the longest x1 45.2 us: expert_stage(): jnp.einsum('blcd,ldf->blcf', exp_x, wg_loc, preferred_element_type=jnp.fl...]
    all_to_all x0 -> x2, blocking collectives: none -> 200 us  [device_fn(): swap = lambda a: lax.all_to_all(a, 'grp', 0, 0, tiled=True)]
    reduce_sum x3 -> x0, other arithmetic: 139 us -> none  [the longest x1 54 us: expert_stage(): jnp.sum(jnp.where(in_group[:, :, None], back_dx[take_slot].astype(jnp.flo...]
    all_to_all x10 -> x1, starting transfers between devices: 70.5 us -> 6.5 us  [device_fn(): swap = lambda a: lax.all_to_all(a, 'grp', 0, 0, tiled=True)]
  transfers between devices with their start and end apart: 10 -> 7, of which waited for: 4 -> 2; matrix products, arithmetic and copies ran while one was open for 57% -> 3% of each run, Pallas kernels for 0% -> 7%
where the time goes in v1:
time: 688 us; the launch traced here: 684 us
  Pallas kernels  235 us (34%)
  waiting for transfers between devices  202 us (29%)
  blocking collectives  200 us (29%)
  local copies, waits for them, and re-layouts  17.9 us (3%)
  between operations  14.4 us (2%)
  other arithmetic  8.09 us (1%)
    all_to_all x2, blocking collectives, device_fn(): swap = lambda a: lax.all_to_all(a, 'grp', 0, 0, tiled=True)  200 us
    pallas_call x2, Pallas kernels, run_experts(): pl.pallas_call(functools.partial(expert_kernel, max_tiles, has_prev), gri...  188 us
    all_to_all x1, waiting for transfers between devices, device_fn(): swap = lambda a: lax.all_to_all(a, 'grp', 0, 0, tiled=True)  181 us
    pallas_call x1, Pallas kernels, home_sum(): pl.pallas_call(home_kernel, grid=(tokens // block,), out_shape=(out, out)...  24.7 us
    pallas_call x1, Pallas kernels, pack_rows(): pl.pallas_call(functools.partial(pack_kernel, groups, per_group, cap), gr...  22.4 us
    reduce_scatter x3, waiting for transfers between devices, device_fn(): lax.psum_scatter(g, 'ing', scatter_dimension=0, tiled=True)  18 us
  transfers between devices with their start and end apart: 7, of which 2 were waited for; matrix products, arithmetic and copies ran while one was open for 3% of the time, Pallas kernels for 7%

profile of v1, /device:TPU:97, one launch (start us, length us, event | category | flops | bytes accessed | tf_op | source)
XLA Modules:
  0.0 683.8 jit_solution(3893958642687064341)
XLA Ops:
  7.2 0.1 all-gather.4.cloned.1.call-start
  7.2 0.7 all-gather.4.cloned.1.call-update
  8.0 0.0 copy-start
  8.0 1.6 copy-done
  9.6 1.6 copy-done.1
  11.2 0.8 copy-done.2
  11.9 0.8 copy-done.3
  12.7 22.4 %pack_rows.1 = (bf16[8,512,2048]{2,1,0:T(8,128)(2,1)}, f32[8,8,512]{2,1,0:T(8,128)S(1)}, f32[8,1024]{1,0:T(8,128)S(1)}) custom-call(s32[8,1024]{1,0:T(8,128)S(1)} %bitcast.2, f32[8,1024]{1,0:T(8,128)S(1)} %bitcast.3, bf16[1024,1024]{1,0:T(8,128)(2,1)S(1)} %copy-done, bf16[1024,1024]{1,0:T(8,128)(2,1)S(1)} %copy-done.1), custom_call_target="tpu_custom_call" | custom-call | flops 17179869184 | bytes 16777216 | tf_op jit(solution)/shard_map/pack_rows/pallas_call | solution.py:69
  35.1 11.0 %all_to_all.15 = f32[8,8,512]{2,1,0:T(8,128)S(1)} all-to-all(f32[8,8,512]{2,1,0:T(8,128)S(1)} %get-tuple-element.19), channel_id=1, replica_groups=mesh['dp'=1,'ing'=4,'grp'=8] {'grp'}, dimensions={0} | all-to-all | bytes 262144 | tf_op jit(solution)/shard_map/all_to_all | solution.py:292
  46.1 6.5 all-to-all-start.1
  52.6 0.0 all-gather.6.cloned.1.call-start
  52.6 0.8 all-gather.6.cloned.1.call-update
  53.4 0.1 all-gather.8.cloned.1.call-start
  53.4 0.7 all-gather.8.cloned.1.call-update
  54.2 0.1 reduce-scatter.4.cloned.1.call-start
  54.2 0.1 slice_reduce_fusion
  54.3 0.6 fusion.2
  54.9 0.7 fusion.1
  55.6 180.5 %all-to-all-done.1 = bf16[8,512,2048]{2,1,0:T(8,128)(2,1)} async-done(((bf16[8,512,2048]{2,1,0:T(8,128)(2,1)}), bf16[8,512,2048]{2,1,0:T(8,128)(2,1)}, u32[]{:S(2)}, u32[]{:S(2)}) %all-to-all-start.1) | async-done | bytes 16777248 | tf_op jit(solution)/shard_map/all_to_all | solution.py:292
  236.1 11.9 %fusion = (bf16[4,512,2048]{2,1,0:T(8,128)(2,1)}, bf16[4,512,2048]{2,1,0:T(8,128)(2,1)}) fusion(bf16[8,512,2048]{2,1,0:T(8,128)(2,1)} %all-to-all-done.1), kind=kLoop, calls=%fused_computation.2 | loop fusion | bytes 33554432 | tf_op jit(solution)/shard_map/slice | solution.py:301
  248.0 0.0 all-gather.8.cloned.1.call-done.refs_4_
  248.0 100.8 %run_experts.2 = (bf16[4,512,2048]{2,1,0:T(8,128)(2,1)}, f32[4,1024,512]{2,1,0:T(8,128)}, f32[4,1024,512]{2,1,0:T(8,128)}, f32[4,512,1024]{2,1,0:T(8,128)}) custom-call(s32[4,4]{1,0:T(4,128)} %get-tuple-element.35.cnt_ref, f32[4,8,512]{2,1,0:T(8,128)} %get-tuple-element.33.refs_0_, bf16[4,512,2048]{2,1,0:T(8,128)(2,1)} %get-tuple-element.31.refs_1_, ...), custom_call_target="tpu_custom_call" | custom-call | flops 55834574848 | bytes 16777216 | tf_op jit(solution)/shard_map/run_experts/pallas_call | solution.py:219
  348.9 86.9 %run_experts.3 = (bf16[4,512,2048]{2,1,0:T(8,128)(2,1)}, f32[4,1024,512]{2,1,0:T(8,128)}, f32[4,1024,512]{2,1,0:T(8,128)}, f32[4,512,1024]{2,1,0:T(8,128)}) custom-call(s32[4,4]{1,0:T(4,128)} %get-tuple-element.36.cnt_ref, f32[4,8,512]{2,1,0:T(8,128)} %get-tuple-element.34.refs_0_, ...), custom_call_target="tpu_custom_call", output_to_operand_aliasing={{1}: (6, {}), {2}: (7, {}), {3}: (8, {})} | custom-call | flops 55834574848 | bytes 16777216 | tf_op jit(solution)/shard_map/run_experts/pallas_call | solution.py:219
  435.8 0.1 reduce-scatter.4.cloned.1.call-update
  435.8 0.1 reduce-scatter.6.cloned.1.call-start
  435.9 0.6 reduce-scatter.6.cloned.1.call-update
  436.5 0.1 reduce-scatter.8.cloned.1.call-start
  436.6 0.6 reduce-scatter.8.cloned.1.call-update
  437.1 8.0 %pad_maximum_fusion = bf16[8,512,2048]{2,1,0:T(8,128)(2,1)S(1)} fusion(bf16[4,512,2048]{2,1,0:T(8,128)(2,1)} %get-tuple-element.25, bf16[4,512,2048]{2,1,0:T(8,128)(2,1)} %get-tuple-element.21), kind=kLoop, calls=%fused_computation | loop fusion | flops 8388608 | bytes 33554432 | tf_op jit(solution)/shard_map/concatenate | solution.py:304
  445.1 188.8 %all_to_all.16.ret_ref = bf16[8,512,2048]{2,1,0:T(8,128)(2,1)} all-to-all(bf16[8,512,2048]{2,1,0:T(8,128)(2,1)S(1)} %pad_maximum_fusion), channel_id=1, replica_groups=mesh['dp'=1,'ing'=4,'grp'=8] {'grp'}, dimensions={0} | all-to-all | bytes 33554432 | tf_op jit(solution)/shard_map/all_to_all | solution.py:292
  634.0 24.7 %home_sum.1 = (bf16[1024,1024]{1,0:T(8,128)(2,1)}, bf16[1024,1024]{1,0:T(8,128)(2,1)}) custom-call(f32[8,1024]{1,0:T(8,128)S(1)} %get-tuple-element.18.slot_ref, bf16[8,512,2048]{2,1,0:T(8,128)(2,1)} %all_to_all.16.ret_ref), custom_call_target="tpu_custom_call" | custom-call | flops 17179869184 | bytes 16777216 | tf_op jit(solution)/shard_map/home_sum/pallas_call | solution.py:262
  658.7 18.0 %reduce-scatter.8.cloned.1.call-done = f32[1,512,1024]{2,1,0:T(8,128)} async-done(((f32[4,512,1024]{2,1,0:T(8,128)}), f32[1,512,1024]{2,1,0:T(8,128)}) %reduce-scatter.8.cloned.1.call-update) | async-done | bytes 2097168 | tf_op jit(solution)/shard_map/reduce_scatter | solution.py:305
  (8 shorter events, 0.0 us)
Async XLA Ops:
  7.2 240.8 %all-gather.4.cloned.1.call-start = ((), (), s32[]{:S(2)}) async-start(), calls=%async_computation.6 | async-start | bytes 5242880 | tf_op jit(solution)/shard_map/all_gather | solution.py:289
  8.0 1.6 copy-start
  9.6 1.6 copy-start.1
  11.2 0.8 copy-start.2
  11.9 0.8 copy-start.3
  46.1 190.0 %all-to-all-start.1 = ((bf16[8,512,2048]{2,1,0:T(8,128)(2,1)}), bf16[8,512,2048]{2,1,0:T(8,128)(2,1)}, u32[]{:S(2)}, u32[]{:S(2)}) async-start(bf16[8,512,2048]{2,1,0:T(8,128)(2,1)} %get-tuple-element.20), calls=%async_computation.1 | async-start | bytes 33554432 | tf_op jit(solution)/shard_map/all_to_all | solution.py:292
  52.6 195.4 %all-gather.6.cloned.1.call-start = ((), (), s32[]{:S(2)}) async-start(), calls=%async_computation.7 | async-start | bytes 5242880 | tf_op jit(solution)/shard_map/all_gather | solution.py:289
  53.4 194.7 %all-gather.8.cloned.1.call-start = ((), (), s32[]{:S(2)}) async-start(), calls=%async_computation.8 | async-start | bytes 5242880 | tf_op jit(solution)/shard_map/all_gather | solution.py:289
  54.2 604.5 %reduce-scatter.4.cloned.1.call-start = ((), (), s32[]{:S(2)}) async-start(), calls=%async_computation.9 | async-start | bytes 10485760 | tf_op jit(solution)/shard_map/reduce_scatter | solution.py:305
  435.8 222.8 %reduce-scatter.6.cloned.1.call-start = ((), (), s32[]{:S(2)}) async-start(), calls=%async_computation.10 | async-start | bytes 10485760 | tf_op jit(solution)/shard_map/reduce_scatter | solution.py:305
  436.5 240.2 %reduce-scatter.8.cloned.1.call-start = ((), (), s32[]{:S(2)}) async-start(), calls=%async_computation.11 | async-start | bytes 10485760 | tf_op jit(solution)/shard_map/reduce_scatter | solution.py:305
Sparse Core Ops, SparseCore 0:
  9.6 49.2 all-gather.3
  60.4 45.8 all-gather.5
  107.9 45.9 all-gather.7
  436.0 79.5 reduce-scatter.3
  518.4 77.6 reduce-scatter.5
  598.9 77.7 reduce-scatter.7

commit v2 on v0

v2 whole, which is shorter than its diff:
```python
import functools

import jax
import jax.numpy as jnp
from jax import lax
from jax.experimental import pallas as pl
from jax.experimental.pallas import tpu as pltpu
from jax.sharding import PartitionSpec as P


F32 = jnp.float32
BF16 = jnp.bfloat16
ALIGN = 16
TILE = 256


def dot(a, b, ca, cb):
    return lax.dot_general(a, b, (((ca,), (cb,)), ((), ())), preferred_element_type=F32)


def split3(v):
    hi = v.astype(BF16)
    rest = v - hi.astype(F32)
    mid = rest.astype(BF16)
    lo = (rest - mid.astype(F32)).astype(BF16)
    return jnp.concatenate([hi.astype(F32), mid.astype(F32), lo.astype(F32)], axis=0).astype(BF16)


def table_rows(groups, per_group, ids_ref, gates_ref, slots, vals):
    top_k, tokens = ids_ref.shape
    num_exp = groups * per_group
    exp_iota = lax.broadcasted_iota(jnp.int32, (num_exp, tokens), 0)
    grp_iota = lax.broadcasted_iota(jnp.int32, (groups, tokens), 0)
    mem = jnp.zeros((num_exp, tokens), F32)
    gate = jnp.zeros((num_exp, tokens), F32)
    gmem = jnp.zeros((groups, tokens), F32)
    for j in range(top_k):
        row = ids_ref[j:j + 1, :]
        hit = row == exp_iota
        mem = jnp.where(hit, 1.0, mem)
        gate = jnp.where(hit, gates_ref[j:j + 1, :], gate)
        gmem = jnp.where((row // per_group) == grp_iota, 1.0, gmem)
    upper = (lax.broadcasted_iota(jnp.int32, (tokens, tokens), 0) <= lax.broadcasted_iota(jnp.int32, (tokens, tokens), 1)).astype(F32).astype(BF16)
    rank = jnp.where(mem > 0, dot(mem.astype(BF16), upper, 1, 0), 0.0)
    slots[...] = jnp.where(gmem > 0, dot(gmem.astype(BF16), upper, 1, 0), 0.0)
    for g in range(groups):
        vals[g, 0:per_group, :] = rank[g * per_group:(g + 1) * per_group, :]
        vals[g, per_group:2 * per_group, :] = gate[g * per_group:(g + 1) * per_group, :]


def pick_rows(slot_row, first, count):
    want = (lax.broadcasted_iota(jnp.int32, (count, slot_row.shape[1]), 0) + (first + 1)).astype(F32)
    return (slot_row == want).astype(F32).astype(BF16)


def table_kernel(groups, per_group, size, ids_ref, gates_ref, slot_ref, meta_ref, vals):
    table_rows(groups, per_group, ids_ref, gates_ref, slot_ref, vals)
    n = 2 * per_group
    is_rank = lax.broadcasted_iota(jnp.int32, (n, 1), 0) < per_group

    @pl.loop(0, groups)
    def _(h):
        row = slot_ref[pl.ds(h, 1), :]
        split = split3(vals[h])
        base = jnp.zeros((n, 1), F32)
        for c in range(meta_ref.shape[2] // size):
            parts = dot(split, pick_rows(row, c * size, size), 1, 1)
            full = (parts[0:n] + parts[n:2 * n]) + parts[2 * n:3 * n]
            meta_ref[h, :, c * size:(c + 1) * size] = jnp.where(is_rank & (full > 0), full - base, full)
            base = jnp.where(is_rank, jnp.maximum(base, jnp.max(full, axis=1, keepdims=True)), 0.0)


def make_tables(ids_t, gates_t, groups, per_group, cap, size):
    tokens = ids_t.shape[1]
    vmem = pl.BlockSpec(memory_space=pltpu.VMEM)
    return pl.pallas_call(
        functools.partial(table_kernel, groups, per_group, size),
        out_shape=(jax.ShapeDtypeStruct((groups, tokens), F32), jax.ShapeDtypeStruct((groups, 2 * per_group, cap), F32)),
        in_specs=[vmem, vmem],
        out_specs=(vmem, vmem),
        scratch_shapes=[pltpu.VMEM((groups, 2 * per_group, tokens), F32)],
        cost_estimate=pl.CostEstimate(flops=2 * groups * cap * tokens * 128, bytes_accessed=groups * cap * 64, transcendentals=0),
        name='make_tables',
    )(ids_t, gates_t)


def pack_kernel(first, slot_ref, x_ref, dy_ref, packed_ref):
    size, width = packed_ref.shape[1:]
    pick = pick_rows(slot_ref[pl.ds(pl.program_id(0), 1), :], first, size)
    packed_ref[0, :, 0:width // 2] = dot(pick, x_ref[...], 1, 0).astype(BF16)
    packed_ref[0, :, width // 2:] = dot(pick, dy_ref[...], 1, 0).astype(BF16)


def pack_rows(slot, x, dy, c, size):
    groups, tokens = slot.shape
    hidden = x.shape[1]
    vmem = pl.BlockSpec(memory_space=pltpu.VMEM)
    return pl.pallas_call(
        functools.partial(pack_kernel, c * size),
        grid=(groups,),
        out_shape=jax.ShapeDtypeStruct((groups, size, 2 * hidden), BF16),
        in_specs=[vmem, vmem, vmem],
        out_specs=pl.BlockSpec((1, size, 2 * hidden), lambda h: (h, 0, 0)),
        compiler_params=pltpu.CompilerParams(vmem_limit_bytes=58 * 1024 * 1024),
        cost_estimate=pl.CostEstimate(flops=4 * groups * size * tokens * hidden, bytes_accessed=groups * size * hidden * 4, transcendentals=0),
        name='pack_rows',
    )(slot, x, dy)


def grad_parts(hidden, ff):
    mid = hidden + ff // 2
    return (
        (pl.ds(0, hidden), pl.ds(0, ff)),
        (pl.ds(0, hidden), pl.ds(ff, ff)),
        (pl.ds(hidden, ff // 2), pl.ds(0, hidden)),
        (pl.ds(mid, ff // 2), pl.ds(0, hidden)),
    )


def expert_kernel(chunk, first_pos, steps, has_prev, carry_in, carry_out, split, order_ref, meta_ref, xd_ref, w_ref, *refs):
    refs = list(refs)
    prev = refs.pop(0) if has_prev else None
    carried = refs.pop(0) if carry_in else None
    rows_ref = refs.pop(0)
    grad_refs = [refs.pop(0) for _ in range(4 * steps if split else 1)]
    buf, acc, offs, in_sem, out_sem, row_sem = refs[:6]
    pq, stage, pq_sem = (None,) * 3 if carry_out else refs[6:]
    step = pl.program_id(0)
    k = order_ref[first_pos + step]
    srcs, size, width = xd_ref.shape
    hidden = width // 2
    rows2 = meta_ref.shape[1]
    per_group = rows2 // 2
    ff = acc.shape[0] - hidden
    lanes = pl.ds(chunk * size, size)

    def each_grad(at, act):
        if not split:
            act(pltpu.make_async_copy(acc, grad_refs[0].at[at], out_sem.at[0]))
            return
        for i in range(steps):
            @pl.when(at == i)
            def _(i=i):
                for j, (rows, cols) in enumerate(grad_parts(hidden, ff)):
                    act(pltpu.make_async_copy(acc.at[rows, cols], grad_refs[4 * i + j], out_sem.at[j]))

    def load_prev():
        return pltpu.make_async_copy(prev.at[first_pos + step], acc, in_sem)

    @pl.when(step > 0)
    def _():
        each_grad(step - 1, lambda copy: copy.wait())

    if has_prev:
        load_prev().start()
    else:
        acc[...] = jnp.zeros_like(acc)

    def pick(s, k):
        slot = (lax.broadcasted_iota(jnp.int32, (size, size), 0) + 1).astype(F32)
        return meta_ref[s, pl.ds(k, 1), lanes] == slot

    def place(s, k, off):
        offs[s] = off
        count = jnp.max(meta_ref[s, pl.ds(k, 1), lanes]).astype(jnp.int32)
        return off + (count + ALIGN - 1) // ALIGN * ALIGN

    def combine(k, first):
        @pl.loop(0, srcs)
        def _(s):
            off = pl.multiple_of(offs[s], ALIGN)
            sel = pick(s, k).astype(F32).astype(BF16)
            cols = jnp.transpose(meta_ref[s, :, lanes])
            lane = lax.broadcasted_iota(jnp.int32, (size, rows2), 1)
            gate = jnp.sum(jnp.where(lane == per_group + k, cols, 0.0), axis=1, keepdims=True)
            p = gate * dot(sel, buf[pl.ds(off, size), 0:hidden], 0, 0)
            q = dot(sel, buf[pl.ds(off, size), hidden:], 0, 0)
            if first:
                pq[s, :, 0:hidden] = p
                pq[s, :, hidden:] = q
            else:
                pq[s, :, 0:hidden] += p
                pq[s, :, hidden:] += q

    if carry_in:
        @pl.when(step == 0)
        def _():
            copy = pltpu.make_async_copy(carried, buf, row_sem)
            copy.start()
            before = order_ref[first_pos - 1]
            lax.fori_loop(0, srcs, lambda s, off: place(s, before, off), jnp.int32(0))
            copy.wait()
            combine(before, True)

    def gather(s, off):
        off = pl.multiple_of(off, ALIGN)
        hit = pick(s, k)
        sel = hit.astype(F32).astype(BF16)
        gate = jnp.sum(jnp.where(hit, meta_ref[s, pl.ds(per_group + k, 1), lanes], 0.0), axis=1, keepdims=True)
        buf[pl.ds(off, size), 0:hidden] = dot(sel, xd_ref[s, :, 0:hidden], 1, 0).astype(BF16)
        buf[pl.ds(off, size), hidden:] = (gate * dot(sel, xd_ref[s, :, hidden:], 1, 0)).astype(BF16)
        return place(s, k, off)

    total = pl.multiple_of(lax.fori_loop(0, srcs, gather, jnp.int32(0)), ALIGN)
    buf[pl.ds(total, TILE), :] = jnp.zeros((TILE, width), BF16)
    if has_prev:
        load_prev().wait()

    def run(r0, rows):
        x = buf[pl.ds(r0, rows), 0:hidden]
        d = buf[pl.ds(r0, rows), hidden:]
        h = dot(x, w_ref[0, 0:hidden, :], 1, 0)
        da = dot(d, w_ref[0, hidden:, :], 1, 1)
        h1 = h[:, 0:ff]
        h3 = h[:, ff:]
        sig = jax.nn.sigmoid(h1)
        silu = h1 * sig
        a = (silu * h3).astype(BF16)
        dh1 = (da * h3 * sig * (1.0 + h1 * (1.0 - sig))).astype(BF16)
        dh3 = (da * silu).astype(BF16)
        dh = jnp.concatenate([dh1, dh3], axis=1)
        acc[0:hidden, :] += dot(x, dh, 0, 0)
        acc[hidden:, :] += dot(a, d, 0, 0)
        buf[pl.ds(r0, rows), 0:hidden] = dot(a, w_ref[0, hidden:, :], 1, 0).astype(BF16)
        buf[pl.ds(r0, rows), hidden:] = dot(dh, w_ref[0, 0:hidden, :], 1, 1).astype(BF16)

    units = (total + TILE // 2 - 1) // (TILE // 2)

    @pl.loop(0, units // 2)
    def _(i):
        run(pl.multiple_of(i * TILE, TILE), TILE)

    @pl.when(units % 2 == 1)
    def _():
        run(pl.multiple_of((units - 1) * (TILE // 2), TILE // 2), TILE // 2)

    each_grad(step, lambda copy: copy.start())

    if carry_out:
        copy = pltpu.make_async_copy(buf, rows_ref, row_sem)
        copy.start()
        copy.wait()
    elif carry_in:
        combine(k, False)
    else:
        @pl.when(step == 0)
        def _():
            combine(k, True)

        @pl.when(step > 0)
        def _():
            combine(k, False)

    @pl.when(step == steps - 1)
    def _():
        if not carry_out:
            for s in range(srcs):
                slot = s % 2
                if s >= 2:
                    pltpu.make_async_copy(stage.at[slot], rows_ref.at[s - 2], pq_sem.at[slot]).wait()
                stage[slot] = pq[s].astype(BF16)
                pltpu.make_async_copy(stage.at[slot], rows_ref.at[s], pq_sem.at[slot]).start()
            for s in range(max(0, srcs - 2), srcs):
                pltpu.make_async_copy(stage.at[s % 2], rows_ref.at[s], pq_sem.at[s % 2]).wait()
        each_grad(step, lambda copy: copy.wait())


def run_experts(chunk, order, positions, meta, xd, w, prev=None, carried=None, carry_out=False, split=False):
    srcs, size, width = xd.shape
    _, rows, hidden = w.shape
    first, steps = positions[0], len(positions)
    any_spec = pl.BlockSpec(memory_space=pl.ANY)
    vmem = pl.BlockSpec(memory_space=pltpu.VMEM)
    buf_rows = srcs * size + max(size, TILE)
    extra = [a for a in (prev, carried) if a is not None]
    n = srcs * size // 2
    if split:
        parts = grad_parts(hidden, rows - hidden)
        grads = [jax.ShapeDtypeStruct((r.size, c.size), F32) for _ in range(steps) for r, c in parts]
    else:
        grads = [jax.ShapeDtypeStruct((steps, rows, hidden), F32)]
    scratch = [
        pltpu.VMEM((buf_rows, width), BF16),
        pltpu.VMEM((rows, hidden), F32),
        pltpu.SMEM((srcs,), jnp.int32),
        pltpu.SemaphoreType.DMA,
        pltpu.SemaphoreType.DMA((4,)),
        pltpu.SemaphoreType.DMA,
    ]
    if not carry_out:
        scratch += [pltpu.VMEM((srcs, size, width), F32), pltpu.VMEM((2, size, width), BF16), pltpu.SemaphoreType.DMA((2,))]
    return pl.pallas_call(
        functools.partial(expert_kernel, chunk, first, steps, prev is not None, carried is not None, carry_out, split),
        grid_spec=pltpu.PrefetchScalarGridSpec(
            num_scalar_prefetch=1,
            grid=(steps,),
            in_specs=[vmem, vmem, pl.BlockSpec((1, rows, hidden), lambda k, o: (o[first + k], 0, 0))] + [any_spec] * len(extra),
            out_specs=[any_spec] * (1 + len(grads)),
            scratch_shapes=scratch,
        ),
        out_shape=(jax.ShapeDtypeStruct((buf_rows, width) if carry_out else xd.shape, BF16), *grads),
        compiler_params=pltpu.CompilerParams(vmem_limit_bytes=63 * 1024 * 1024, dimension_semantics=('arbitrary',)),
        cost_estimate=pl.CostEstimate(flops=steps * n * (6 * rows * hidden + 8 * size * hidden), bytes_accessed=srcs * size * width * 4, transcendentals=0),
        name='run_experts',
    )(order, meta, xd, w, *extra)


def home_kernel(slot_ref, *refs):
    rets, (y_ref, dx_ref) = refs[:-2], refs[-2:]
    groups, size, width = rets[0].shape
    acc = None
    for c, ret in enumerate(rets):
        for g in range(groups):
            part = dot(pick_rows(slot_ref[g:g + 1, :], c * size, size), ret[g], 0, 0)
            acc = part if acc is None else acc + part
    y_ref[...] = acc[:, :width // 2].astype(BF16)
    dx_ref[...] = acc[:, width // 2:].astype(BF16)


def home_sum(slot, rets, block):
    groups, tokens = slot.shape
    _, size, width = rets[0].shape
    out = jax.ShapeDtypeStruct((tokens, width // 2), BF16)
    return pl.pallas_call(
        home_kernel,
        grid=(tokens // block,),
        out_shape=(out, out),
        in_specs=[pl.BlockSpec((groups, block), lambda i: (0, i))] + [pl.BlockSpec(memory_space=pltpu.VMEM)] * len(rets),
        out_specs=(pl.BlockSpec((block, width // 2), lambda i: (i, 0)),) * 2,
        compiler_params=pltpu.CompilerParams(vmem_limit_bytes=48 * 1024 * 1024),
        cost_estimate=pl.CostEstimate(flops=2 * groups * len(rets) * size * tokens * width, bytes_accessed=groups * size * width * 4, transcendentals=0),
        name='home_sum',
    )(slot, *rets)


def solution(mesh):
    groups = mesh.shape['grp']
    inner = mesh.shape['ing']
    tok_spec = P(('dp', 'grp', 'ing'), None)
    weight_spec = P(('grp', 'ing'), None, None)
    grad_spec = P(('dp', 'grp', 'ing'), None, None)
    chunks = 2

    def layer(x_loc, ids_loc, gates_loc, dy_loc, wg_loc, wu_loc, wd_loc):
        tokens, _ = x_loc.shape
        top_k = ids_loc.shape[1]
        per_group = wg_loc.shape[0] * inner
        group_limit = min(max(1, groups // 2), top_k // 2)
        cap = tokens * group_limit // groups
        swap = lambda a: lax.all_to_all(a, 'grp', 0, 0, tiled=True)
        w_own = jnp.concatenate([jnp.concatenate([wg_loc, wu_loc], axis=2), wd_loc], axis=1)
        w_all = lax.all_gather(w_own, 'ing', axis=0, tiled=True)
        size = cap // chunks
        slot, meta = make_tables(ids_loc.T, gates_loc.T, groups, per_group, cap, size)
        meta = swap(meta)
        recv = []
        for c in range(chunks):
            packed = pack_rows(slot, x_loc, dy_loc, c, size)
            if c == 0:
                packed, slot, meta = lax.optimization_barrier((packed, slot, meta))
            recv.append(swap(packed))
        me = lax.axis_index('ing')
        away = [inner // 2] + [i for i in range(1, inner) if i != inner // 2] + [0]
        order = (me + jnp.asarray(away, jnp.int32)) % inner
        everyone = list(range(per_group))
        ring = lambda a, d: lax.ppermute(a, 'ing', [(i, (i + d) % inner) for i in range(inner)])
        grads = None
        rets = []
        for c in range(chunks - 1):
            pq, grads = run_experts(c, order, everyone, meta, recv[c], w_all, grads)
            rets.append(swap(pq))
        c = chunks - 1
        ways = (1, -1, 1, -1)
        rows, *far = run_experts(c, order, everyone[:1], meta, recv[c], w_all, grads, None, True, True)
        for i, way in enumerate(ways):
            far[i] = ring(far[i], way)
        pq, *parts = run_experts(c, order, everyone[1:], meta, recv[c], w_all, grads, rows, False, True)
        after, before, own = parts[:4], parts[4:8], parts[8:]
        sums = [None] * 4
        for late in (False, True):
            for i, way in enumerate(ways):
                up, down = after[i], before[i]
                if late:
                    up, down = (up + far[i], None) if way == 1 else (None, down + far[i])
                else:
                    up, down = (None, down) if way == 1 else (up, None)
                sums[i] = (sums[i] or ()) + ((ring(up, 1),) if up is not None else (ring(down, -1),))
        rets.append(swap(pq))
        y_out, dx_out = home_sum(slot, rets, 256)
        g1, g3, g2a, g2b = [a + (b[0] + b[1]) for a, b in zip(own, sums)]
        return y_out, dx_out, g1[None], g3[None], jnp.concatenate([g2a, g2b], axis=0)[None]

    return jax.shard_map(layer, mesh=mesh, in_specs=(tok_spec, tok_spec, tok_spec, tok_spec, weight_spec, weight_spec, weight_spec), out_specs=(tok_spec, tok_spec, grad_spec, grad_spec, grad_spec), check_vma=False)
```

time: 2490 us -> 610 us (0.24)
  local copies, waits for them, and re-layouts: 1250 us -> 2.66 us
  waiting for transfers between devices: 746 us -> 268 us
  Pallas kernels: 0 us -> 265 us
  matrix products: 230 us -> 0 us
  other arithmetic: 179 us -> 11.8 us
    gather x19 -> x0, local copies, waits for them, and re-layouts: 956 us -> none  [the longest x3 279 us: expert_stage(): jnp.take_along_axis(exp_pos, jnp.minimum(loc_exp, per_group - 1), axis=1)]
    all_to_all x10 -> x5, waiting for transfers between devices: 746 us -> 80.2 us  [layer(): swap = lambda a: lax.all_to_all(a, 'grp', 0, 0, tiled=True)]
    scatter x3 -> x0, local copies, waits for them, and re-layouts: 272 us -> none  [the longest x1 121 us: expert_stage(): jnp.zeros((per_group * in_cap,), jnp.float32).at[fwd_slot.reshape(-1)]]
    pallas_call x0 -> x7, Pallas kernels: none -> 265 us  [the longest x3 206 us: run_experts(): pl.pallas_call(functools.partial(expert_kernel, chunk, first, steps, prev...]
    dot_general x9 -> x0, matrix products: 230 us -> none  [the longest x1 45.2 us: expert_stage(): jnp.einsum('blcd,ldf->blcf', exp_x, wg_loc, preferred_element_type=jnp.fl...]
    ppermute x0 -> x12, waiting for transfers between devices: none -> 187 us  [layer(): lax.ppermute(a, 'ing', [(i, (i + d) % inner) for i in range(inner)])]
    reduce_sum x3 -> x0, other arithmetic: 139 us -> none  [the longest x1 54 us: expert_stage(): jnp.sum(jnp.where(in_group[:, :, None], back_dx[take_slot].astype(jnp.flo...]
    all_to_all x10 -> x5, starting transfers between devices: 70.5 us -> 27.6 us  [layer(): swap = lambda a: lax.all_to_all(a, 'grp', 0, 0, tiled=True)]
  transfers between devices with their start and end apart: 10 -> 18, of which waited for: 4 -> 5; matrix products, arithmetic and copies ran while one was open for 57% -> 1% of each run, Pallas kernels for 0% -> 39%
where the time goes in v2:
time: 610 us; the launch traced here: 609 us
  waiting for transfers between devices  268 us (44%)
  Pallas kernels  265 us (43%)
  starting transfers between devices  48 us (8%)
  between operations  14.2 us (2%)
  other arithmetic  11.8 us (2%)
    pallas_call x3, Pallas kernels, run_experts(): pl.pallas_call(functools.partial(expert_kernel, chunk, first, steps, prev...  206 us
    ppermute x12, waiting for transfers between devices, layer(): lax.ppermute(a, 'ing', [(i, (i + d) % inner) for i in range(inner)])  187 us
    all_to_all x5, waiting for transfers between devices, layer(): swap = lambda a: lax.all_to_all(a, 'grp', 0, 0, tiled=True)  80.2 us
    pallas_call x2, Pallas kernels, pack_rows(): pl.pallas_call(functools.partial(pack_kernel, c * size), grid=(groups,),...  27.7 us
    all_to_all x5, starting transfers between devices, layer(): swap = lambda a: lax.all_to_all(a, 'grp', 0, 0, tiled=True)  27.6 us
    pallas_call x1, Pallas kernels, home_sum(): pl.pallas_call(home_kernel, grid=(tokens // block,), out_shape=(out, out)...  24.7 us
    ppermute x12, starting transfers between devices, layer(): lax.ppermute(a, 'ing', [(i, (i + d) % inner) for i in range(inner)])  20.3 us
  transfers between devices with their start and end apart: 18, of which 5 were waited for; matrix products, arithmetic and copies ran while one was open for 1% of the time, Pallas kernels for 39%

profile of v2, /device:TPU:97, one launch (start us, length us, event | category | flops | bytes accessed | tf_op | source)
XLA Modules:
  0.0 609.1 jit_solution(11671961245803906056)
XLA Ops:
  7.2 3.8 pad_maximum_fusion
  11.1 6.1 %make_tables.1 = (f32[8,1024]{1,0:T(8,128)}, f32[8,8,512]{2,1,0:T(8,128)}) custom-call(s32[8,1024]{1,0:T(8,128)} %bitcast.8, f32[8,1024]{1,0:T(8,128)} %bitcast.9), custom_call_target="tpu_custom_call" | custom-call | flops 1073741824 | bytes 262144 | tf_op jit(solution)/shard_map/make_tables/pallas_call | solution.py:76
  17.2 6.0 all-to-all-start
  23.3 14.3 %pack_rows.2 = bf16[8,256,2048]{2,1,0:T(8,128)(2,1)} custom-call(f32[8,1024]{1,0:T(8,128)} %get-tuple-element.34.slot_ref, bf16[1024,1024]{1,0:T(8,128)(2,1)} %x_ref.3, bf16[1024,1024]{1,0:T(8,128)(2,1)} %dy_ref.3), custom_call_target="tpu_custom_call" | custom-call | flops 8589934592 | bytes 8388608 | tf_op jit(solution)/shard_map/pack_rows/pallas_call | solution.py:98
  37.5 0.6 copy-done.9
  38.2 5.0 all-to-all-start.1
  43.2 13.4 %pack_rows.3 = bf16[8,256,2048]{2,1,0:T(8,128)(2,1)} custom-call(f32[8,1024]{1,0:T(8,128)} %get-tuple-element.34.slot_ref, bf16[1024,1024]{1,0:T(8,128)(2,1)} %x_ref.3, bf16[1024,1024]{1,0:T(8,128)(2,1)} %dy_ref.3), custom_call_target="tpu_custom_call" | custom-call | flops 8589934592 | bytes 8388608 | tf_op jit(solution)/shard_map/pack_rows/pallas_call | solution.py:98
  56.6 80.2 %all-to-all-done.1.xd_ref = bf16[8,256,2048]{2,1,0:T(8,128)(2,1)} async-done(((bf16[8,256,2048]{2,1,0:T(8,128)(2,1)}), bf16[8,256,2048]{2,1,0:T(8,128)(2,1)}, u32[]{:S(2)}, u32[]{:S(2)}) %all-to-all-start.1) | async-done | bytes 8388640 | tf_op jit(solution)/shard_map/all_to_all | solution.py:350
  136.8 5.8 all-to-all-start.3
  143.2 95.7 %run_experts.3 = (bf16[8,256,2048]{2,1,0:T(8,128)(2,1)}, f32[4,1536,1024]{2,1,0:T(8,128)}) custom-call(s32[4]{0:T(128)} %and_select_fusion.order_ref, f32[8,8,512]{2,1,0:T(8,128)} %copy-done.9, bf16[8,256,2048]{2,1,0:T(8,128)(2,1)} %all-to-all-done.1.xd_ref, bf16[4,1536,1024]{2,1,0:T(8,128)(2,1)} %all-gather.2.cloned.1.call-done.w_ref), custom_call_target="tpu_custom_call" | custom-call | flops 47244640256 | bytes 16777216 | tf_op jit(solution)/shard_map/run_experts/pallas_call | solution.py:292
  238.9 5.3 all-to-all-start.2
  244.2 25.6 %run_experts.4 = (bf16[2304,2048]{1,0:T(8,128)(2,1)}, f32[1024,512]{1,0:T(8,128)}, f32[1024,512]{1,0:T(8,128)}, f32[256,1024]{1,0:T(8,128)}, f32[256,1024]{1,0:T(8,128)}) custom-call(s32[4]{0:T(128)} %and_select_fusion.order_ref, f32[8,8,512]{2,1,0:T(8,128)} %copy-done.9, bf16[8,256,2048]{2,1,0:T(8,128)(2,1)} %all-to-all-done.3.xd_ref, ...), custom_call_target="tpu_custom_call" | custom-call | flops 11811160064 | bytes 16777216 | tf_op jit(solution)/shard_map/run_experts/pallas_call | solution.py:292
  269.8 85.1 %run_experts.5 = (bf16[8,256,2048]{2,1,0:T(8,128)(2,1)}, f32[1024,512]{1,0:T(8,128)}, f32[1024,512]{1,0:T(8,128)}, f32[256,1024]{1,0:T(8,128)}, f32[256,1024]{1,...) custom-call(s32[4]{0:T(128)} %and_select_fusion.order_ref, ...), custom_call_target="tpu_custom_call" | custom-call | flops 35433480192 | bytes 16777216 | tf_op jit(solution)/shard_map/run_experts/pallas_call | solution.py:292
  354.9 5.4 all-to-all-start.4
  360.4 5.7 collective-permute-start.1
  366.1 1.5 collective-permute-start.7
  367.6 1.2 collective-permute-start.6
  369.0 64.7 %collective-permute-done.7 = f32[256,1024]{1,0:T(8,128)S(1)} collective-permute-done((f32[256,1024]{1,0:T(8,128)}, f32[256,1024]{1,0:T(8,128)S(1)}, u32[]{:S(2)}, u32[]{:S(2)}) %collective-permute-start.7) | collective-permute-done | bytes 1048608 | tf_op jit(solution)/shard_map/ppermute | solution.py:366
  433.8 2.0 collective-permute-start.10
  436.7 1.1 copy-done.11
  437.8 2.5 collective-permute-start
  440.9 15.4 %collective-permute-done.9 = f32[256,1024]{1,0:T(8,128)S(1)} collective-permute-done((f32[256,1024]{1,0:T(8,128)}, f32[256,1024]{1,0:T(8,128)S(1)}, u32[]{:S(2)}, u32[]{:S(2)}) %collective-permute-start.9) | collective-permute-done | bytes 1048608 | tf_op jit(solution)/shard_map/ppermute | solution.py:366
  456.2 2.2 collective-permute-start.3
  458.4 2.5 collective-permute-start.5
  461.1 17.5 %collective-permute-done.8 = f32[256,1024]{1,0:T(8,128)S(1)} collective-permute-done((f32[256,1024]{1,0:T(8,128)S(1)}, f32[256,1024]{1,0:T(8,128)S(1)}, u32[]{:S(2)}, u32[]{:S(2)}) %collective-permute-start.8) | collective-permute-done | bytes 1048608 | tf_op jit(solution)/shard_map/ppermute | solution.py:366
  478.6 2.1 collective-permute-start.11
  481.0 89.6 %collective-permute-done.11 = f32[256,1024]{1,0:T(8,128)S(1)} collective-permute-done((f32[256,1024]{1,0:T(8,128)S(1)}, f32[256,1024]{1,0:T(8,128)S(1)}, u32[]{:S(2)}, u32[]{:S(2)}) %collective-permute-start.11) | collective-permute-done | bytes 1048608 | tf_op jit(solution)/shard_map/ppermute | solution.py:366
  571.0 1.5 maximum_bitcast_fusion
  572.5 0.9 copy-done.4
  573.3 2.1 add_bitcast_fusion.1
  575.4 2.1 add_bitcast_fusion
  577.5 24.7 %home_sum.1 = (bf16[1024,1024]{1,0:T(8,128)(2,1)}, bf16[1024,1024]{1,0:T(8,128)(2,1)}) custom-call(f32[8,1024]{1,0:T(8,128)S(1)} %copy-done, bf16[8,256,2048]{2,1,0:T(8,128)(2,1)} %all-to-all-done.2.refs_0_, bf16[8,256,2048]{2,1,0:T(8,128)(2,1)} %all-to-all-done.4.refs_1_), custom_call_target="tpu_custom_call" | custom-call | flops 17179869184 | bytes 16777216 | tf_op jit(solution)/shard_map/home_sum/pallas_call | solution.py:324
  (51 shorter events, 3.1 us)
Async XLA Ops:
  7.2 136.0 %all-gather.2.cloned.1.call-start = ((), (), s32[]{:S(2)}) async-start(), calls=%async_computation.5 | async-start | bytes 15728640 | tf_op jit(solution)/shard_map/all_gather | solution.py:352
  17.2 20.3 %all-to-all-start = ((f32[8,8,512]{2,1,0:T(8,128)}), f32[8,8,512]{2,1,0:T(8,128)S(1)}, u32[]{:S(2)}, u32[]{:S(2)}) async-start(f32[8,8,512]{2,1,0:T(8,128)} %get-tuple-element.33), calls=%async_computation | async-start | bytes 262144 | tf_op jit(solution)/shard_map/all_to_all | solution.py:350
  37.5 0.6 copy-start.9
  38.2 98.7 %all-to-all-start.1 = ((bf16[8,256,2048]{2,1,0:T(8,128)(2,1)}), bf16[8,256,2048]{2,1,0:T(8,128)(2,1)}, u32[]{:S(2)}, u32[]{:S(2)}) async-start(bf16[8,256,2048]{2,1,0:T(8,128)(2,1)} %pack_rows.2), calls=%async_computation.1 | async-start | bytes 16777216 | tf_op jit(solution)/shard_map/all_to_all | solution.py:350
  56.6 86.0 %copy-start.13 = (s32[4]{0:T(128)S(1)}, s32[4]{0:T(128)}, u32[]{:S(2)}) copy-start(s32[4]{0:T(128)} %constant.22.clone) | copy-start | bytes 52
  136.8 102.0 %all-to-all-start.3 = ((bf16[8,256,2048]{2,1,0:T(8,128)(2,1)}), bf16[8,256,2048]{2,1,0:T(8,128)(2,1)}, u32[]{:S(2)}, u32[]{:S(2)}) async-start(bf16[8,256,2048]{2,1,0:T(8,128)(2,1)} %pack_rows.3), calls=%async_computation.3 | async-start | bytes 16777216 | tf_op jit(solution)/shard_map/all_to_all | solution.py:350
  238.9 116.0 %all-to-all-start.2 = ((bf16[8,256,2048]{2,1,0:T(8,128)(2,1)}), bf16[8,256,2048]{2,1,0:T(8,128)(2,1)}, u32[]{:S(2)}, u32[]{:S(2)}) async-start(bf16[8,256,2048]{2,1,0:T(8,128)(2,1)} %get-tuple-element.37), calls=%async_computation.2 | async-start | bytes 16777216 | tf_op jit(solution)/shard_map/all_to_all | solution.py:350
  354.9 11.2 %copy-start.12 = (f32[1024,512]{1,0:T(8,128)S(1)}, f32[1024,512]{1,0:T(8,128)}, u32[]{:S(2)}) copy-start(f32[1024,512]{1,0:T(8,128)} %get-tuple-element.50) | copy-start | bytes 6291460
  354.9 80.9 %copy-start.6 = (f32[256,1024]{1,0:T(8,128)S(1)}, f32[256,1024]{1,0:T(8,128)}, u32[]{:S(2)}) copy-start(f32[256,1024]{1,0:T(8,128)} %get-tuple-element.53) | copy-start | bytes 3145732
  354.9 222.6 %all-to-all-start.4 = ((bf16[8,256,2048]{2,1,0:T(8,128)(2,1)}), bf16[8,256,2048]{2,1,0:T(8,128)(2,1)}, u32[]{:S(2)}, u32[]{:S(2)}) async-start(bf16[8,256,2048]{2,1,0:T(8,128)(2,1)} %get-tuple-element.40), calls=%async_computation.4 | async-start | bytes 16777216 | tf_op jit(solution)/shard_map/all_to_all | solution.py:350
  360.3 75.9 %copy-start.2 = (f32[1024,512]{1,0:T(8,128)S(1)}, f32[1024,512]{1,0:T(8,128)}, u32[]{:S(2)}) copy-start(f32[1024,512]{1,0:T(8,128)} %get-tuple-element.45) | copy-start | bytes 6291460
  360.4 75.6 %collective-permute-start.1 = (f32[1024,512]{1,0:T(8,128)}, f32[1024,512]{1,0:T(8,128)S(1)}, u32[]{:S(2)}, u32[]{:S(2)}) collective-permute-start(f32[1024,512]{1,0:T(8,128)} %get-tuple-element.46), channel_id=1, source_target_pairs={{0,8},{8,16},{16,24},{24,0},{1,9},{9,17},{17,25},{25,1},{2,10},{10... | collective-permute-start | bytes 6291464 | tf_op jit(solution)/shard_map/ppermute | solution.py:366
  366.1 74.2 %collective-permute-start.4 = (f32[1024,512]{1,0:T(8,128)S(1)}, f32[1024,512]{1,0:T(8,128)S(1)}, u32[]{:S(2)}, u32[]{:S(2)}) collective-permute-start(f32[1024,512]{1,0:T(8,128)S(1)} %copy-done.12), channel_id=1, source_target_pairs={{0,24},{8,0},{16,8},{24,16},{1,25},{9,1},{17,9},{25,17},{2,26},{10... | collective-permute-start | bytes 6291464 | tf_op jit(solution)/shard_map/ppermute | solution.py:366
  366.1 67.7 %collective-permute-start.7 = (f32[256,1024]{1,0:T(8,128)}, f32[256,1024]{1,0:T(8,128)S(1)}, u32[]{:S(2)}, u32[]{:S(2)}) collective-permute-start(f32[256,1024]{1,0:T(8,128)} %get-tuple-element.54), channel_id=1, source_target_pairs={{0,8},{8,16},{16,24},{24,0},{1,9},{9,17},{17,25},{25,1},{2,10},{10... | collective-permute-start | bytes 3145736 | tf_op jit(solution)/shard_map/ppermute | solution.py:366
  367.6 69.2 %collective-permute-start.6 = (f32[256,1024]{1,0:T(8,128)}, f32[256,1024]{1,0:T(8,128)S(1)}, u32[]{:S(2)}, u32[]{:S(2)}) collective-permute-start(f32[256,1024]{1,0:T(8,128)} %get-tuple-element.52), channel_id=1, source_target_pairs={{0,24},{8,0},{16,8},{24,16},{1,25},{9,1},{17,9},{25,17},{2,26},{10... | collective-permute-start | bytes 3145736 | tf_op jit(solution)/shard_map/ppermute | solution.py:366
  368.8 87.5 %collective-permute-start.9 = (f32[256,1024]{1,0:T(8,128)}, f32[256,1024]{1,0:T(8,128)S(1)}, u32[]{:S(2)}, u32[]{:S(2)}) collective-permute-start(f32[256,1024]{1,0:T(8,128)} %get-tuple-element.56), channel_id=1, source_target_pairs={{0,8},{8,16},{16,24},{24,0},{1,9},{9,17},{17,25},{25,1},{2,10},{10... | collective-permute-start | bytes 3145736 | tf_op jit(solution)/shard_map/ppermute | solution.py:366
  433.8 24.7 %collective-permute-start.10 = (f32[256,1024]{1,0:T(8,128)}, f32[256,1024]{1,0:T(8,128)S(1)}, u32[]{:S(2)}, u32[]{:S(2)}) collective-permute-start(f32[256,1024]{1,0:T(8,128)} %get-tuple-element.58), channel_id=1, source_target_pairs={{0,24},{8,0},{16,8},{24,16},{1,25},{9,1},{17,9},{25,17},{2,26},{10... | collective-permute-start | bytes 3145736 | tf_op jit(solution)/shard_map/ppermute | solution.py:366
  436.0 42.6 %collective-permute-start.8 = (f32[256,1024]{1,0:T(8,128)S(1)}, f32[256,1024]{1,0:T(8,128)S(1)}, u32[]{:S(2)}, u32[]{:S(2)}) collective-permute-start(f32[256,1024]{1,0:T(8,128)S(1)} %add.57), channel_id=1, source_target_pairs={{0,8},{8,16},{16,24},{24,0},{1,9},{9,17},{17,25},{25,1},{2,10},{10... | collective-permute-start | bytes 3145736 | tf_op jit(solution)/shard_map/ppermute | solution.py:366
  436.2 1.6 copy-start.11
  436.2 4.1 copy-start.1
  437.8 134.6 %collective-permute-start = (f32[1024,512]{1,0:T(8,128)S(1)}, f32[1024,512]{1,0:T(8,128)S(1)}, u32[]{:S(2)}, u32[]{:S(2)}) collective-permute-start(f32[1024,512]{1,0:T(8,128)S(1)} %copy-done.11), channel_id=1, source_target_pairs={{0,24},{8,0},{16,8},{24,16},{1,25},{9,1},{17,9},{25,17},{2,26},{10... | collective-permute-start | bytes 6291464 | tf_op jit(solution)/shard_map/ppermute | solution.py:366
  440.3 132.1 %collective-permute-start.2 = (f32[1024,512]{1,0:T(8,128)S(1)}, f32[1024,512]{1,0:T(8,128)S(1)}, u32[]{:S(2)}, u32[]{:S(2)}) collective-permute-start(f32[1024,512]{1,0:T(8,128)S(1)} %add.51), channel_id=1, source_target_pairs={{0,8},{8,16},{16,24},{24,0},{1,9},{9,17},{17,25},{25,1},{2,10},{10... | collective-permute-start | bytes 6291464 | tf_op jit(solution)/shard_map/ppermute | solution.py:366
  440.3 15.9 %copy-start.10 = (f32[1024,512]{1,0:T(8,128)S(1)}, f32[1024,512]{1,0:T(8,128)}, u32[]{:S(2)}) copy-start(f32[1024,512]{1,0:T(8,128)} %get-tuple-element.48) | copy-start | bytes 6291460
  440.4 20.6 %copy-start.5 = (f32[256,1024]{1,0:T(8,128)S(1)}, f32[256,1024]{1,0:T(8,128)}, u32[]{:S(2)}) copy-start(f32[256,1024]{1,0:T(8,128)} %get-tuple-element.57) | copy-start | bytes 3145732
  440.9 39.9 %copy-start.8 = (f32[256,1024]{1,0:T(8,128)S(1)}, f32[256,1024]{1,0:T(8,128)}, u32[]{:S(2)}) copy-start(f32[256,1024]{1,0:T(8,128)} %get-tuple-element.51) | copy-start | bytes 3145732
  456.2 119.2 %collective-permute-start.3 = (f32[1024,512]{1,0:T(8,128)S(1)}, f32[1024,512]{1,0:T(8,128)S(1)}, u32[]{:S(2)}, u32[]{:S(2)}) collective-permute-start(f32[1024,512]{1,0:T(8,128)S(1)} %copy-done.10), channel_id=1, source_target_pairs={{0,8},{8,16},{16,24},{24,0},{1,9},{9,17},{17,25},{25,1},{2,10},{10... | collective-permute-start | bytes 6291464 | tf_op jit(solution)/shard_map/ppermute | solution.py:366
  458.4 117.0 %collective-permute-start.5 = (f32[1024,512]{1,0:T(8,128)S(1)}, f32[1024,512]{1,0:T(8,128)S(1)}, u32[]{:S(2)}, u32[]{:S(2)}) collective-permute-start(f32[1024,512]{1,0:T(8,128)S(1)} %add.54), channel_id=1, source_target_pairs={{0,24},{8,0},{16,8},{24,16},{1,25},{9,1},{17,9},{25,17},{2,26},{10... | collective-permute-start | bytes 6291464 | tf_op jit(solution)/shard_map/ppermute | solution.py:366
  478.6 92.1 %collective-permute-start.11 = (f32[256,1024]{1,0:T(8,128)S(1)}, f32[256,1024]{1,0:T(8,128)S(1)}, u32[]{:S(2)}, u32[]{:S(2)}) collective-permute-start(f32[256,1024]{1,0:T(8,128)S(1)} %add.60), channel_id=1, source_target_pairs={{0,24},{8,0},{16,8},{24,16},{1,25},{9,1},{17,9},{25,17},{2,26},{10... | collective-permute-start | bytes 3145736 | tf_op jit(solution)/shard_map/ppermute | solution.py:366
  480.7 89.9 %copy-start.7 = (f32[256,1024]{1,0:T(8,128)S(1)}, f32[256,1024]{1,0:T(8,128)}, u32[]{:S(2)}) copy-start(f32[256,1024]{1,0:T(8,128)} %get-tuple-element.55) | copy-start | bytes 3145732
  571.0 2.3 copy-start.4
  573.3 2.1 copy-start.3
  575.4 2.1 copy-start
Sparse Core Ops, SparseCore 0:
  11.3 119.7 all-gather.1

commit v3 on v2

--- a/solution.py
+++ b/solution.py
@@ -107,24 +107,15 @@
     )(slot, x, dy)
 
 
-def grad_parts(hidden, ff):
-    mid = hidden + ff // 2
-    return (
-        (pl.ds(0, hidden), pl.ds(0, ff)),
-        (pl.ds(0, hidden), pl.ds(ff, ff)),
-        (pl.ds(hidden, ff // 2), pl.ds(0, hidden)),
-        (pl.ds(mid, ff // 2), pl.ds(0, hidden)),
-    )
-
-
-def expert_kernel(chunk, first_pos, steps, has_prev, carry_in, carry_out, split, order_ref, meta_ref, xd_ref, w_ref, *refs):
+def expert_kernel(chunk, first_pos, steps, has_prev, sums_in, sums_out, order_ref, meta_ref, xd_ref, w_ref, *refs):
     refs = list(refs)
     prev = refs.pop(0) if has_prev else None
-    carried = refs.pop(0) if carry_in else None
+    before = refs.pop(0) if sums_in else None
     rows_ref = refs.pop(0)
-    grad_refs = [refs.pop(0) for _ in range(4 * steps if split else 1)]
-    buf, acc, offs, in_sem, out_sem, row_sem = refs[:6]
-    pq, stage, pq_sem = (None,) * 3 if carry_out else refs[6:]
+    split = sums_in or sums_out
+    grad_refs = [refs.pop(0) for _ in range(2 * steps if split else 1)]
+    buf, acc, pq, offs, in_sem, out_sem, sum_sem = refs[:7]
+    stage, pq_sem = (None, None) if sums_out else refs[7:]
     step = pl.program_id(0)
     k = order_ref[first_pos + step]
     srcs, size, width = xd_ref.shape
@@ -141,8 +132,8 @@
         for i in range(steps):
             @pl.when(at == i)
             def _(i=i):
-                for j, (rows, cols) in enumerate(grad_parts(hidden, ff)):
-                    act(pltpu.make_async_copy(acc.at[rows, cols], grad_refs[4 * i + j], out_sem.at[j]))
+                for j in range(2):
+                    act(pltpu.make_async_copy(acc.at[:, pl.ds(j * ff, ff)], grad_refs[2 * i + j], out_sem.at[j]))
 
     def load_prev():
         return pltpu.make_async_copy(prev.at[first_pos + step], acc, in_sem)
@@ -156,59 +147,36 @@
     else:
         acc[...] = jnp.zeros_like(acc)
 
-    def pick(s, k):
+    if sums_in:
+        @pl.when(step == 0)
+        def _():
+            pltpu.make_async_copy(before, pq, sum_sem).start()
+
+    def pick(s):
         slot = (lax.broadcasted_iota(jnp.int32, (size, size), 0) + 1).astype(F32)
         return meta_ref[s, pl.ds(k, 1), lanes] == slot
 
-    def place(s, k, off):
-        offs[s] = off
-        count = jnp.max(meta_ref[s, pl.ds(k, 1), lanes]).astype(jnp.int32)
-        return off + (count + ALIGN - 1) // ALIGN * ALIGN
-
-    def combine(k, first):
-        @pl.loop(0, srcs)
-        def _(s):
-            off = pl.multiple_of(offs[s], ALIGN)
-            sel = pick(s, k).astype(F32).astype(BF16)
-            cols = jnp.transpose(meta_ref[s, :, lanes])
-            lane = lax.broadcasted_iota(jnp.int32, (size, rows2), 1)
-            gate = jnp.sum(jnp.where(lane == per_group + k, cols, 0.0), axis=1, keepdims=True)
-            p = gate * dot(sel, buf[pl.ds(off, size), 0:hidden], 0, 0)
-            q = dot(sel, buf[pl.ds(off, size), hidden:], 0, 0)
-            if first:
-                pq[s, :, 0:hidden] = p
-                pq[s, :, hidden:] = q
-            else:
-                pq[s, :, 0:hidden] += p
-                pq[s, :, hidden:] += q
-
-    if carry_in:
-        @pl.when(step == 0)
-        def _():
-            copy = pltpu.make_async_copy(carried, buf, row_sem)
-            copy.start()
-            before = order_ref[first_pos - 1]
-            lax.fori_loop(0, srcs, lambda s, off: place(s, before, off), jnp.int32(0))
-            copy.wait()
-            combine(before, True)
-
     def gather(s, off):
         off = pl.multiple_of(off, ALIGN)
-        hit = pick(s, k)
+        offs[s] = off
+        hit = pick(s)
         sel = hit.astype(F32).astype(BF16)
         gate = jnp.sum(jnp.where(hit, meta_ref[s, pl.ds(per_group + k, 1), lanes], 0.0), axis=1, keepdims=True)
         buf[pl.ds(off, size), 0:hidden] = dot(sel, xd_ref[s, :, 0:hidden], 1, 0).astype(BF16)
         buf[pl.ds(off, size), hidden:] = (gate * dot(sel, xd_ref[s, :, hidden:], 1, 0)).astype(BF16)
-        return place(s, k, off)
+        count = jnp.max(meta_ref[s, pl.ds(k, 1), lanes]).astype(jnp.int32)
+        return off + (count + ALIGN - 1) // ALIGN * ALIGN
 
     total = pl.multiple_of(lax.fori_loop(0, srcs, gather, jnp.int32(0)), ALIGN)
     buf[pl.ds(total, TILE), :] = jnp.zeros((TILE, width), BF16)
     if has_prev:
         load_prev().wait()
 
-    def run(r0, rows):
-        x = buf[pl.ds(r0, rows), 0:hidden]
-        d = buf[pl.ds(r0, rows), hidden:]
+    @pl.loop(0, (total + TILE - 1) // TILE)
+    def _(i):
+        tile = pl.ds(pl.multiple_of(i * TILE, TILE), TILE)
+        x = buf[tile, 0:hidden]
+        d = buf[tile, hidden:]
         h = dot(x, w_ref[0, 0:hidden, :], 1, 0)
         da = dot(d, w_ref[0, hidden:, :], 1, 1)
         h1 = h[:, 0:ff]
@@ -221,39 +189,50 @@
         dh = jnp.concatenate([dh1, dh3], axis=1)
         acc[0:hidden, :] += dot(x, dh, 0, 0)
         acc[hidden:, :] += dot(a, d, 0, 0)
-        buf[pl.ds(r0, rows), 0:hidden] = dot(a, w_ref[0, hidden:, :], 1, 0).astype(BF16)
-        buf[pl.ds(r0, rows), hidden:] = dot(dh, w_ref[0, 0:hidden, :], 1, 1).astype(BF16)
-
-    units = (total + TILE // 2 - 1) // (TILE // 2)
-
-    @pl.loop(0, units // 2)
-    def _(i):
-        run(pl.multiple_of(i * TILE, TILE), TILE)
-
-    @pl.when(units % 2 == 1)
-    def _():
-        run(pl.multiple_of((units - 1) * (TILE // 2), TILE // 2), TILE // 2)
+        buf[tile, 0:hidden] = dot(a, w_ref[0, hidden:, :], 1, 0).astype(BF16)
+        buf[tile, hidden:] = dot(dh, w_ref[0, 0:hidden, :], 1, 1).astype(BF16)
 
     each_grad(step, lambda copy: copy.start())
-
-    if carry_out:
-        copy = pltpu.make_async_copy(buf, rows_ref, row_sem)
-        copy.start()
-        copy.wait()
-    elif carry_in:
-        combine(k, False)
+    if sums_in:
+        @pl.when(step == 0)
+        def _():
+            pltpu.make_async_copy(before, pq, sum_sem).wait()
+
+    def combine(first):
+        @pl.loop(0, srcs)
+        def _(s):
+            off = pl.multiple_of(offs[s], ALIGN)
+            sel = pick(s).astype(F32).astype(BF16)
+            cols = jnp.transpose(meta_ref[s, :, lanes])
+            lane = lax.broadcasted_iota(jnp.int32, (size, rows2), 1)
+            gate = jnp.sum(jnp.where(lane == per_group + k, cols, 0.0), axis=1, keepdims=True)
+            p = gate * dot(sel, buf[pl.ds(off, size), 0:hidden], 0, 0)
+            q = dot(sel, buf[pl.ds(off, size), hidden:], 0, 0)
+            if first:
+                pq[s, :, 0:hidden] = p
+                pq[s, :, hidden:] = q
+            else:
+                pq[s, :, 0:hidden] += p
+                pq[s, :, hidden:] += q
+
+    if sums_in or steps == 1:
+        combine(not sums_in)
     else:
         @pl.when(step == 0)
         def _():
-            combine(k, True)
+            combine(True)
 
         @pl.when(step > 0)
         def _():
-            combine(k, False)
+            combine(False)
 
     @pl.when(step == steps - 1)
     def _():
-        if not carry_out:
+        if sums_out:
+            copy = pltpu.make_async_copy(pq, rows_ref, sum_sem)
+            copy.start()
+            copy.wait()
+        else:
             for s in range(srcs):
                 slot = s % 2
                 if s >= 2:
@@ -265,32 +244,31 @@
         each_grad(step, lambda copy: copy.wait())
 
 
-def run_experts(chunk, order, positions, meta, xd, w, prev=None, carried=None, carry_out=False, split=False):
+def run_experts(chunk, order, positions, meta, xd, w, prev=None, sums=None, more=None):
     srcs, size, width = xd.shape
     _, rows, hidden = w.shape
     first, steps = positions[0], len(positions)
     any_spec = pl.BlockSpec(memory_space=pl.ANY)
     vmem = pl.BlockSpec(memory_space=pltpu.VMEM)
-    buf_rows = srcs * size + max(size, TILE)
-    extra = [a for a in (prev, carried) if a is not None]
+    extra = [a for a in (prev, sums) if a is not None]
     n = srcs * size // 2
-    if split:
-        parts = grad_parts(hidden, rows - hidden)
-        grads = [jax.ShapeDtypeStruct((r.size, c.size), F32) for _ in range(steps) for r, c in parts]
+    if more is None:
+        grads = [jax.ShapeDtypeStruct((steps, rows, hidden), F32)]
     else:
-        grads = [jax.ShapeDtypeStruct((steps, rows, hidden), F32)]
+        grads = [jax.ShapeDtypeStruct((rows, hidden // 2), F32)] * (2 * steps)
     scratch = [
-        pltpu.VMEM((buf_rows, width), BF16),
+        pltpu.VMEM((srcs * size + max(size, TILE), width), BF16),
         pltpu.VMEM((rows, hidden), F32),
+        pltpu.VMEM((srcs, size, width), F32),
         pltpu.SMEM((srcs,), jnp.int32),
         pltpu.SemaphoreType.DMA,
-        pltpu.SemaphoreType.DMA((4,)),
+        pltpu.SemaphoreType.DMA((2,)),
         pltpu.SemaphoreType.DMA,
     ]
-    if not carry_out:
-        scratch += [pltpu.VMEM((srcs, size, width), F32), pltpu.VMEM((2, size, width), BF16), pltpu.SemaphoreType.DMA((2,))]
+    if not more:
+        scratch += [pltpu.VMEM((2, size, width), BF16), pltpu.SemaphoreType.DMA((2,))]
     return pl.pallas_call(
-        functools.partial(expert_kernel, chunk, first, steps, prev is not None, carried is not None, carry_out, split),
+        functools.partial(expert_kernel, chunk, first, steps, prev is not None, sums is not None, bool(more)),
         grid_spec=pltpu.PrefetchScalarGridSpec(
             num_scalar_prefetch=1,
             grid=(steps,),
@@ -298,39 +276,79 @@
             out_specs=[any_spec] * (1 + len(grads)),
             scratch_shapes=scratch,
         ),
-        out_shape=(jax.ShapeDtypeStruct((buf_rows, width) if carry_out else xd.shape, BF16), *grads),
+        out_shape=(jax.ShapeDtypeStruct(xd.shape, F32 if more else BF16), *grads),
         compiler_params=pltpu.CompilerParams(vmem_limit_bytes=63 * 1024 * 1024, dimension_semantics=('arbitrary',)),
         cost_estimate=pl.CostEstimate(flops=steps * n * (6 * rows * hidden + 8 * size * hidden), bytes_accessed=srcs * size * width * 4, transcendentals=0),
         name='run_experts',
     )(order, meta, xd, w, *extra)
 
 
-def home_kernel(slot_ref, *refs):
-    rets, (y_ref, dx_ref) = refs[:-2], refs[-2:]
-    groups, size, width = rets[0].shape
-    acc = None
-    for c, ret in enumerate(rets):
-        for g in range(groups):
-            part = dot(pick_rows(slot_ref[g:g + 1, :], c * size, size), ret[g], 0, 0)
-            acc = part if acc is None else acc + part
-    y_ref[...] = acc[:, :width // 2].astype(BF16)
-    dx_ref[...] = acc[:, width // 2:].astype(BF16)
-
-
-def home_sum(slot, rets, block):
+def home_kernel(first, slot_ref, ret_ref, *refs):
+    groups, size, width = ret_ref.shape
+    acc = refs[0][...] if first else None
+    outs = refs[1:] if first else refs
+    for g in range(groups):
+        part = dot(pick_rows(slot_ref[g:g + 1, :], first, size), ret_ref[g], 0, 0)
+        acc = part if acc is None else acc + part
+    if len(outs) == 1:
+        outs[0][...] = acc
+    else:
+        outs[0][...] = acc[:, :width // 2].astype(BF16)
+        outs[1][...] = acc[:, width // 2:].astype(BF16)
+
+
+def home_sum(slot, ret, c, before, last, block):
     groups, tokens = slot.shape
-    _, size, width = rets[0].shape
-    out = jax.ShapeDtypeStruct((tokens, width // 2), BF16)
+    _, size, width = ret.shape
+    rows = lambda w: pl.BlockSpec((block, w), lambda i: (i, 0))
+    hidden = width // 2
+    outs = [(hidden, BF16)] * 2 if last else [(width, F32)]
+    extra = [] if before is None else [before]
     return pl.pallas_call(
-        home_kernel,
+        functools.partial(home_kernel, c * size),
         grid=(tokens // block,),
-        out_shape=(out, out),
-        in_specs=[pl.BlockSpec((groups, block), lambda i: (0, i))] + [pl.BlockSpec(memory_space=pltpu.VMEM)] * len(rets),
-        out_specs=(pl.BlockSpec((block, width // 2), lambda i: (i, 0)),) * 2,
+        out_shape=[jax.ShapeDtypeStruct((tokens, w), t) for w, t in outs],
+        in_specs=[pl.BlockSpec((groups, block), lambda i: (0, i)), pl.BlockSpec(memory_space=pltpu.VMEM)] + [rows(width)] * len(extra),
+        out_specs=[rows(w) for w, _ in outs],
         compiler_params=pltpu.CompilerParams(vmem_limit_bytes=48 * 1024 * 1024),
-        cost_estimate=pl.CostEstimate(flops=2 * groups * len(rets) * size * tokens * width, bytes_accessed=groups * size * width * 4, transcendentals=0),
+        cost_estimate=pl.CostEstimate(flops=2 * groups * size * tokens * width, bytes_accessed=groups * size * width * 2, transcendentals=0),
         name='home_sum',
-    )(slot, *rets)
+    )(slot, ret, *extra)
+
+
+def finish_kernel(*refs):
+    g1_ref, g3_ref, g2_ref = refs[6:]
+    tops = pl.num_programs(0) - pl.num_programs(0) // 3
+    i = pl.program_id(0)
+    left = refs[0][...] + (refs[1][...] + refs[2][...])
+    right = refs[3][...] + (refs[4][...] + refs[5][...])
+
+    @pl.when(i < tops)
+    def _():
+        g1_ref[0] = left
+        g3_ref[0] = right
+
+    @pl.when(i >= tops)
+    def _():
+        g2_ref[0] = jnp.concatenate([left, right], axis=1)
+
+
+def finish(lefts, rights, hidden):
+    rows, ff = lefts[0].shape
+    assert rows == hidden + ff and hidden == 2 * ff
+    block = ff // 2
+    tops = hidden // block
+    top = pl.BlockSpec((1, block, ff), lambda i: (0, jnp.minimum(i, tops - 1), 0))
+    return pl.pallas_call(
+        finish_kernel,
+        grid=(rows // block,),
+        out_shape=[jax.ShapeDtypeStruct((1,) + a, F32) for a in ((hidden, ff), (hidden, ff), (ff, hidden))],
+        in_specs=[pl.BlockSpec((block, ff), lambda i: (i, 0))] * 6,
+        out_specs=[top, top, pl.BlockSpec((1, block, hidden), lambda i: (0, jnp.maximum(i - tops, 0), 0))],
+        compiler_params=pltpu.CompilerParams(vmem_limit_bytes=58 * 1024 * 1024),
+        cost_estimate=pl.CostEstimate(flops=4 * rows * ff, bytes_accessed=32 * rows * ff, transcendentals=0),
+        name='finish',
+    )(*lefts, *rights)
 
 
 def solution(mesh):
@@ -342,7 +360,7 @@
     chunks = 2
 
     def layer(x_loc, ids_loc, gates_loc, dy_loc, wg_loc, wu_loc, wd_loc):
-        tokens, _ = x_loc.shape
+        tokens, hidden = x_loc.shape
         top_k = ids_loc.shape[1]
         per_group = wg_loc.shape[0] * inner
         group_limit = min(max(1, groups // 2), top_k // 2)
@@ -365,29 +383,27 @@
         everyone = list(range(per_group))
         ring = lambda a, d: lax.ppermute(a, 'ing', [(i, (i + d) % inner) for i in range(inner)])
         grads = None
+        total = None
+        c = chunks - 1
         rets = []
-        for c in range(chunks - 1):
-            pq, grads = run_experts(c, order, everyone, meta, recv[c], w_all, grads)
+        for i in range(c):
+            pq, grads = run_experts(i, order, everyone, meta, recv[i], w_all, grads)
             rets.append(swap(pq))
-        c = chunks - 1
-        ways = (1, -1, 1, -1)
-        rows, *far = run_experts(c, order, everyone[:1], meta, recv[c], w_all, grads, None, True, True)
-        for i, way in enumerate(ways):
-            far[i] = ring(far[i], way)
-        pq, *parts = run_experts(c, order, everyone[1:], meta, recv[c], w_all, grads, rows, False, True)
-        after, before, own = parts[:4], parts[4:8], parts[8:]
-        sums = [None] * 4
-        for late in (False, True):
-            for i, way in enumerate(ways):
-                up, down = after[i], before[i]
-                if late:
-                    up, down = (up + far[i], None) if way == 1 else (None, down + far[i])
-                else:
-                    up, down = (None, down) if way == 1 else (up, None)
-                sums[i] = (sums[i] or ()) + ((ring(up, 1),) if up is not None else (ring(down, -1),))
+        sums, *far = run_experts(c, order, everyone[:1], meta, recv[c], w_all, grads, None, True)
+        far0 = ring(far[0], 1)
+        far1 = ring(far[1], -1)
+        sums, next0, next1, last0, last1 = run_experts(c, order, everyone[1:-1], meta, recv[c], w_all, grads, sums, True)
+        soon1 = ring(next1, 1)
+        soon0 = ring(last0, -1)
+        pq, own0, own1 = run_experts(c, order, everyone[-1:], meta, recv[c], w_all, grads, sums, False)
         rets.append(swap(pq))
-        y_out, dx_out = home_sum(slot, rets, 256)
-        g1, g3, g2a, g2b = [a + (b[0] + b[1]) for a, b in zip(own, sums)]
-        return y_out, dx_out, g1[None], g3[None], jnp.concatenate([g2a, g2b], axis=0)[None]
+        late0 = ring(next0 + far0, 1)
+        late1 = ring(last1 + far1, -1)
+        for i in range(chunks):
+            total = home_sum(slot, rets[i], i, total, i == c, 256)
+            total = total[0] if i < c else total
+        y_out, dx_out = total
+        g1, g3, g2 = finish((own0, soon0, late0), (own1, soon1, late1), hidden)
+        return y_out, dx_out, g1, g3, g2
 
     return jax.shard_map(layer, mesh=mesh, in_specs=(tok_spec, tok_spec, tok_spec, tok_spec, weight_spec, weight_spec, weight_spec), out_specs=(tok_spec, tok_spec, grad_spec, grad_spec, grad_spec), check_vma=False)

time: 610 us -> 625 us (1.025)
  Pallas kernels: 265 us -> 285 us
  starting transfers between devices: 48 us -> 38.7 us
  waiting for transfers between devices: 268 us -> 277 us
    pallas_call x1 -> x3, Pallas kernels: 24.7 us -> 38.5 us  [the longest x2 28.6 us: home_sum(): pl.pallas_call(functools.partial(home_kernel, c * size), grid=(tokens //...]
    ppermute x12 -> x6, waiting for transfers between devices: 187 us -> 197 us  [layer(): lax.ppermute(a, 'ing', [(i, (i + d) % inner) for i in range(inner)])]
    ppermute x12 -> x6, starting transfers between devices: 20.3 us -> 11.4 us  [layer(): lax.ppermute(a, 'ing', [(i, (i + d) % inner) for i in range(inner)])]
    pallas_call x3 -> x4, Pallas kernels: 206 us -> 213 us  [run_experts(): pl.pallas_call(functools.partial(expert_kernel, chunk, first, steps, prev...]
  transfers between devices with their start and end apart: 18 -> 12, of which waited for: 5 -> 5; matrix products, arithmetic and copies ran while one was open for 1% -> 1% of each run, Pallas kernels for 39% -> 43%
where the time goes in v3:
time: 625 us
  Pallas kernels  285 us (46%)
  waiting for transfers between devices  277 us (44%)
  starting transfers between devices  38.7 us (6%)
  between operations  14.1 us (2%)
  other arithmetic  7.9 us (1%)
    pallas_call x4, Pallas kernels, run_experts(): pl.pallas_call(functools.partial(expert_kernel, chunk, first, steps, prev...  213 us
    ppermute x6, waiting for transfers between devices, layer(): lax.ppermute(a, 'ing', [(i, (i + d) % inner) for i in range(inner)])  197 us
    all_to_all x5, waiting for transfers between devices, layer(): swap = lambda a: lax.all_to_all(a, 'grp', 0, 0, tiled=True)  80.2 us
    pallas_call x2, Pallas kernels, home_sum(): pl.pallas_call(functools.partial(home_kernel, c * size), grid=(tokens //...  28.6 us
    pallas_call x2, Pallas kernels, pack_rows(): pl.pallas_call(functools.partial(pack_kernel, c * size), grid=(groups,),...  27.7 us
    all_to_all x5, starting transfers between devices, layer(): swap = lambda a: lax.all_to_all(a, 'grp', 0, 0, tiled=True)  27.2 us
  transfers between devices with their start and end apart: 12, of which 5 were waited for; matrix products, arithmetic and copies ran while one was open for 1% of the time, Pallas kernels for 43%

profile of v3, /device:TPU:97, one launch (start us, length us, event | category | flops | bytes accessed | tf_op | source)
XLA Modules:
  0.0 624.7 jit_solution(15207733058784985)
XLA Ops:
  7.2 0.1 all-gather.2.cloned.1.call-start
  7.2 3.8 pad_maximum_fusion
  11.2 6.1 make_tables.1
  17.3 6.0 all-to-all-start
  23.3 14.3 %pack_rows.2 = bf16[8,256,2048]{2,1,0:T(8,128)(2,1)} custom-call(f32[8,1024]{1,0:T(8,128)} %get-tuple-element.30.slot_ref, bf16[1024,1024]{1,0:T(8,128)(2,1)} %x_ref.3, bf16[1024,1024]{1,0:T(8,128)(2,1)} %dy_ref.3), custom_call_target="tpu_custom_call" | custom-call | flops 8589934592 | bytes 8388608 | tf_op jit(solution)/shard_map/pack_rows/pallas_call | solution.py:98
  37.5 0.7 copy-done.6
  38.2 5.0 all-to-all-start.2
  43.2 13.4 %pack_rows.3 = bf16[8,256,2048]{2,1,0:T(8,128)(2,1)} custom-call(f32[8,1024]{1,0:T(8,128)} %get-tuple-element.30.slot_ref, bf16[1024,1024]{1,0:T(8,128)(2,1)} %x_ref.3, bf16[1024,1024]{1,0:T(8,128)(2,1)} %dy_ref.3), custom_call_target="tpu_custom_call" | custom-call | flops 8589934592 | bytes 8388608 | tf_op jit(solution)/shard_map/pack_rows/pallas_call | solution.py:98
  56.7 80.2 %all-to-all-done.2.xd_ref = bf16[8,256,2048]{2,1,0:T(8,128)(2,1)} async-done(((bf16[8,256,2048]{2,1,0:T(8,128)(2,1)}), bf16[8,256,2048]{2,1,0:T(8,128)(2,1)}, u32[]{:S(2)}, u32[]{:S(2)}) %all-to-all-start.2) | async-done | bytes 8388640 | tf_op jit(solution)/shard_map/all_to_all | solution.py:368
  136.9 5.9 all-to-all-start.1
  142.7 0.5 and_select_fusion.order_ref
  143.2 96.3 %run_experts.4 = (bf16[8,256,2048]{2,1,0:T(8,128)(2,1)}, f32[4,1536,1024]{2,1,0:T(8,128)}) custom-call(s32[4]{0:T(128)} %and_select_fusion.order_ref, f32[8,8,512]{2,1,0:T(8,128)} %copy-done.6, bf16[8,256,2048]{2,1,0:T(8,128)(2,1)} %all-to-all-done.2.xd_ref, bf16[4,1536,1024]{2,1,0:T(8,128)(2,1)} %all-gather.2.cloned.1.call-done.w_ref), custom_call_target="tpu_custom_call" | custom-call | flops 47244640256 | bytes 16777216 | tf_op jit(solution)/shard_map/run_experts/pallas_call | solution.py:270
  239.6 5.1 all-to-all-start.4
  244.7 29.9 %run_experts.5 = (f32[8,256,2048]{2,1,0:T(8,128)}, f32[1536,512]{1,0:T(8,128)}, f32[1536,512]{1,0:T(8,128)}) custom-call(s32[4]{0:T(128)} %and_select_fusion.order_ref, f32[8,8,512]{2,1,0:T(8,128)} %copy-done.6, bf16[8,256,2048]{2,1,0:T(8,128)(2,1)} %all-to-all-done.1.xd_ref, bf16[4,1536,1024]{2,1,0:T(8,128)(2,1)} %all-gather.2.cloned.1.call-done.w_ref, ...), custom_call_target="tpu_custom_call" | custom-call | flops 11811160064 | bytes 16777216 | tf_op jit(solution)/shard_map/run_experts/pallas_call | solution.py:270
  274.7 57.6 %run_experts.6 = (f32[8,256,2048]{2,1,0:T(8,128)}, f32[1536,512]{1,0:T(8,128)}, f32[1536,512]{1,0:T(8,128)}, f32[1536,512]{1,0:T(8,128)}, f32[1536,512]{1,0:T(8,128)}) custom-call(s32[4]{0:T(128)} %and_select_fusion.order_ref, f32[8,8,512]{2,1,0:T(8,128)} %copy-done.6, bf16[8,256,2048]{2,1,0:T(8,128)(2,1)} %all-to-all-done.1.xd_ref, ...), custom_call_target="tpu_custom_call" | custom-call | flops 23622320128 | bytes 16777216 | tf_op jit(solution)/shard_map/run_experts/pallas_call | solution.py:270
  332.2 28.8 %run_experts.7 = (bf16[8,256,2048]{2,1,0:T(8,128)(2,1)}, f32[1536,512]{1,0:T(8,128)}, f32[1536,512]{1,0:T(8,128)}) custom-call(s32[4]{0:T(128)} %and_select_fusion.order_ref, f32[8,8,512]{2,1,0:T(8,128)} %copy-done.6, bf16[8,256,2048]{2,1,0:T(8,128)(2,1)} %all-to-all-done.1.xd_ref, bf16[4,1536,1024]{2,1,0:T(8,128)(2,1)} %all-gather.2.cloned.1.call-done.w_ref, ...), custom_call_target="tpu_custom_call" | custom-call | flops 11811160064 | bytes 16777216 | tf_op jit(solution)/shard_map/run_experts/pallas_call | solution.py:270
  361.0 5.2 all-to-all-start.3
  366.3 7.0 %collective-permute-start.1 = (f32[1536,512]{1,0:T(8,128)}, f32[1536,512]{1,0:T(8,128)S(1)}, u32[]{:S(2)}, u32[]{:S(2)}) collective-permute-start(f32[1536,512]{1,0:T(8,128)} %get-tuple-element.43), channel_id=1, source_target_pairs={{0,8},{8,16},{16,24},{24,0},{1,9},{9,17},{17,25},{25,1},{2,10},{10... | collective-permute-start | bytes 9437192 | tf_op jit(solution)/shard_map/ppermute | solution.py:384
  373.3 1.0 collective-permute-start
  374.2 0.5 collective-permute-start.3
  374.8 66.3 %collective-permute-done.1 = f32[1536,512]{1,0:T(8,128)S(1)} collective-permute-done((f32[1536,512]{1,0:T(8,128)}, f32[1536,512]{1,0:T(8,128)S(1)}, u32[]{:S(2)}, u32[]{:S(2)}) %collective-permute-start.1) | collective-permute-done | bytes 3145760 | tf_op jit(solution)/shard_map/ppermute | solution.py:384
  441.1 2.8 add.21
  443.9 2.3 collective-permute-start.2
  446.1 0.7 add.22
  446.9 0.6 collective-permute-start.5
  447.5 62.8 %collective-permute-done.refs_1_ = f32[1536,512]{1,0:T(8,128)S(1)} collective-permute-done((f32[1536,512]{1,0:T(8,128)}, f32[1536,512]{1,0:T(8,128)S(1)}, u32[]{:S(2)}, u32[]{:S(2)}) %collective-permute-start) | collective-permute-done | bytes 3145760 | tf_op jit(solution)/shard_map/ppermute | solution.py:384
  510.3 65.5 %collective-permute-done.2.refs_2_ = f32[1536,512]{1,0:T(8,128)S(1)} collective-permute-done((f32[1536,512]{1,0:T(8,128)S(1)}, f32[1536,512]{1,0:T(8,128)S(1)}, u32[]{:S(2)}, u32[]{:S(2)}) %collective-permute-start.2) | collective-permute-done | bytes 3145760 | tf_op jit(solution)/shard_map/ppermute | solution.py:384
  575.8 1.9 collective-permute-done.5.refs_5_
  577.7 1.7 copy-done.4
  579.4 9.9 %finish.1 = (f32[1,1024,512]{2,1,0:T(8,128)}, f32[1,1024,512]{2,1,0:T(8,128)}, f32[1,512,1024]{2,1,0:T(8,128)}) custom-call(f32[1536,512]{1,0:T(8,128)} %get-tuple-element.40.refs_0_, f32[1536,512]{1,0:T(8,128)} %copy-done.1, f32[1536,512]{1,0:T(8,128)} %copy-done.3, f32[1536,512]{1,0:T(8,128)} %get-tuple-element.44.refs_3_, f32[1536,512]{1,0:T(8,128)} %copy-done.2, ...), custom_call_target="tpu_custom_call" | custom-call | flops 3145728 | bytes 25165824 | tf_op jit(solution)/shard_map/finish/pallas_call | solution.py:342
  589.3 14.2 %home_sum.2.refs_0_ = f32[1024,2048]{1,0:T(8,128)} custom-call(f32[8,1024]{1,0:T(8,128)S(1)} %copy-done, bf16[8,256,2048]{2,1,0:T(8,128)(2,1)} %all-to-all-done.4.ret_ref), custom_call_target="tpu_custom_call" | custom-call | flops 8589934592 | bytes 8388608 | tf_op jit(solution)/shard_map/home_sum/pallas_call | solution.py:307
  603.5 14.4 %home_sum.3 = (bf16[1024,1024]{1,0:T(8,128)(2,1)}, bf16[1024,1024]{1,0:T(8,128)(2,1)}) custom-call(f32[8,1024]{1,0:T(8,128)S(1)} %copy-done, bf16[8,256,2048]{2,1,0:T(8,128)(2,1)} %all-to-all-done.3.ret_ref, f32[1024,2048]{1,0:T(8,128)} %home_sum.2.refs_0_), custom_call_target="tpu_custom_call" | custom-call | flops 8589934592 | bytes 8388608 | tf_op jit(solution)/shard_map/home_sum/pallas_call | solution.py:307
  (23 shorter events, 0.1 us)
Async XLA Ops:
  7.2 136.1 %all-gather.2.cloned.1.call-start = ((), (), s32[]{:S(2)}) async-start(), calls=%async_computation.5 | async-start | bytes 15728640 | tf_op jit(solution)/shard_map/all_gather | solution.py:370
  17.3 20.3 %all-to-all-start = ((f32[8,8,512]{2,1,0:T(8,128)}), f32[8,8,512]{2,1,0:T(8,128)S(1)}, u32[]{:S(2)}, u32[]{:S(2)}) async-start(f32[8,8,512]{2,1,0:T(8,128)} %get-tuple-element.29), calls=%async_computation | async-start | bytes 262144 | tf_op jit(solution)/shard_map/all_to_all | solution.py:368
  37.5 0.7 copy-start.6
  38.2 98.7 %all-to-all-start.2 = ((bf16[8,256,2048]{2,1,0:T(8,128)(2,1)}), bf16[8,256,2048]{2,1,0:T(8,128)(2,1)}, u32[]{:S(2)}, u32[]{:S(2)}) async-start(bf16[8,256,2048]{2,1,0:T(8,128)(2,1)} %pack_rows.2), calls=%async_computation.2 | async-start | bytes 16777216 | tf_op jit(solution)/shard_map/all_to_all | solution.py:368
  56.7 86.0 %copy-start.7 = (s32[4]{0:T(128)S(1)}, s32[4]{0:T(128)}, u32[]{:S(2)}) copy-start(s32[4]{0:T(128)} %constant.22.clone) | copy-start | bytes 52
  136.9 102.7 %all-to-all-start.1 = ((bf16[8,256,2048]{2,1,0:T(8,128)(2,1)}), bf16[8,256,2048]{2,1,0:T(8,128)(2,1)}, u32[]{:S(2)}, u32[]{:S(2)}) async-start(bf16[8,256,2048]{2,1,0:T(8,128)(2,1)} %pack_rows.3), calls=%async_computation.1 | async-start | bytes 16777216 | tf_op jit(solution)/shard_map/all_to_all | solution.py:368
  239.6 121.5 %all-to-all-start.4 = ((bf16[8,256,2048]{2,1,0:T(8,128)(2,1)}), bf16[8,256,2048]{2,1,0:T(8,128)(2,1)}, u32[]{:S(2)}, u32[]{:S(2)}) async-start(bf16[8,256,2048]{2,1,0:T(8,128)(2,1)} %get-tuple-element.37), calls=%async_computation.4 | async-start | bytes 16777216 | tf_op jit(solution)/shard_map/all_to_all | solution.py:368
  361.0 242.5 %all-to-all-start.3 = ((bf16[8,256,2048]{2,1,0:T(8,128)(2,1)}), bf16[8,256,2048]{2,1,0:T(8,128)(2,1)}, u32[]{:S(2)}, u32[]{:S(2)}) async-start(bf16[8,256,2048]{2,1,0:T(8,128)(2,1)} %get-tuple-element.36), calls=%async_computation.3 | async-start | bytes 16777216 | tf_op jit(solution)/shard_map/all_to_all | solution.py:368
  366.3 74.8 %collective-permute-start.1 = (f32[1536,512]{1,0:T(8,128)}, f32[1536,512]{1,0:T(8,128)S(1)}, u32[]{:S(2)}, u32[]{:S(2)}) collective-permute-start(f32[1536,512]{1,0:T(8,128)} %get-tuple-element.43), channel_id=1, source_target_pairs={{0,8},{8,16},{16,24},{24,0},{1,9},{9,17},{17,25},{25,1},{2,10},{10... | collective-permute-start | bytes 9437192 | tf_op jit(solution)/shard_map/ppermute | solution.py:384
  373.3 72.9 %collective-permute-start.4 = (f32[1536,512]{1,0:T(8,128)}, f32[1536,512]{1,0:T(8,128)S(1)}, u32[]{:S(2)}, u32[]{:S(2)}) collective-permute-start(f32[1536,512]{1,0:T(8,128)} %get-tuple-element.47), channel_id=1, source_target_pairs={{0,24},{8,0},{16,8},{24,16},{1,25},{9,1},{17,9},{25,17},{2,26},{10... | collective-permute-start | bytes 9437192 | tf_op jit(solution)/shard_map/ppermute | solution.py:384
  373.3 137.0 %collective-permute-start = (f32[1536,512]{1,0:T(8,128)}, f32[1536,512]{1,0:T(8,128)S(1)}, u32[]{:S(2)}, u32[]{:S(2)}) collective-permute-start(f32[1536,512]{1,0:T(8,128)} %get-tuple-element.41), channel_id=1, source_target_pairs={{0,24},{8,0},{16,8},{24,16},{1,25},{9,1},{17,9},{25,17},{2,26},{10... | collective-permute-start | bytes 9437192 | tf_op jit(solution)/shard_map/ppermute | solution.py:384
  374.2 136.0 %collective-permute-start.3 = (f32[1536,512]{1,0:T(8,128)}, f32[1536,512]{1,0:T(8,128)S(1)}, u32[]{:S(2)}, u32[]{:S(2)}) collective-permute-start(f32[1536,512]{1,0:T(8,128)} %get-tuple-element.45), channel_id=1, source_target_pairs={{0,8},{8,16},{16,24},{24,0},{1,9},{9,17},{17,25},{25,1},{2,10},{10... | collective-permute-start | bytes 9437192 | tf_op jit(solution)/shard_map/ppermute | solution.py:384
  441.1 5.1 copy-start.5
  443.9 131.9 %collective-permute-start.2 = (f32[1536,512]{1,0:T(8,128)S(1)}, f32[1536,512]{1,0:T(8,128)S(1)}, u32[]{:S(2)}, u32[]{:S(2)}) collective-permute-start(f32[1536,512]{1,0:T(8,128)S(1)} %add.21), channel_id=1, source_target_pairs={{0,8},{8,16},{16,24},{24,0},{1,9},{9,17},{17,25},{25,1},{2,10},{10... | collective-permute-start | bytes 9437192 | tf_op jit(solution)/shard_map/ppermute | solution.py:384
  446.9 130.8 %collective-permute-start.5 = (f32[1536,512]{1,0:T(8,128)S(1)}, f32[1536,512]{1,0:T(8,128)S(1)}, u32[]{:S(2)}, u32[]{:S(2)}) collective-permute-start(f32[1536,512]{1,0:T(8,128)S(1)} %add.22), channel_id=1, source_target_pairs={{0,24},{8,0},{16,8},{24,16},{1,25},{9,1},{17,9},{25,17},{2,26},{10... | collective-permute-start | bytes 9437192 | tf_op jit(solution)/shard_map/ppermute | solution.py:384
  510.3 69.1 %copy-start.1 = (f32[1536,512]{1,0:T(8,128)}, f32[1536,512]{1,0:T(8,128)S(1)}, u32[]{:S(2)}) copy-start(f32[1536,512]{1,0:T(8,128)S(1)} %collective-permute-done.refs_1_) | copy-start | bytes 9437188
  510.3 67.4 %copy-start.2 = (f32[1536,512]{1,0:T(8,128)}, f32[1536,512]{1,0:T(8,128)S(1)}, u32[]{:S(2)}) copy-start(f32[1536,512]{1,0:T(8,128)S(1)} %collective-permute-done.3.refs_4_) | copy-start | bytes 9437188
  575.8 1.9 copy-start.3
  577.7 1.7 copy-start.4
  579.4 9.9 %copy-start = (f32[8,1024]{1,0:T(8,128)S(1)}, f32[8,1024]{1,0:T(8,128)}, u32[]{:S(2)}) copy-start(f32[8,1024]{1,0:T(8,128)} %get-tuple-element.30.slot_ref) | copy-start | bytes 98308
Sparse Core Ops, SparseCore 0:
  11.3 119.7 all-gather.1

commit v4 on v3

--- a/solution.py
+++ b/solution.py
@@ -53,8 +53,18 @@
     return (slot_row == want).astype(F32).astype(BF16)
 
 
-def table_kernel(groups, per_group, size, ids_ref, gates_ref, slot_ref, meta_ref, vals):
+def table_kernel(groups, per_group, size, ids_ref, gates_ref, *refs):
+    weights, (slot_ref, meta_ref, joined_ref, vals, joined, sems) = refs[:3], refs[3:]
+    hidden, ff = weights[0].shape[1:]
+    places = ((pl.ds(0, hidden), pl.ds(0, ff)), (pl.ds(0, hidden), pl.ds(ff, ff)), (pl.ds(hidden, ff), pl.ds(0, hidden)))
+    loads = [pltpu.make_async_copy(weights[i].at[0], joined.at[r, c], sems.at[i]) for i, (r, c) in enumerate(places)]
+    store = pltpu.make_async_copy(joined, joined_ref.at[0], sems.at[3])
+    for copy in loads:
+        copy.start()
     table_rows(groups, per_group, ids_ref, gates_ref, slot_ref, vals)
+    for copy in loads:
+        copy.wait()
+    store.start()
     n = 2 * per_group
     is_rank = lax.broadcasted_iota(jnp.int32, (n, 1), 0) < per_group
 
@@ -69,19 +79,34 @@
             meta_ref[h, :, c * size:(c + 1) * size] = jnp.where(is_rank & (full > 0), full - base, full)
             base = jnp.where(is_rank, jnp.maximum(base, jnp.max(full, axis=1, keepdims=True)), 0.0)
 
-
-def make_tables(ids_t, gates_t, groups, per_group, cap, size):
+    store.wait()
+
+
+def make_tables(ids_t, gates_t, weights, groups, per_group, cap, size):
     tokens = ids_t.shape[1]
     vmem = pl.BlockSpec(memory_space=pltpu.VMEM)
+    any_spec = pl.BlockSpec(memory_space=pl.ANY)
+    _, hidden, ff = weights[0].shape
+    assert hidden == 2 * ff and weights[2].shape == (1, ff, hidden)
+    joined = (hidden + ff, hidden)
     return pl.pallas_call(
         functools.partial(table_kernel, groups, per_group, size),
-        out_shape=(jax.ShapeDtypeStruct((groups, tokens), F32), jax.ShapeDtypeStruct((groups, 2 * per_group, cap), F32)),
-        in_specs=[vmem, vmem],
-        out_specs=(vmem, vmem),
-        scratch_shapes=[pltpu.VMEM((groups, 2 * per_group, tokens), F32)],
+        out_shape=(
+            jax.ShapeDtypeStruct((groups, tokens), F32),
+            jax.ShapeDtypeStruct((groups, 2 * per_group, cap), F32),
+            jax.ShapeDtypeStruct((1,) + joined, BF16),
+        ),
+        in_specs=[vmem, vmem] + [any_spec] * 3,
+        out_specs=(vmem, vmem, any_spec),
+        scratch_shapes=[
+            pltpu.VMEM((groups, 2 * per_group, tokens), F32),
+            pltpu.VMEM(joined, BF16),
+            pltpu.SemaphoreType.DMA((4,)),
+        ],
+        compiler_params=pltpu.CompilerParams(vmem_limit_bytes=58 * 1024 * 1024),
         cost_estimate=pl.CostEstimate(flops=2 * groups * cap * tokens * 128, bytes_accessed=groups * cap * 64, transcendentals=0),
         name='make_tables',
-    )(ids_t, gates_t)
+    )(ids_t, gates_t, *weights)
 
 
 def pack_kernel(first, slot_ref, x_ref, dy_ref, packed_ref):
@@ -114,8 +139,8 @@
     rows_ref = refs.pop(0)
     split = sums_in or sums_out
     grad_refs = [refs.pop(0) for _ in range(2 * steps if split else 1)]
-    buf, acc, pq, offs, in_sem, out_sem, sum_sem = refs[:7]
-    stage, pq_sem = (None, None) if sums_out else refs[7:]
+    buf, acc, pq, xd, w, offs, in_sem, out_sem, sum_sem, xd_sem, w_sem = refs[:11]
+    stage, pq_sem = (None, None) if sums_out else refs[11:]
     step = pl.program_id(0)
     k = order_ref[first_pos + step]
     srcs, size, width = xd_ref.shape
@@ -138,6 +163,26 @@
     def load_prev():
         return pltpu.make_async_copy(prev.at[first_pos + step], acc, in_sem)
 
+    def load_rows(s):
+        return pltpu.make_async_copy(xd_ref.at[s], xd.at[s], xd_sem.at[s])
+
+    def load_weights(at):
+        slot = at % 2
+        return pltpu.make_async_copy(w_ref.at[order_ref[first_pos + at]], w.at[slot], w_sem.at[slot])
+
+    @pl.when(step == 0)
+    def _():
+        @pl.loop(0, srcs)
+        def _(s):
+            load_rows(s).start()
+
+        load_weights(0).start()
+
+    if steps > 1:
+        @pl.when(step < steps - 1)
+        def _():
+            load_weights(step + 1).start()
+
     @pl.when(step > 0)
     def _():
         each_grad(step - 1, lambda copy: copy.wait())
@@ -157,13 +202,17 @@
         return meta_ref[s, pl.ds(k, 1), lanes] == slot
 
     def gather(s, off):
+        @pl.when(step == 0)
+        def _():
+            load_rows(s).wait()
+
         off = pl.multiple_of(off, ALIGN)
         offs[s] = off
         hit = pick(s)
         sel = hit.astype(F32).astype(BF16)
         gate = jnp.sum(jnp.where(hit, meta_ref[s, pl.ds(per_group + k, 1), lanes], 0.0), axis=1, keepdims=True)
-        buf[pl.ds(off, size), 0:hidden] = dot(sel, xd_ref[s, :, 0:hidden], 1, 0).astype(BF16)
-        buf[pl.ds(off, size), hidden:] = (gate * dot(sel, xd_ref[s, :, hidden:], 1, 0)).astype(BF16)
+        buf[pl.ds(off, size), 0:hidden] = dot(sel, xd[s, :, 0:hidden], 1, 0).astype(BF16)
+        buf[pl.ds(off, size), hidden:] = (gate * dot(sel, xd[s, :, hidden:], 1, 0)).astype(BF16)
         count = jnp.max(meta_ref[s, pl.ds(k, 1), lanes]).astype(jnp.int32)
         return off + (count + ALIGN - 1) // ALIGN * ALIGN
 
@@ -171,14 +220,16 @@
     buf[pl.ds(total, TILE), :] = jnp.zeros((TILE, width), BF16)
     if has_prev:
         load_prev().wait()
+    load_weights(step).wait()
+    ws = step % 2
 
     @pl.loop(0, (total + TILE - 1) // TILE)
     def _(i):
         tile = pl.ds(pl.multiple_of(i * TILE, TILE), TILE)
         x = buf[tile, 0:hidden]
         d = buf[tile, hidden:]
-        h = dot(x, w_ref[0, 0:hidden, :], 1, 0)
-        da = dot(d, w_ref[0, hidden:, :], 1, 1)
+        h = dot(x, w[ws, 0:hidden, :], 1, 0)
+        da = dot(d, w[ws, hidden:, :], 1, 1)
         h1 = h[:, 0:ff]
         h3 = h[:, ff:]
         sig = jax.nn.sigmoid(h1)
@@ -189,8 +240,8 @@
         dh = jnp.concatenate([dh1, dh3], axis=1)
         acc[0:hidden, :] += dot(x, dh, 0, 0)
         acc[hidden:, :] += dot(a, d, 0, 0)
-        buf[tile, 0:hidden] = dot(a, w_ref[0, hidden:, :], 1, 0).astype(BF16)
-        buf[tile, hidden:] = dot(dh, w_ref[0, 0:hidden, :], 1, 1).astype(BF16)
+        buf[tile, 0:hidden] = dot(a, w[ws, hidden:, :], 1, 0).astype(BF16)
+        buf[tile, hidden:] = dot(dh, w[ws, 0:hidden, :], 1, 1).astype(BF16)
 
     each_grad(step, lambda copy: copy.start())
     if sums_in:
@@ -198,7 +249,7 @@
         def _():
             pltpu.make_async_copy(before, pq, sum_sem).wait()
 
-    def combine(first):
+    def combine(first, last):
         @pl.loop(0, srcs)
         def _(s):
             off = pl.multiple_of(offs[s], ALIGN)
@@ -208,37 +259,49 @@
             gate = jnp.sum(jnp.where(lane == per_group + k, cols, 0.0), axis=1, keepdims=True)
             p = gate * dot(sel, buf[pl.ds(off, size), 0:hidden], 0, 0)
             q = dot(sel, buf[pl.ds(off, size), hidden:], 0, 0)
-            if first:
-                pq[s, :, 0:hidden] = p
-                pq[s, :, hidden:] = q
-            else:
-                pq[s, :, 0:hidden] += p
-                pq[s, :, hidden:] += q
-
-    if sums_in or steps == 1:
-        combine(not sums_in)
+            if not first:
+                p = pq[s, :, 0:hidden] + p
+                q = pq[s, :, hidden:] + q
+            if last and not sums_out:
+                slot = s % 2
+
+                @pl.when(s >= 2)
+                def _():
+                    pltpu.make_async_copy(stage.at[slot], rows_ref.at[s - 2], pq_sem.at[slot]).wait()
+
+                stage[slot, :, 0:hidden] = p.astype(BF16)
+                stage[slot, :, hidden:] = q.astype(BF16)
+                pltpu.make_async_copy(stage.at[slot], rows_ref.at[s], pq_sem.at[slot]).start()
+                return
+            pq[s, :, 0:hidden] = p
+            pq[s, :, hidden:] = q
+            if last:
+                pltpu.make_async_copy(pq.at[s], rows_ref.at[s], pq_out.at[s]).start()
+
+    pq_out = xd_sem
+    if steps == 1:
+        combine(not sums_in, True)
     else:
-        @pl.when(step == 0)
+        if not sums_in:
+            @pl.when(step == 0)
+            def _():
+                combine(True, False)
+
+        if sums_in or steps > 2:
+            @pl.when((step < steps - 1) if sums_in else ((step > 0) & (step < steps - 1)))
+            def _():
+                combine(False, False)
+
+        @pl.when(step == steps - 1)
         def _():
-            combine(True)
-
-        @pl.when(step > 0)
-        def _():
-            combine(False)
+            combine(False, True)
 
     @pl.when(step == steps - 1)
     def _():
         if sums_out:
-            copy = pltpu.make_async_copy(pq, rows_ref, sum_sem)
-            copy.start()
-            copy.wait()
+            for s in range(srcs):
+                pltpu.make_async_copy(pq.at[s], rows_ref.at[s], pq_out.at[s]).wait()
         else:
-            for s in range(srcs):
-                slot = s % 2
-                if s >= 2:
-                    pltpu.make_async_copy(stage.at[slot], rows_ref.at[s - 2], pq_sem.at[slot]).wait()
-                stage[slot] = pq[s].astype(BF16)
-                pltpu.make_async_copy(stage.at[slot], rows_ref.at[s], pq_sem.at[slot]).start()
             for s in range(max(0, srcs - 2), srcs):
                 pltpu.make_async_copy(stage.at[s % 2], rows_ref.at[s], pq_sem.at[s % 2]).wait()
         each_grad(step, lambda copy: copy.wait())
@@ -260,10 +323,14 @@
         pltpu.VMEM((srcs * size + max(size, TILE), width), BF16),
         pltpu.VMEM((rows, hidden), F32),
         pltpu.VMEM((srcs, size, width), F32),
+        pltpu.VMEM((srcs, size, width), BF16),
+        pltpu.VMEM((2, rows, hidden), BF16),
         pltpu.SMEM((srcs,), jnp.int32),
         pltpu.SemaphoreType.DMA,
         pltpu.SemaphoreType.DMA((2,)),
         pltpu.SemaphoreType.DMA,
+        pltpu.SemaphoreType.DMA((srcs,)),
+        pltpu.SemaphoreType.DMA((2,)),
     ]
     if not more:
         scratch += [pltpu.VMEM((2, size, width), BF16), pltpu.SemaphoreType.DMA((2,))]
@@ -272,7 +339,7 @@
         grid_spec=pltpu.PrefetchScalarGridSpec(
             num_scalar_prefetch=1,
             grid=(steps,),
-            in_specs=[vmem, vmem, pl.BlockSpec((1, rows, hidden), lambda k, o: (o[first + k], 0, 0))] + [any_spec] * len(extra),
+            in_specs=[vmem, any_spec, any_spec] + [any_spec] * len(extra),
             out_specs=[any_spec] * (1 + len(grads)),
             scratch_shapes=scratch,
         ),
@@ -366,10 +433,9 @@
         group_limit = min(max(1, groups // 2), top_k // 2)
         cap = tokens * group_limit // groups
         swap = lambda a: lax.all_to_all(a, 'grp', 0, 0, tiled=True)
-        w_own = jnp.concatenate([jnp.concatenate([wg_loc, wu_loc], axis=2), wd_loc], axis=1)
+        size = cap // chunks
+        slot, meta, w_own = make_tables(ids_loc.T, gates_loc.T, (wg_loc, wu_loc, wd_loc), groups, per_group, cap, size)
         w_all = lax.all_gather(w_own, 'ing', axis=0, tiled=True)
-        size = cap // chunks
-        slot, meta = make_tables(ids_loc.T, gates_loc.T, groups, per_group, cap, size)
         meta = swap(meta)
         recv = []
         for c in range(chunks):

time: 625 us -> 615 us (0.984)
    pallas_call x4, Pallas kernels: 213 us -> 206 us  [run_experts(): pl.pallas_call(functools.partial(expert_kernel, chunk, first, steps, prev...]
  transfers between devices with their start and end apart: 12 -> 12, of which waited for: 5 -> 6; matrix products, arithmetic and copies ran while one was open for 1% -> 1% of each run, Pallas kernels for 43% -> 42%
where the time goes in v4:
time: 615 us
  Pallas kernels  279 us (45%)
  waiting for transfers between devices  278 us (45%)
  starting transfers between devices  37.3 us (6%)
  between operations  14.1 us (2%)
    pallas_call x4, Pallas kernels, run_experts(): pl.pallas_call(functools.partial(expert_kernel, chunk, first, steps, prev...  206 us
    ppermute x6, waiting for transfers between devices, layer(): lax.ppermute(a, 'ing', [(i, (i + d) % inner) for i in range(inner)])  197 us
    all_to_all x5, waiting for transfers between devices, layer(): swap = lambda a: lax.all_to_all(a, 'grp', 0, 0, tiled=True)  81.3 us
    pallas_call x2, Pallas kernels, home_sum(): pl.pallas_call(functools.partial(home_kernel, c * size), grid=(tokens //...  28.6 us
    all_to_all x5, starting transfers between devices, layer(): swap = lambda a: lax.all_to_all(a, 'grp', 0, 0, tiled=True)  27.8 us
    pallas_call x2, Pallas kernels, pack_rows(): pl.pallas_call(functools.partial(pack_kernel, c * size), grid=(groups,),...  26.9 us
  transfers between devices with their start and end apart: 12, of which 6 were waited for; matrix products, arithmetic and copies ran while one was open for 1% of the time, Pallas kernels for 42%

profile of v4, /device:TPU:97, one launch (start us, length us, event | category | flops | bytes accessed | tf_op | source)
XLA Modules:
  0.0 614.6 jit_solution(5602366062797571122)
XLA Ops:
  7.2 0.1 all-gather.2.cloned.1.call-start
  7.2 7.4 %make_tables.1 = (f32[8,1024]{1,0:T(8,128)}, f32[8,8,512]{2,1,0:T(8,128)}, bf16[1,1536,1024]{2,1,0:T(8,128)(2,1)}) custom-call(s32[8,1024]{1,0:T(8,128)} %bitcast.2, f32[8,1024]{1,0:T(8,128)} %bitcast.3, bf16[1,1024,512]{2,1,0:T(8,128)(2,1)} %refs_0_.1, bf16[1,1024,512]{2,1,0:T(8,128)(2,1)} %refs_1_.1, bf16[1,512,1024]{2,1,0:T(8,128)(2,1)} %refs_2_.1), custom_call_target="tpu_custom_call" | custom-call | flops 1073741824 | bytes 262144 | tf_op jit(solution)/shard_map/make_tables/pallas_call | solution.py:92
  14.7 6.0 all-to-all-start
  20.7 13.5 %pack_rows.2 = bf16[8,256,2048]{2,1,0:T(8,128)(2,1)} custom-call(f32[8,1024]{1,0:T(8,128)} %get-tuple-element.31.slot_ref, bf16[1024,1024]{1,0:T(8,128)(2,1)} %x_ref.3, bf16[1024,1024]{1,0:T(8,128)(2,1)} %dy_ref.3), custom_call_target="tpu_custom_call" | custom-call | flops 8589934592 | bytes 8388608 | tf_op jit(solution)/shard_map/pack_rows/pallas_call | solution.py:123
  34.2 0.7 copy-done.6
  34.9 5.0 all-to-all-start.2
  39.9 13.4 %pack_rows.3 = bf16[8,256,2048]{2,1,0:T(8,128)(2,1)} custom-call(f32[8,1024]{1,0:T(8,128)} %get-tuple-element.31.slot_ref, bf16[1024,1024]{1,0:T(8,128)(2,1)} %x_ref.3, bf16[1024,1024]{1,0:T(8,128)(2,1)} %dy_ref.3), custom_call_target="tpu_custom_call" | custom-call | flops 8589934592 | bytes 8388608 | tf_op jit(solution)/shard_map/pack_rows/pallas_call | solution.py:123
  53.3 80.2 %all-to-all-done.2.xd_ref = bf16[8,256,2048]{2,1,0:T(8,128)(2,1)} async-done(((bf16[8,256,2048]{2,1,0:T(8,128)(2,1)}), bf16[8,256,2048]{2,1,0:T(8,128)(2,1)}, u32[]{:S(2)}, u32[]{:S(2)}) %all-to-all-start.2) | async-done | bytes 8388640 | tf_op jit(solution)/shard_map/all_to_all | solution.py:435
  133.6 5.8 all-to-all-start.1
  139.4 0.5 and_select_fusion.order_ref
  139.9 92.2 %run_experts.4 = (bf16[8,256,2048]{2,1,0:T(8,128)(2,1)}, f32[4,1536,1024]{2,1,0:T(8,128)}) custom-call(s32[4]{0:T(128)} %and_select_fusion.order_ref, f32[8,8,512]{2,1,0:T(8,128)} %copy-done.6, bf16[8,256,2048]{2,1,0:T(8,128)(2,1)} %all-to-all-done.2.xd_ref, bf16[4,1536,1024]{2,1,0:T(8,128)(2,1)} %all-gather.2.cloned.1.call-done.w_ref), custom_call_target="tpu_custom_call" | custom-call | flops 47244640256 | bytes 16777216 | tf_op jit(solution)/shard_map/run_experts/pallas_call | solution.py:337
  232.2 1.0 all-to-all-done.1.xd_ref
  233.2 5.8 all-to-all-start.4
  239.0 26.9 %run_experts.5 = (f32[8,256,2048]{2,1,0:T(8,128)}, f32[1536,512]{1,0:T(8,128)}, f32[1536,512]{1,0:T(8,128)}) custom-call(s32[4]{0:T(128)} %and_select_fusion.order_ref, f32[8,8,512]{2,1,0:T(8,128)} %copy-done.6, bf16[8,256,2048]{2,1,0:T(8,128)(2,1)} %all-to-all-done.1.xd_ref, bf16[4,1536,1024]{2,1,0:T(8,128)(2,1)} %all-gather.2.cloned.1.call-done.w_ref, ...), custom_call_target="tpu_custom_call" | custom-call | flops 11811160064 | bytes 16777216 | tf_op jit(solution)/shard_map/run_experts/pallas_call | solution.py:337
  266.0 55.8 %run_experts.6 = (f32[8,256,2048]{2,1,0:T(8,128)}, f32[1536,512]{1,0:T(8,128)}, f32[1536,512]{1,0:T(8,128)}, f32[1536,512]{1,0:T(8,128)}, f32[1536,512]{1,0:T(8,128)}) custom-call(s32[4]{0:T(128)} %and_select_fusion.order_ref, f32[8,8,512]{2,1,0:T(8,128)} %copy-done.6, bf16[8,256,2048]{2,1,0:T(8,128)(2,1)} %all-to-all-done.1.xd_ref, ...), custom_call_target="tpu_custom_call" | custom-call | flops 23622320128 | bytes 16777216 | tf_op jit(solution)/shard_map/run_experts/pallas_call | solution.py:337
  321.8 31.1 %run_experts.7 = (bf16[8,256,2048]{2,1,0:T(8,128)(2,1)}, f32[1536,512]{1,0:T(8,128)}, f32[1536,512]{1,0:T(8,128)}) custom-call(s32[4]{0:T(128)} %and_select_fusion.order_ref, f32[8,8,512]{2,1,0:T(8,128)} %copy-done.6, bf16[8,256,2048]{2,1,0:T(8,128)(2,1)} %all-to-all-done.1.xd_ref, bf16[4,1536,1024]{2,1,0:T(8,128)(2,1)} %all-gather.2.cloned.1.call-done.w_ref, ...), custom_call_target="tpu_custom_call" | custom-call | flops 11811160064 | bytes 16777216 | tf_op jit(solution)/shard_map/run_experts/pallas_call | solution.py:337
  352.9 5.2 all-to-all-start.3
  358.1 5.1 collective-permute-start.1
  363.2 1.3 collective-permute-start
  364.5 0.2 collective-permute-start.3
  364.7 66.3 %collective-permute-done.1 = f32[1536,512]{1,0:T(8,128)S(1)} collective-permute-done((f32[1536,512]{1,0:T(8,128)}, f32[1536,512]{1,0:T(8,128)S(1)}, u32[]{:S(2)}, u32[]{:S(2)}) %collective-permute-start.1) | collective-permute-done | bytes 3145760 | tf_op jit(solution)/shard_map/ppermute | solution.py:450
  431.0 2.8 add.21
  433.8 2.3 collective-permute-start.2
  436.0 0.7 add.22
  436.8 0.6 collective-permute-start.5
  437.4 62.8 %collective-permute-done.refs_1_ = f32[1536,512]{1,0:T(8,128)S(1)} collective-permute-done((f32[1536,512]{1,0:T(8,128)}, f32[1536,512]{1,0:T(8,128)S(1)}, u32[]{:S(2)}, u32[]{:S(2)}) %collective-permute-start) | collective-permute-done | bytes 3145760 | tf_op jit(solution)/shard_map/ppermute | solution.py:450
  500.2 65.5 %collective-permute-done.2.refs_2_ = f32[1536,512]{1,0:T(8,128)S(1)} collective-permute-done((f32[1536,512]{1,0:T(8,128)S(1)}, f32[1536,512]{1,0:T(8,128)S(1)}, u32[]{:S(2)}, u32[]{:S(2)}) %collective-permute-start.2) | collective-permute-done | bytes 3145760 | tf_op jit(solution)/shard_map/ppermute | solution.py:450
  565.7 1.9 collective-permute-done.5.refs_5_
  567.6 1.7 copy-done.4
  569.3 9.9 %finish.1 = (f32[1,1024,512]{2,1,0:T(8,128)}, f32[1,1024,512]{2,1,0:T(8,128)}, f32[1,512,1024]{2,1,0:T(8,128)}) custom-call(f32[1536,512]{1,0:T(8,128)} %get-tuple-element.42.refs_0_, f32[1536,512]{1,0:T(8,128)} %copy-done.1, f32[1536,512]{1,0:T(8,128)} %copy-done.3, f32[1536,512]{1,0:T(8,128)} %get-tuple-element.46.refs_3_, f32[1536,512]{1,0:T(8,128)} %copy-done.2, ...), custom_call_target="tpu_custom_call" | custom-call | flops 3145728 | bytes 25165824 | tf_op jit(solution)/shard_map/finish/pallas_call | solution.py:409
  579.2 14.2 %home_sum.2.refs_0_ = f32[1024,2048]{1,0:T(8,128)} custom-call(f32[8,1024]{1,0:T(8,128)S(1)} %copy-done, bf16[8,256,2048]{2,1,0:T(8,128)(2,1)} %all-to-all-done.4.ret_ref), custom_call_target="tpu_custom_call" | custom-call | flops 8589934592 | bytes 8388608 | tf_op jit(solution)/shard_map/home_sum/pallas_call | solution.py:374
  593.4 14.4 %home_sum.3 = (bf16[1024,1024]{1,0:T(8,128)(2,1)}, bf16[1024,1024]{1,0:T(8,128)(2,1)}) custom-call(f32[8,1024]{1,0:T(8,128)S(1)} %copy-done, bf16[8,256,2048]{2,1,0:T(8,128)(2,1)} %all-to-all-done.3.ret_ref, f32[1024,2048]{1,0:T(8,128)} %home_sum.2.refs_0_), custom_call_target="tpu_custom_call" | custom-call | flops 8589934592 | bytes 8388608 | tf_op jit(solution)/shard_map/home_sum/pallas_call | solution.py:374
  (22 shorter events, 0.1 us)
Async XLA Ops:
  7.2 132.7 %all-gather.2.cloned.1.call-start = ((), (), s32[]{:S(2)}) async-start(), calls=%async_computation.5 | async-start | bytes 15728640 | tf_op jit(solution)/shard_map/all_gather | solution.py:438
  14.7 19.5 %all-to-all-start = ((f32[8,8,512]{2,1,0:T(8,128)}), f32[8,8,512]{2,1,0:T(8,128)S(1)}, u32[]{:S(2)}, u32[]{:S(2)}) async-start(f32[8,8,512]{2,1,0:T(8,128)} %get-tuple-element.30), calls=%async_computation | async-start | bytes 262144 | tf_op jit(solution)/shard_map/all_to_all | solution.py:435
  34.2 0.7 copy-start.6
  34.9 98.7 %all-to-all-start.2 = ((bf16[8,256,2048]{2,1,0:T(8,128)(2,1)}), bf16[8,256,2048]{2,1,0:T(8,128)(2,1)}, u32[]{:S(2)}, u32[]{:S(2)}) async-start(bf16[8,256,2048]{2,1,0:T(8,128)(2,1)} %pack_rows.2), calls=%async_computation.2 | async-start | bytes 16777216 | tf_op jit(solution)/shard_map/all_to_all | solution.py:435
  53.3 86.1 %copy-start.7 = (s32[4]{0:T(128)S(1)}, s32[4]{0:T(128)}, u32[]{:S(2)}) copy-start(s32[4]{0:T(128)} %constant.22.clone) | copy-start | bytes 52
  133.6 99.7 %all-to-all-start.1 = ((bf16[8,256,2048]{2,1,0:T(8,128)(2,1)}), bf16[8,256,2048]{2,1,0:T(8,128)(2,1)}, u32[]{:S(2)}, u32[]{:S(2)}) async-start(bf16[8,256,2048]{2,1,0:T(8,128)(2,1)} %pack_rows.3), calls=%async_computation.1 | async-start | bytes 16777216 | tf_op jit(solution)/shard_map/all_to_all | solution.py:435
  233.2 119.7 %all-to-all-start.4 = ((bf16[8,256,2048]{2,1,0:T(8,128)(2,1)}), bf16[8,256,2048]{2,1,0:T(8,128)(2,1)}, u32[]{:S(2)}, u32[]{:S(2)}) async-start(bf16[8,256,2048]{2,1,0:T(8,128)(2,1)} %get-tuple-element.39), calls=%async_computation.4 | async-start | bytes 16777216 | tf_op jit(solution)/shard_map/all_to_all | solution.py:435
  352.9 240.5 %all-to-all-start.3 = ((bf16[8,256,2048]{2,1,0:T(8,128)(2,1)}), bf16[8,256,2048]{2,1,0:T(8,128)(2,1)}, u32[]{:S(2)}, u32[]{:S(2)}) async-start(bf16[8,256,2048]{2,1,0:T(8,128)(2,1)} %get-tuple-element.38), calls=%async_computation.3 | async-start | bytes 16777216 | tf_op jit(solution)/shard_map/all_to_all | solution.py:435
  358.1 72.9 %collective-permute-start.1 = (f32[1536,512]{1,0:T(8,128)}, f32[1536,512]{1,0:T(8,128)S(1)}, u32[]{:S(2)}, u32[]{:S(2)}) collective-permute-start(f32[1536,512]{1,0:T(8,128)} %get-tuple-element.45), channel_id=1, source_target_pairs={{0,8},{8,16},{16,24},{24,0},{1,9},{9,17},{17,25},{25,1},{2,10},{10... | collective-permute-start | bytes 9437192 | tf_op jit(solution)/shard_map/ppermute | solution.py:450
  363.2 72.9 %collective-permute-start.4 = (f32[1536,512]{1,0:T(8,128)}, f32[1536,512]{1,0:T(8,128)S(1)}, u32[]{:S(2)}, u32[]{:S(2)}) collective-permute-start(f32[1536,512]{1,0:T(8,128)} %get-tuple-element.49), channel_id=1, source_target_pairs={{0,24},{8,0},{16,8},{24,16},{1,25},{9,1},{17,9},{25,17},{2,26},{10... | collective-permute-start | bytes 9437192 | tf_op jit(solution)/shard_map/ppermute | solution.py:450
  363.2 137.0 %collective-permute-start = (f32[1536,512]{1,0:T(8,128)}, f32[1536,512]{1,0:T(8,128)S(1)}, u32[]{:S(2)}, u32[]{:S(2)}) collective-permute-start(f32[1536,512]{1,0:T(8,128)} %get-tuple-element.43), channel_id=1, source_target_pairs={{0,24},{8,0},{16,8},{24,16},{1,25},{9,1},{17,9},{25,17},{2,26},{10... | collective-permute-start | bytes 9437192 | tf_op jit(solution)/shard_map/ppermute | solution.py:450
  364.5 135.7 %collective-permute-start.3 = (f32[1536,512]{1,0:T(8,128)}, f32[1536,512]{1,0:T(8,128)S(1)}, u32[]{:S(2)}, u32[]{:S(2)}) collective-permute-start(f32[1536,512]{1,0:T(8,128)} %get-tuple-element.47), channel_id=1, source_target_pairs={{0,8},{8,16},{16,24},{24,0},{1,9},{9,17},{17,25},{25,1},{2,10},{10... | collective-permute-start | bytes 9437192 | tf_op jit(solution)/shard_map/ppermute | solution.py:450
  431.0 5.1 copy-start.5
  433.8 131.9 %collective-permute-start.2 = (f32[1536,512]{1,0:T(8,128)S(1)}, f32[1536,512]{1,0:T(8,128)S(1)}, u32[]{:S(2)}, u32[]{:S(2)}) collective-permute-start(f32[1536,512]{1,0:T(8,128)S(1)} %add.21), channel_id=1, source_target_pairs={{0,8},{8,16},{16,24},{24,0},{1,9},{9,17},{17,25},{25,1},{2,10},{10... | collective-permute-start | bytes 9437192 | tf_op jit(solution)/shard_map/ppermute | solution.py:450
  436.8 130.8 %collective-permute-start.5 = (f32[1536,512]{1,0:T(8,128)S(1)}, f32[1536,512]{1,0:T(8,128)S(1)}, u32[]{:S(2)}, u32[]{:S(2)}) collective-permute-start(f32[1536,512]{1,0:T(8,128)S(1)} %add.22), channel_id=1, source_target_pairs={{0,24},{8,0},{16,8},{24,16},{1,25},{9,1},{17,9},{25,17},{2,26},{10... | collective-permute-start | bytes 9437192 | tf_op jit(solution)/shard_map/ppermute | solution.py:450
  500.2 69.1 %copy-start.1 = (f32[1536,512]{1,0:T(8,128)}, f32[1536,512]{1,0:T(8,128)S(1)}, u32[]{:S(2)}) copy-start(f32[1536,512]{1,0:T(8,128)S(1)} %collective-permute-done.refs_1_) | copy-start | bytes 9437188
  500.2 67.4 %copy-start.2 = (f32[1536,512]{1,0:T(8,128)}, f32[1536,512]{1,0:T(8,128)S(1)}, u32[]{:S(2)}) copy-start(f32[1536,512]{1,0:T(8,128)S(1)} %collective-permute-done.3.refs_4_) | copy-start | bytes 9437188
  565.7 1.9 copy-start.3
  567.6 1.7 copy-start.4
  569.3 9.9 %copy-start = (f32[8,1024]{1,0:T(8,128)S(1)}, f32[8,1024]{1,0:T(8,128)}, u32[]{:S(2)}) copy-start(f32[8,1024]{1,0:T(8,128)} %get-tuple-element.31.slot_ref) | copy-start | bytes 98308
Sparse Core Ops, SparseCore 0:
  14.8 119.8 all-gather.1

commit v5 on v4

--- a/solution.py
+++ b/solution.py
@@ -192,11 +192,6 @@
     else:
         acc[...] = jnp.zeros_like(acc)
 
-    if sums_in:
-        @pl.when(step == 0)
-        def _():
-            pltpu.make_async_copy(before, pq, sum_sem).start()
-
     def pick(s):
         slot = (lax.broadcasted_iota(jnp.int32, (size, size), 0) + 1).astype(F32)
         return meta_ref[s, pl.ds(k, 1), lanes] == slot
@@ -222,6 +217,10 @@
         load_prev().wait()
     load_weights(step).wait()
     ws = step % 2
+    if sums_in:
+        @pl.when(step == 0)
+        def _():
+            pltpu.make_async_copy(before, pq, sum_sem).start()
 
     @pl.loop(0, (total + TILE - 1) // TILE)
     def _(i):
@@ -351,14 +350,32 @@
 
 
 def home_kernel(first, slot_ref, ret_ref, *refs):
+    refs, (ret, acc, sems) = refs[:-3], refs[-3:]
     groups, size, width = ret_ref.shape
-    acc = refs[0][...] if first else None
+    loads = [pltpu.make_async_copy(ret_ref.at[g], ret.at[g], sems.at[g]) for g in range(groups)]
+
+    @pl.when(pl.program_id(0) == 0)
+    def _():
+        for copy in loads:
+            copy.start()
+
     outs = refs[1:] if first else refs
-    for g in range(groups):
-        part = dot(pick_rows(slot_ref[g:g + 1, :], first, size), ret_ref[g], 0, 0)
-        acc = part if acc is None else acc + part
+    acc[...] = refs[0][...] if first else jnp.zeros_like(acc)
+    slots = jnp.transpose(slot_ref[...])
+    lane = lax.broadcasted_iota(jnp.int32, slots.shape, 1)
+    want = (lax.broadcasted_iota(jnp.int32, (slots.shape[0], size), 1) + (first + 1)).astype(F32)
+
+    @pl.loop(0, groups)
+    def _(g):
+        @pl.when(pl.program_id(0) == 0)
+        def _():
+            pltpu.make_async_copy(ret_ref.at[g], ret.at[g], sems.at[g]).wait()
+
+        col = jnp.sum(jnp.where(lane == g, slots, 0.0), axis=1, keepdims=True)
+        acc[...] += dot((col == want).astype(F32).astype(BF16), ret[g], 1, 0)
+
     if len(outs) == 1:
-        outs[0][...] = acc
+        outs[0][...] = acc[...]
     else:
         outs[0][...] = acc[:, :width // 2].astype(BF16)
         outs[1][...] = acc[:, width // 2:].astype(BF16)
@@ -375,20 +392,40 @@
         functools.partial(home_kernel, c * size),
         grid=(tokens // block,),
         out_shape=[jax.ShapeDtypeStruct((tokens, w), t) for w, t in outs],
-        in_specs=[pl.BlockSpec((groups, block), lambda i: (0, i)), pl.BlockSpec(memory_space=pltpu.VMEM)] + [rows(width)] * len(extra),
+        in_specs=[pl.BlockSpec((groups, block), lambda i: (0, i)), pl.BlockSpec(memory_space=pl.ANY)] + [rows(width)] * len(extra),
         out_specs=[rows(w) for w, _ in outs],
-        compiler_params=pltpu.CompilerParams(vmem_limit_bytes=48 * 1024 * 1024),
+        scratch_shapes=[pltpu.VMEM(ret.shape, BF16), pltpu.VMEM((block, width), F32), pltpu.SemaphoreType.DMA((groups,))],
+        compiler_params=pltpu.CompilerParams(vmem_limit_bytes=58 * 1024 * 1024),
         cost_estimate=pl.CostEstimate(flops=2 * groups * size * tokens * width, bytes_accessed=groups * size * width * 2, transcendentals=0),
         name='home_sum',
     )(slot, ret, *extra)
 
 
-def finish_kernel(*refs):
-    g1_ref, g3_ref, g2_ref = refs[6:]
+def pair_kernel(a_ref, b_ref, c_ref, d_ref, left_ref, right_ref):
+    left_ref[...] = a_ref[...] + b_ref[...]
+    right_ref[...] = c_ref[...] + d_ref[...]
+
+
+def pair_sums(own0, soon0, own1, soon1):
+    rows, ff = own0.shape
+    spec = pl.BlockSpec((ff // 2, ff), lambda i: (i, 0))
+    return pl.pallas_call(
+        pair_kernel,
+        grid=(2 * rows // ff,),
+        out_shape=[jax.ShapeDtypeStruct(own0.shape, F32)] * 2,
+        in_specs=[spec] * 4,
+        out_specs=[spec] * 2,
+        compiler_params=pltpu.CompilerParams(vmem_limit_bytes=58 * 1024 * 1024),
+        cost_estimate=pl.CostEstimate(flops=2 * rows * ff, bytes_accessed=24 * rows * ff, transcendentals=0),
+        name='pair_sums',
+    )(own0, soon0, own1, soon1)
+
+
+def finish_kernel(a_ref, b_ref, c_ref, d_ref, g1_ref, g3_ref, g2_ref):
     tops = pl.num_programs(0) - pl.num_programs(0) // 3
     i = pl.program_id(0)
-    left = refs[0][...] + (refs[1][...] + refs[2][...])
-    right = refs[3][...] + (refs[4][...] + refs[5][...])
+    left = a_ref[...] + b_ref[...]
+    right = c_ref[...] + d_ref[...]
 
     @pl.when(i < tops)
     def _():
@@ -400,8 +437,8 @@
         g2_ref[0] = jnp.concatenate([left, right], axis=1)
 
 
-def finish(lefts, rights, hidden):
-    rows, ff = lefts[0].shape
+def finish(left, late0, right, late1, hidden):
+    rows, ff = left.shape
     assert rows == hidden + ff and hidden == 2 * ff
     block = ff // 2
     tops = hidden // block
@@ -410,12 +447,12 @@
         finish_kernel,
         grid=(rows // block,),
         out_shape=[jax.ShapeDtypeStruct((1,) + a, F32) for a in ((hidden, ff), (hidden, ff), (ff, hidden))],
-        in_specs=[pl.BlockSpec((block, ff), lambda i: (i, 0))] * 6,
+        in_specs=[pl.BlockSpec((block, ff), lambda i: (i, 0))] * 4,
         out_specs=[top, top, pl.BlockSpec((1, block, hidden), lambda i: (0, jnp.maximum(i - tops, 0), 0))],
-        compiler_params=pltpu.CompilerParams(vmem_limit_bytes=58 * 1024 * 1024),
-        cost_estimate=pl.CostEstimate(flops=4 * rows * ff, bytes_accessed=32 * rows * ff, transcendentals=0),
+        compiler_params=pltpu.CompilerParams(vmem_limit_bytes=16 * 1024 * 1024),
+        cost_estimate=pl.CostEstimate(flops=2 * rows * ff, bytes_accessed=24 * rows * ff, transcendentals=0),
         name='finish',
-    )(*lefts, *rights)
+    )(left, late0, right, late1)
 
 
 def solution(mesh):
@@ -465,11 +502,12 @@
         rets.append(swap(pq))
         late0 = ring(next0 + far0, 1)
         late1 = ring(last1 + far1, -1)
+        left, right = pair_sums(own0, soon0, own1, soon1)
         for i in range(chunks):
-            total = home_sum(slot, rets[i], i, total, i == c, 256)
+            total = home_sum(slot, rets[i], i, total, i == c, tokens // 2)
             total = total[0] if i < c else total
         y_out, dx_out = total
-        g1, g3, g2 = finish((own0, soon0, late0), (own1, soon1, late1), hidden)
+        g1, g3, g2 = finish(left, late0, right, late1, hidden)
         return y_out, dx_out, g1, g3, g2
 
     return jax.shard_map(layer, mesh=mesh, in_specs=(tok_spec, tok_spec, tok_spec, tok_spec, weight_spec, weight_spec, weight_spec), out_specs=(tok_spec, tok_spec, grad_spec, grad_spec, grad_spec), check_vma=False)

time: 615 us -> 616 us (level)
  waiting for transfers between devices: 278 us -> 269 us
    ppermute x6, waiting for transfers between devices: 197 us -> 187 us  [layer(): lax.ppermute(a, 'ing', [(i, (i + d) % inner) for i in range(inner)])]
    pallas_call x0 -> x1, Pallas kernels: none -> 8.21 us  [pair_sums(): pl.pallas_call(pair_kernel, grid=(2 * rows // ff,), out_shape=[jax.ShapeD...]
    pallas_call x2, Pallas kernels: 28.6 us -> 35.1 us  [home_sum(): pl.pallas_call(functools.partial(home_kernel, c * size), grid=(tokens //...]
where the time goes in v5:
time: 616 us; the launch traced here: 615 us
  Pallas kernels  285 us (46%)
  waiting for transfers between devices  269 us (44%)
  starting transfers between devices  37.5 us (6%)
  between operations  14.2 us (2%)
    pallas_call x4, Pallas kernels, run_experts(): pl.pallas_call(functools.partial(expert_kernel, chunk, first, steps, prev...  201 us
    ppermute x6, waiting for transfers between devices, layer(): lax.ppermute(a, 'ing', [(i, (i + d) % inner) for i in range(inner)])  187 us
    all_to_all x5, waiting for transfers between devices, layer(): swap = lambda a: lax.all_to_all(a, 'grp', 0, 0, tiled=True)  81.3 us
    pallas_call x2, Pallas kernels, home_sum(): pl.pallas_call(functools.partial(home_kernel, c * size), grid=(tokens //...  35.1 us
    all_to_all x5, starting transfers between devices, layer(): swap = lambda a: lax.all_to_all(a, 'grp', 0, 0, tiled=True)  28.1 us
    pallas_call x2, Pallas kernels, pack_rows(): pl.pallas_call(functools.partial(pack_kernel, c * size), grid=(groups,),...  26.9 us
  transfers between devices with their start and end apart: 12, of which 6 were waited for; matrix products, arithmetic and copies ran while one was open for 1% of the time, Pallas kernels for 42%

profile of v5, /device:TPU:97, one launch (start us, length us, event | category | flops | bytes accessed | tf_op | source)
XLA Modules:
  0.0 615.4 jit_solution(5879554401943821305)
XLA Ops:
  7.2 7.4 %make_tables.1 = (f32[8,1024]{1,0:T(8,128)}, f32[8,8,512]{2,1,0:T(8,128)}, bf16[1,1536,1024]{2,1,0:T(8,128)(2,1)}) custom-call(s32[8,1024]{1,0:T(8,128)} %bitcast.2, f32[8,1024]{1,0:T(8,128)} %bitcast.3, bf16[1,1024,512]{2,1,0:T(8,128)(2,1)} %refs_0_.1, bf16[1,1024,512]{2,1,0:T(8,128)(2,1)} %refs_1_.1, bf16[1,512,1024]{2,1,0:T(8,128)(2,1)} %refs_2_.1), custom_call_target="tpu_custom_call" | custom-call | flops 1073741824 | bytes 262144 | tf_op jit(solution)/shard_map/make_tables/pallas_call | solution.py:92
  14.7 6.0 all-to-all-start
  20.7 13.5 %pack_rows.2 = bf16[8,256,2048]{2,1,0:T(8,128)(2,1)} custom-call(f32[8,1024]{1,0:T(8,128)} %get-tuple-element.33.slot_ref, bf16[1024,1024]{1,0:T(8,128)(2,1)} %x_ref.3, bf16[1024,1024]{1,0:T(8,128)(2,1)} %dy_ref.3), custom_call_target="tpu_custom_call" | custom-call | flops 8589934592 | bytes 8388608 | tf_op jit(solution)/shard_map/pack_rows/pallas_call | solution.py:123
  34.2 0.7 copy-done.4
  34.9 5.0 all-to-all-start.2
  39.9 13.4 %pack_rows.3 = bf16[8,256,2048]{2,1,0:T(8,128)(2,1)} custom-call(f32[8,1024]{1,0:T(8,128)} %get-tuple-element.33.slot_ref, bf16[1024,1024]{1,0:T(8,128)(2,1)} %x_ref.3, bf16[1024,1024]{1,0:T(8,128)(2,1)} %dy_ref.3), custom_call_target="tpu_custom_call" | custom-call | flops 8589934592 | bytes 8388608 | tf_op jit(solution)/shard_map/pack_rows/pallas_call | solution.py:123
  53.3 80.2 %all-to-all-done.2.xd_ref = bf16[8,256,2048]{2,1,0:T(8,128)(2,1)} async-done(((bf16[8,256,2048]{2,1,0:T(8,128)(2,1)}), bf16[8,256,2048]{2,1,0:T(8,128)(2,1)}, u32[]{:S(2)}, u32[]{:S(2)}) %all-to-all-start.2) | async-done | bytes 8388640 | tf_op jit(solution)/shard_map/all_to_all | solution.py:472
  133.6 5.8 all-to-all-start.1
  139.4 0.5 and_select_fusion.order_ref
  139.9 92.2 %run_experts.4 = (bf16[8,256,2048]{2,1,0:T(8,128)(2,1)}, f32[4,1536,1024]{2,1,0:T(8,128)}) custom-call(s32[4]{0:T(128)} %and_select_fusion.order_ref, f32[8,8,512]{2,1,0:T(8,128)} %copy-done.4, bf16[8,256,2048]{2,1,0:T(8,128)(2,1)} %all-to-all-done.2.xd_ref, bf16[4,1536,1024]{2,1,0:T(8,128)(2,1)} %all-gather.2.cloned.1.call-done.w_ref), custom_call_target="tpu_custom_call" | custom-call | flops 47244640256 | bytes 16777216 | tf_op jit(solution)/shard_map/run_experts/pallas_call | solution.py:336
  232.1 1.1 all-to-all-done.1.xd_ref
  233.2 5.8 all-to-all-start.4
  239.0 27.0 %run_experts.5 = (f32[8,256,2048]{2,1,0:T(8,128)}, f32[1536,512]{1,0:T(8,128)}, f32[1536,512]{1,0:T(8,128)}) custom-call(s32[4]{0:T(128)} %and_select_fusion.order_ref, f32[8,8,512]{2,1,0:T(8,128)} %copy-done.4, bf16[8,256,2048]{2,1,0:T(8,128)(2,1)} %all-to-all-done.1.xd_ref, bf16[4,1536,1024]{2,1,0:T(8,128)(2,1)} %all-gather.2.cloned.1.call-done.w_ref, ...), custom_call_target="tpu_custom_call" | custom-call | flops 11811160064 | bytes 16777216 | tf_op jit(solution)/shard_map/run_experts/pallas_call | solution.py:336
  266.0 55.8 %run_experts.6 = (f32[8,256,2048]{2,1,0:T(8,128)}, f32[1536,512]{1,0:T(8,128)}, f32[1536,512]{1,0:T(8,128)}, f32[1536,512]{1,0:T(8,128)}, f32[1536,512]{1,0:T(8,128)}) custom-call(s32[4]{0:T(128)} %and_select_fusion.order_ref, f32[8,8,512]{2,1,0:T(8,128)} %copy-done.4, bf16[8,256,2048]{2,1,0:T(8,128)(2,1)} %all-to-all-done.1.xd_ref, ...), custom_call_target="tpu_custom_call" | custom-call | flops 23622320128 | bytes 16777216 | tf_op jit(solution)/shard_map/run_experts/pallas_call | solution.py:336
  321.7 26.3 %run_experts.7 = (bf16[8,256,2048]{2,1,0:T(8,128)(2,1)}, f32[1536,512]{1,0:T(8,128)}, f32[1536,512]{1,0:T(8,128)}) custom-call(s32[4]{0:T(128)} %and_select_fusion.order_ref, f32[8,8,512]{2,1,0:T(8,128)} %copy-done.4, bf16[8,256,2048]{2,1,0:T(8,128)(2,1)} %all-to-all-done.1.xd_ref, bf16[4,1536,1024]{2,1,0:T(8,128)(2,1)} %all-gather.2.cloned.1.call-done.w_ref, ...), custom_call_target="tpu_custom_call" | custom-call | flops 11811160064 | bytes 16777216 | tf_op jit(solution)/shard_map/run_experts/pallas_call | solution.py:336
  348.1 5.4 all-to-all-start.3
  353.5 5.2 collective-permute-start.2
  358.7 1.1 collective-permute-start
  360.2 66.3 %collective-permute-done.2 = f32[1536,512]{1,0:T(8,128)S(1)} collective-permute-done((f32[1536,512]{1,0:T(8,128)}, f32[1536,512]{1,0:T(8,128)S(1)}, u32[]{:S(2)}, u32[]{:S(2)}) %collective-permute-start.2) | collective-permute-done | bytes 3145760 | tf_op jit(solution)/shard_map/ppermute | solution.py:487
  426.5 2.4 add.21
  429.0 2.2 collective-permute-start.3
  431.2 2.4 add.22
  433.6 0.5 collective-permute-start.5
  434.1 61.8 %collective-permute-done.b_ref = f32[1536,512]{1,0:T(8,128)} collective-permute-done((f32[1536,512]{1,0:T(8,128)}, f32[1536,512]{1,0:T(8,128)}, u32[]{:S(2)}, u32[]{:S(2)}) %collective-permute-start) | collective-permute-done | bytes 3145760 | tf_op jit(solution)/shard_map/ppermute | solution.py:487
  495.8 8.2 %pair_sums.1 = (f32[1536,512]{1,0:T(8,128)}, f32[1536,512]{1,0:T(8,128)}) custom-call(f32[1536,512]{1,0:T(8,128)} %get-tuple-element.44.a_ref, f32[1536,512]{1,0:T(8,128)} %collective-permute-done.b_ref, f32[1536,512]{1,0:T(8,128)} %get-tuple-element.46.c_ref, f32[1536,512]{1,0:T(8,128)} %collective-permute-done.1.d_ref), custom_call_target="tpu_custom_call" | custom-call | flops 1572864 | bytes 18874368 | tf_op jit(solution)/shard_map/pair_sums/pallas_call | solution.py:412
  504.1 57.3 %collective-permute-done.3.b_ref = f32[1536,512]{1,0:T(8,128)S(1)} collective-permute-done((f32[1536,512]{1,0:T(8,128)}, f32[1536,512]{1,0:T(8,128)S(1)}, u32[]{:S(2)}, u32[]{:S(2)}) %collective-permute-start.3) | collective-permute-done | bytes 3145760 | tf_op jit(solution)/shard_map/ppermute | solution.py:487
  561.3 1.9 collective-permute-done.5.d_ref
  563.3 1.9 copy-done
  565.1 1.9 copy-done.1
  567.0 6.4 %finish.1 = (f32[1,1024,512]{2,1,0:T(8,128)}, f32[1,1024,512]{2,1,0:T(8,128)}, f32[1,512,1024]{2,1,0:T(8,128)}) custom-call(f32[1536,512]{1,0:T(8,128)S(1)} %copy-done, f32[1536,512]{1,0:T(8,128)S(1)} %collective-permute-done.3.b_ref, f32[1536,512]{1,0:T(8,128)S(1)} %copy-done.1, f32[1536,512]{1,0:T(8,128)} %collective-permute-done.5.d_ref), custom_call_target="tpu_custom_call" | custom-call | flops 1572864 | bytes 18874368 | tf_op jit(solution)/shard_map/finish/pallas_call | solution.py:446
  573.4 16.9 %home_sum.2.refs_0_ = f32[1024,2048]{1,0:T(8,128)} custom-call(f32[8,1024]{1,0:T(8,128)} %get-tuple-element.33.slot_ref, bf16[8,256,2048]{2,1,0:T(8,128)(2,1)} %all-to-all-done.4.ret_ref), custom_call_target="tpu_custom_call" | custom-call | flops 8589934592 | bytes 8388608 | tf_op jit(solution)/shard_map/home_sum/pallas_call | solution.py:391
  590.4 18.2 %home_sum.3 = (bf16[1024,1024]{1,0:T(8,128)(2,1)}, bf16[1024,1024]{1,0:T(8,128)(2,1)}) custom-call(f32[8,1024]{1,0:T(8,128)} %get-tuple-element.33.slot_ref, bf16[8,256,2048]{2,1,0:T(8,128)(2,1)} %all-to-all-done.3.ret_ref, f32[1024,2048]{1,0:T(8,128)} %home_sum.2.refs_0_), custom_call_target="tpu_custom_call" | custom-call | flops 8589934592 | bytes 8388608 | tf_op jit(solution)/shard_map/home_sum/pallas_call | solution.py:391
  (19 shorter events, 0.5 us)
Async XLA Ops:
  7.2 132.7 %all-gather.2.cloned.1.call-start = ((), (), s32[]{:S(2)}) async-start(), calls=%async_computation.5 | async-start | bytes 15728640 | tf_op jit(solution)/shard_map/all_gather | solution.py:475
  14.7 19.5 %all-to-all-start = ((f32[8,8,512]{2,1,0:T(8,128)}), f32[8,8,512]{2,1,0:T(8,128)S(1)}, u32[]{:S(2)}, u32[]{:S(2)}) async-start(f32[8,8,512]{2,1,0:T(8,128)} %get-tuple-element.32), calls=%async_computation | async-start | bytes 262144 | tf_op jit(solution)/shard_map/all_to_all | solution.py:472
  34.2 0.7 copy-start.4
  34.9 98.7 %all-to-all-start.2 = ((bf16[8,256,2048]{2,1,0:T(8,128)(2,1)}), bf16[8,256,2048]{2,1,0:T(8,128)(2,1)}, u32[]{:S(2)}, u32[]{:S(2)}) async-start(bf16[8,256,2048]{2,1,0:T(8,128)(2,1)} %pack_rows.2), calls=%async_computation.2 | async-start | bytes 16777216 | tf_op jit(solution)/shard_map/all_to_all | solution.py:472
  53.3 86.1 %copy-start.5 = (s32[4]{0:T(128)S(1)}, s32[4]{0:T(128)}, u32[]{:S(2)}) copy-start(s32[4]{0:T(128)} %constant.22.clone) | copy-start | bytes 52
  133.6 99.7 %all-to-all-start.1 = ((bf16[8,256,2048]{2,1,0:T(8,128)(2,1)}), bf16[8,256,2048]{2,1,0:T(8,128)(2,1)}, u32[]{:S(2)}, u32[]{:S(2)}) async-start(bf16[8,256,2048]{2,1,0:T(8,128)(2,1)} %pack_rows.3), calls=%async_computation.1 | async-start | bytes 16777216 | tf_op jit(solution)/shard_map/all_to_all | solution.py:472
  233.2 114.9 %all-to-all-start.4 = ((bf16[8,256,2048]{2,1,0:T(8,128)(2,1)}), bf16[8,256,2048]{2,1,0:T(8,128)(2,1)}, u32[]{:S(2)}, u32[]{:S(2)}) async-start(bf16[8,256,2048]{2,1,0:T(8,128)(2,1)} %get-tuple-element.41), calls=%async_computation.4 | async-start | bytes 16777216 | tf_op jit(solution)/shard_map/all_to_all | solution.py:472
  348.1 78.4 %copy-start.3 = (f32[1536,512]{1,0:T(8,128)S(1)}, f32[1536,512]{1,0:T(8,128)}, u32[]{:S(2)}) copy-start(f32[1536,512]{1,0:T(8,128)} %get-tuple-element.49) | copy-start | bytes 9437188
  348.1 242.3 %all-to-all-start.3 = ((bf16[8,256,2048]{2,1,0:T(8,128)(2,1)}), bf16[8,256,2048]{2,1,0:T(8,128)(2,1)}, u32[]{:S(2)}, u32[]{:S(2)}) async-start(bf16[8,256,2048]{2,1,0:T(8,128)(2,1)} %get-tuple-element.40), calls=%async_computation.3 | async-start | bytes 16777216 | tf_op jit(solution)/shard_map/all_to_all | solution.py:472
  353.5 73.0 %collective-permute-start.2 = (f32[1536,512]{1,0:T(8,128)}, f32[1536,512]{1,0:T(8,128)S(1)}, u32[]{:S(2)}, u32[]{:S(2)}) collective-permute-start(f32[1536,512]{1,0:T(8,128)} %get-tuple-element.50), channel_id=1, source_target_pairs={{0,8},{8,16},{16,24},{24,0},{1,9},{9,17},{17,25},{25,1},{2,10},{10... | collective-permute-start | bytes 9437192 | tf_op jit(solution)/shard_map/ppermute | solution.py:487
  358.7 72.4 %collective-permute-start.4 = (f32[1536,512]{1,0:T(8,128)}, f32[1536,512]{1,0:T(8,128)S(1)}, u32[]{:S(2)}, u32[]{:S(2)}) collective-permute-start(f32[1536,512]{1,0:T(8,128)} %get-tuple-element.53), channel_id=1, source_target_pairs={{0,24},{8,0},{16,8},{24,16},{1,25},{9,1},{17,9},{25,17},{2,26},{10... | collective-permute-start | bytes 9437192 | tf_op jit(solution)/shard_map/ppermute | solution.py:487
  358.7 137.1 %collective-permute-start = (f32[1536,512]{1,0:T(8,128)}, f32[1536,512]{1,0:T(8,128)}, u32[]{:S(2)}, u32[]{:S(2)}) collective-permute-start(f32[1536,512]{1,0:T(8,128)} %get-tuple-element.45), channel_id=1, source_target_pairs={{0,24},{8,0},{16,8},{24,16},{1,25},{9,1},{17,9},{25,17},{2,26},{10... | collective-permute-start | bytes 9437192 | tf_op jit(solution)/shard_map/ppermute | solution.py:487
  359.9 136.0 %collective-permute-start.1 = (f32[1536,512]{1,0:T(8,128)}, f32[1536,512]{1,0:T(8,128)}, u32[]{:S(2)}, u32[]{:S(2)}) collective-permute-start(f32[1536,512]{1,0:T(8,128)} %get-tuple-element.47), channel_id=1, source_target_pairs={{0,8},{8,16},{16,24},{24,0},{1,9},{9,17},{17,25},{25,1},{2,10},{10... | collective-permute-start | bytes 9437192 | tf_op jit(solution)/shard_map/ppermute | solution.py:487
  426.5 4.7 copy-start.2
  429.0 132.4 %collective-permute-start.3 = (f32[1536,512]{1,0:T(8,128)}, f32[1536,512]{1,0:T(8,128)S(1)}, u32[]{:S(2)}, u32[]{:S(2)}) collective-permute-start(f32[1536,512]{1,0:T(8,128)} %add.21), channel_id=1, source_target_pairs={{0,8},{8,16},{16,24},{24,0},{1,9},{9,17},{17,25},{25,1},{2,10},{10... | collective-permute-start | bytes 9437192 | tf_op jit(solution)/shard_map/ppermute | solution.py:487
  433.6 129.7 %collective-permute-start.5 = (f32[1536,512]{1,0:T(8,128)}, f32[1536,512]{1,0:T(8,128)}, u32[]{:S(2)}, u32[]{:S(2)}) collective-permute-start(f32[1536,512]{1,0:T(8,128)} %add.22), channel_id=1, source_target_pairs={{0,24},{8,0},{16,8},{24,16},{1,25},{9,1},{17,9},{25,17},{2,26},{10... | collective-permute-start | bytes 9437192 | tf_op jit(solution)/shard_map/ppermute | solution.py:487
  563.3 1.9 copy-start
  565.1 1.9 copy-start.1
Sparse Core Ops, SparseCore 0:
  14.8 119.8 all-gather.1

commit v6 on v5

--- a/solution.py
+++ b/solution.py
@@ -350,7 +350,7 @@
 
 
 def home_kernel(first, slot_ref, ret_ref, *refs):
-    refs, (ret, acc, sems) = refs[:-3], refs[-3:]
+    refs, (ret, sems) = refs[:-2], refs[-2:]
     groups, size, width = ret_ref.shape
     loads = [pltpu.make_async_copy(ret_ref.at[g], ret.at[g], sems.at[g]) for g in range(groups)]
 
@@ -360,22 +360,16 @@
             copy.start()
 
     outs = refs[1:] if first else refs
-    acc[...] = refs[0][...] if first else jnp.zeros_like(acc)
-    slots = jnp.transpose(slot_ref[...])
-    lane = lax.broadcasted_iota(jnp.int32, slots.shape, 1)
-    want = (lax.broadcasted_iota(jnp.int32, (slots.shape[0], size), 1) + (first + 1)).astype(F32)
-
-    @pl.loop(0, groups)
-    def _(g):
+    acc = refs[0][...] if first else None
+    for g in range(groups):
         @pl.when(pl.program_id(0) == 0)
-        def _():
-            pltpu.make_async_copy(ret_ref.at[g], ret.at[g], sems.at[g]).wait()
-
-        col = jnp.sum(jnp.where(lane == g, slots, 0.0), axis=1, keepdims=True)
-        acc[...] += dot((col == want).astype(F32).astype(BF16), ret[g], 1, 0)
-
+        def _(g=g):
+            loads[g].wait()
+
+        part = dot(pick_rows(slot_ref[g:g + 1, :], first, size), ret[g], 0, 0)
+        acc = part if acc is None else acc + part
     if len(outs) == 1:
-        outs[0][...] = acc[...]
+        outs[0][...] = acc
     else:
         outs[0][...] = acc[:, :width // 2].astype(BF16)
         outs[1][...] = acc[:, width // 2:].astype(BF16)
@@ -394,7 +388,7 @@
         out_shape=[jax.ShapeDtypeStruct((tokens, w), t) for w, t in outs],
         in_specs=[pl.BlockSpec((groups, block), lambda i: (0, i)), pl.BlockSpec(memory_space=pl.ANY)] + [rows(width)] * len(extra),
         out_specs=[rows(w) for w, _ in outs],
-        scratch_shapes=[pltpu.VMEM(ret.shape, BF16), pltpu.VMEM((block, width), F32), pltpu.SemaphoreType.DMA((groups,))],
+        scratch_shapes=[pltpu.VMEM(ret.shape, BF16), pltpu.SemaphoreType.DMA((groups,))],
         compiler_params=pltpu.CompilerParams(vmem_limit_bytes=58 * 1024 * 1024),
         cost_estimate=pl.CostEstimate(flops=2 * groups * size * tokens * width, bytes_accessed=groups * size * width * 2, transcendentals=0),
         name='home_sum',
@@ -449,7 +443,7 @@
         out_shape=[jax.ShapeDtypeStruct((1,) + a, F32) for a in ((hidden, ff), (hidden, ff), (ff, hidden))],
         in_specs=[pl.BlockSpec((block, ff), lambda i: (i, 0))] * 4,
         out_specs=[top, top, pl.BlockSpec((1, block, hidden), lambda i: (0, jnp.maximum(i - tops, 0), 0))],
-        compiler_params=pltpu.CompilerParams(vmem_limit_bytes=16 * 1024 * 1024),
+        compiler_params=pltpu.CompilerParams(vmem_limit_bytes=58 * 1024 * 1024),
         cost_estimate=pl.CostEstimate(flops=2 * rows * ff, bytes_accessed=24 * rows * ff, transcendentals=0),
         name='finish',
     )(left, late0, right, late1)
@@ -504,7 +498,7 @@
         late1 = ring(last1 + far1, -1)
         left, right = pair_sums(own0, soon0, own1, soon1)
         for i in range(chunks):
-            total = home_sum(slot, rets[i], i, total, i == c, tokens // 2)
+            total = home_sum(slot, rets[i], i, total, i == c, tokens // 4)
             total = total[0] if i < c else total
         y_out, dx_out = total
         g1, g3, g2 = finish(left, late0, right, late1, hidden)

time: 616 us -> 610 us (level)
  transfers between devices with their start and end apart: 12 -> 12, of which waited for: 6 -> 6; matrix products, arithmetic and copies ran while one was open for 1% -> 1% of each run, Pallas kernels for 42% -> 43%
where the time goes in v6:
time: 610 us
  Pallas kernels  283 us (46%)
  waiting for transfers between devices  269 us (44%)
  starting transfers between devices  37.4 us (6%)
  between operations  14.2 us (2%)
    pallas_call x4, Pallas kernels, run_experts(): pl.pallas_call(functools.partial(expert_kernel, chunk, first, steps, prev...  201 us
    ppermute x6, waiting for transfers between devices, layer(): lax.ppermute(a, 'ing', [(i, (i + d) % inner) for i in range(inner)])  187 us
    all_to_all x5, waiting for transfers between devices, layer(): swap = lambda a: lax.all_to_all(a, 'grp', 0, 0, tiled=True)  81.3 us
    pallas_call x2, Pallas kernels, home_sum(): pl.pallas_call(functools.partial(home_kernel, c * size), grid=(tokens //...  31.1 us
    all_to_all x5, starting transfers between devices, layer(): swap = lambda a: lax.all_to_all(a, 'grp', 0, 0, tiled=True)  28.1 us
    pallas_call x2, Pallas kernels, pack_rows(): pl.pallas_call(functools.partial(pack_kernel, c * size), grid=(groups,),...  26.9 us
  transfers between devices with their start and end apart: 12, of which 6 were waited for; matrix products, arithmetic and copies ran while one was open for 1% of the time, Pallas kernels for 43%

profile of v6, /device:TPU:97, one launch (start us, length us, event | category | flops | bytes accessed | tf_op | source)
XLA Modules:
  0.0 609.6 jit_solution(4376003607572778120)
XLA Ops:
  7.2 0.1 all-gather.2.cloned.1.call-start
  7.2 7.4 %make_tables.1 = (f32[8,1024]{1,0:T(8,128)}, f32[8,8,512]{2,1,0:T(8,128)}, bf16[1,1536,1024]{2,1,0:T(8,128)(2,1)}) custom-call(s32[8,1024]{1,0:T(8,128)} %bitcast.2, f32[8,1024]{1,0:T(8,128)} %bitcast.3, bf16[1,1024,512]{2,1,0:T(8,128)(2,1)} %refs_0_.1, bf16[1,1024,512]{2,1,0:T(8,128)(2,1)} %refs_1_.1, bf16[1,512,1024]{2,1,0:T(8,128)(2,1)} %refs_2_.1), custom_call_target="tpu_custom_call" | custom-call | flops 1073741824 | bytes 262144 | tf_op jit(solution)/shard_map/make_tables/pallas_call | solution.py:92
  14.7 6.0 all-to-all-start
  20.7 13.5 %pack_rows.2 = bf16[8,256,2048]{2,1,0:T(8,128)(2,1)} custom-call(f32[8,1024]{1,0:T(8,128)} %get-tuple-element.33.slot_ref, bf16[1024,1024]{1,0:T(8,128)(2,1)} %x_ref.3, bf16[1024,1024]{1,0:T(8,128)(2,1)} %dy_ref.3), custom_call_target="tpu_custom_call" | custom-call | flops 8589934592 | bytes 8388608 | tf_op jit(solution)/shard_map/pack_rows/pallas_call | solution.py:123
  34.2 0.7 copy-done.3
  34.9 5.0 all-to-all-start.2
  39.9 13.4 %pack_rows.3 = bf16[8,256,2048]{2,1,0:T(8,128)(2,1)} custom-call(f32[8,1024]{1,0:T(8,128)} %get-tuple-element.33.slot_ref, bf16[1024,1024]{1,0:T(8,128)(2,1)} %x_ref.3, bf16[1024,1024]{1,0:T(8,128)(2,1)} %dy_ref.3), custom_call_target="tpu_custom_call" | custom-call | flops 8589934592 | bytes 8388608 | tf_op jit(solution)/shard_map/pack_rows/pallas_call | solution.py:123
  53.3 80.2 %all-to-all-done.2.xd_ref = bf16[8,256,2048]{2,1,0:T(8,128)(2,1)} async-done(((bf16[8,256,2048]{2,1,0:T(8,128)(2,1)}), bf16[8,256,2048]{2,1,0:T(8,128)(2,1)}, u32[]{:S(2)}, u32[]{:S(2)}) %all-to-all-start.2) | async-done | bytes 8388640 | tf_op jit(solution)/shard_map/all_to_all | solution.py:466
  133.6 5.8 all-to-all-start.1
  139.4 0.5 and_select_fusion.order_ref
  139.9 92.2 %run_experts.4 = (bf16[8,256,2048]{2,1,0:T(8,128)(2,1)}, f32[4,1536,1024]{2,1,0:T(8,128)}) custom-call(s32[4]{0:T(128)} %and_select_fusion.order_ref, f32[8,8,512]{2,1,0:T(8,128)} %copy-done.3, bf16[8,256,2048]{2,1,0:T(8,128)(2,1)} %all-to-all-done.2.xd_ref, bf16[4,1536,1024]{2,1,0:T(8,128)(2,1)} %all-gather.2.cloned.1.call-done.w_ref), custom_call_target="tpu_custom_call" | custom-call | flops 47244640256 | bytes 16777216 | tf_op jit(solution)/shard_map/run_experts/pallas_call | solution.py:336
  232.1 1.1 all-to-all-done.1.xd_ref
  233.2 5.8 all-to-all-start.4
  239.0 27.0 %run_experts.5 = (f32[8,256,2048]{2,1,0:T(8,128)}, f32[1536,512]{1,0:T(8,128)}, f32[1536,512]{1,0:T(8,128)}) custom-call(s32[4]{0:T(128)} %and_select_fusion.order_ref, f32[8,8,512]{2,1,0:T(8,128)} %copy-done.3, bf16[8,256,2048]{2,1,0:T(8,128)(2,1)} %all-to-all-done.1.xd_ref, bf16[4,1536,1024]{2,1,0:T(8,128)(2,1)} %all-gather.2.cloned.1.call-done.w_ref, ...), custom_call_target="tpu_custom_call" | custom-call | flops 11811160064 | bytes 16777216 | tf_op jit(solution)/shard_map/run_experts/pallas_call | solution.py:336
  266.0 55.8 %run_experts.6 = (f32[8,256,2048]{2,1,0:T(8,128)}, f32[1536,512]{1,0:T(8,128)}, f32[1536,512]{1,0:T(8,128)}, f32[1536,512]{1,0:T(8,128)}, f32[1536,512]{1,0:T(8,128)}) custom-call(s32[4]{0:T(128)} %and_select_fusion.order_ref, f32[8,8,512]{2,1,0:T(8,128)} %copy-done.3, bf16[8,256,2048]{2,1,0:T(8,128)(2,1)} %all-to-all-done.1.xd_ref, ...), custom_call_target="tpu_custom_call" | custom-call | flops 23622320128 | bytes 16777216 | tf_op jit(solution)/shard_map/run_experts/pallas_call | solution.py:336
  321.8 26.3 %run_experts.7 = (bf16[8,256,2048]{2,1,0:T(8,128)(2,1)}, f32[1536,512]{1,0:T(8,128)}, f32[1536,512]{1,0:T(8,128)}) custom-call(s32[4]{0:T(128)} %and_select_fusion.order_ref, f32[8,8,512]{2,1,0:T(8,128)} %copy-done.3, bf16[8,256,2048]{2,1,0:T(8,128)(2,1)} %all-to-all-done.1.xd_ref, bf16[4,1536,1024]{2,1,0:T(8,128)(2,1)} %all-gather.2.cloned.1.call-done.w_ref, ...), custom_call_target="tpu_custom_call" | custom-call | flops 11811160064 | bytes 16777216 | tf_op jit(solution)/shard_map/run_experts/pallas_call | solution.py:336
  348.1 5.4 all-to-all-start.3
  353.6 5.1 collective-permute-start.2
  358.7 1.3 collective-permute-start
  360.0 0.2 collective-permute-start.1
  360.2 66.3 %collective-permute-done.2 = f32[1536,512]{1,0:T(8,128)S(1)} collective-permute-done((f32[1536,512]{1,0:T(8,128)}, f32[1536,512]{1,0:T(8,128)S(1)}, u32[]{:S(2)}, u32[]{:S(2)}) %collective-permute-start.2) | collective-permute-done | bytes 3145760 | tf_op jit(solution)/shard_map/ppermute | solution.py:481
  426.4 2.4 add.21
  428.9 2.2 collective-permute-start.3
  431.1 2.4 add.22
  433.5 0.5 collective-permute-start.5
  433.9 61.8 %collective-permute-done.b_ref = f32[1536,512]{1,0:T(8,128)} collective-permute-done((f32[1536,512]{1,0:T(8,128)}, f32[1536,512]{1,0:T(8,128)}, u32[]{:S(2)}, u32[]{:S(2)}) %collective-permute-start) | collective-permute-done | bytes 3145760 | tf_op jit(solution)/shard_map/ppermute | solution.py:481
  495.8 8.2 %pair_sums.1 = (f32[1536,512]{1,0:T(8,128)}, f32[1536,512]{1,0:T(8,128)}) custom-call(f32[1536,512]{1,0:T(8,128)} %get-tuple-element.44.a_ref, f32[1536,512]{1,0:T(8,128)} %collective-permute-done.b_ref, f32[1536,512]{1,0:T(8,128)} %get-tuple-element.46.c_ref, f32[1536,512]{1,0:T(8,128)} %collective-permute-done.1.d_ref), custom_call_target="tpu_custom_call" | custom-call | flops 1572864 | bytes 18874368 | tf_op jit(solution)/shard_map/pair_sums/pallas_call | solution.py:406
  504.0 57.3 %collective-permute-done.3.b_ref = f32[1536,512]{1,0:T(8,128)S(1)} collective-permute-done((f32[1536,512]{1,0:T(8,128)}, f32[1536,512]{1,0:T(8,128)S(1)}, u32[]{:S(2)}, u32[]{:S(2)}) %collective-permute-start.3) | collective-permute-done | bytes 3145760 | tf_op jit(solution)/shard_map/ppermute | solution.py:481
  561.3 1.9 collective-permute-done.5.d_ref
  563.2 8.4 %finish.1 = (f32[1,1024,512]{2,1,0:T(8,128)}, f32[1,1024,512]{2,1,0:T(8,128)}, f32[1,512,1024]{2,1,0:T(8,128)}) custom-call(f32[1536,512]{1,0:T(8,128)} %get-tuple-element.48.a_ref, f32[1536,512]{1,0:T(8,128)} %copy-done.2, f32[1536,512]{1,0:T(8,128)} %get-tuple-element.51.c_ref, f32[1536,512]{1,0:T(8,128)} %collective-permute-done.5.d_ref), custom_call_target="tpu_custom_call" | custom-call | flops 1572864 | bytes 18874368 | tf_op jit(solution)/shard_map/finish/pallas_call | solution.py:440
  571.6 15.2 %home_sum.2.refs_0_ = f32[1024,2048]{1,0:T(8,128)} custom-call(f32[8,1024]{1,0:T(8,128)} %get-tuple-element.33.slot_ref, bf16[8,256,2048]{2,1,0:T(8,128)(2,1)} %all-to-all-done.4.ret_ref), custom_call_target="tpu_custom_call" | custom-call | flops 8589934592 | bytes 8388608 | tf_op jit(solution)/shard_map/home_sum/pallas_call | solution.py:385
  586.8 15.9 %home_sum.3 = (bf16[1024,1024]{1,0:T(8,128)(2,1)}, bf16[1024,1024]{1,0:T(8,128)(2,1)}) custom-call(f32[8,1024]{1,0:T(8,128)} %get-tuple-element.33.slot_ref, bf16[8,256,2048]{2,1,0:T(8,128)(2,1)} %all-to-all-done.3.ret_ref, f32[1024,2048]{1,0:T(8,128)} %home_sum.2.refs_0_), custom_call_target="tpu_custom_call" | custom-call | flops 8589934592 | bytes 8388608 | tf_op jit(solution)/shard_map/home_sum/pallas_call | solution.py:385
  (17 shorter events, 0.1 us)
Async XLA Ops:
  7.2 132.8 %all-gather.2.cloned.1.call-start = ((), (), s32[]{:S(2)}) async-start(), calls=%async_computation.5 | async-start | bytes 15728640 | tf_op jit(solution)/shard_map/all_gather | solution.py:469
  14.7 19.5 %all-to-all-start = ((f32[8,8,512]{2,1,0:T(8,128)}), f32[8,8,512]{2,1,0:T(8,128)S(1)}, u32[]{:S(2)}, u32[]{:S(2)}) async-start(f32[8,8,512]{2,1,0:T(8,128)} %get-tuple-element.32), calls=%async_computation | async-start | bytes 262144 | tf_op jit(solution)/shard_map/all_to_all | solution.py:466
  34.2 0.7 copy-start.3
  34.9 98.7 %all-to-all-start.2 = ((bf16[8,256,2048]{2,1,0:T(8,128)(2,1)}), bf16[8,256,2048]{2,1,0:T(8,128)(2,1)}, u32[]{:S(2)}, u32[]{:S(2)}) async-start(bf16[8,256,2048]{2,1,0:T(8,128)(2,1)} %pack_rows.2), calls=%async_computation.2 | async-start | bytes 16777216 | tf_op jit(solution)/shard_map/all_to_all | solution.py:466
  53.3 86.1 %copy-start.4 = (s32[4]{0:T(128)S(1)}, s32[4]{0:T(128)}, u32[]{:S(2)}) copy-start(s32[4]{0:T(128)} %constant.22.clone) | copy-start | bytes 52
  133.6 99.7 %all-to-all-start.1 = ((bf16[8,256,2048]{2,1,0:T(8,128)(2,1)}), bf16[8,256,2048]{2,1,0:T(8,128)(2,1)}, u32[]{:S(2)}, u32[]{:S(2)}) async-start(bf16[8,256,2048]{2,1,0:T(8,128)(2,1)} %pack_rows.3), calls=%async_computation.1 | async-start | bytes 16777216 | tf_op jit(solution)/shard_map/all_to_all | solution.py:466
  233.2 114.9 %all-to-all-start.4 = ((bf16[8,256,2048]{2,1,0:T(8,128)(2,1)}), bf16[8,256,2048]{2,1,0:T(8,128)(2,1)}, u32[]{:S(2)}, u32[]{:S(2)}) async-start(bf16[8,256,2048]{2,1,0:T(8,128)(2,1)} %get-tuple-element.41), calls=%async_computation.4 | async-start | bytes 16777216 | tf_op jit(solution)/shard_map/all_to_all | solution.py:466
  348.1 78.3 %copy-start.1 = (f32[1536,512]{1,0:T(8,128)S(1)}, f32[1536,512]{1,0:T(8,128)}, u32[]{:S(2)}) copy-start(f32[1536,512]{1,0:T(8,128)} %get-tuple-element.49) | copy-start | bytes 9437188
  348.1 238.7 %all-to-all-start.3 = ((bf16[8,256,2048]{2,1,0:T(8,128)(2,1)}), bf16[8,256,2048]{2,1,0:T(8,128)(2,1)}, u32[]{:S(2)}, u32[]{:S(2)}) async-start(bf16[8,256,2048]{2,1,0:T(8,128)(2,1)} %get-tuple-element.40), calls=%async_computation.3 | async-start | bytes 16777216 | tf_op jit(solution)/shard_map/all_to_all | solution.py:466
  353.6 72.9 %collective-permute-start.2 = (f32[1536,512]{1,0:T(8,128)}, f32[1536,512]{1,0:T(8,128)S(1)}, u32[]{:S(2)}, u32[]{:S(2)}) collective-permute-start(f32[1536,512]{1,0:T(8,128)} %get-tuple-element.50), channel_id=1, source_target_pairs={{0,8},{8,16},{16,24},{24,0},{1,9},{9,17},{17,25},{25,1},{2,10},{10... | collective-permute-start | bytes 9437192 | tf_op jit(solution)/shard_map/ppermute | solution.py:481
  358.7 72.4 %collective-permute-start.4 = (f32[1536,512]{1,0:T(8,128)}, f32[1536,512]{1,0:T(8,128)S(1)}, u32[]{:S(2)}, u32[]{:S(2)}) collective-permute-start(f32[1536,512]{1,0:T(8,128)} %get-tuple-element.53), channel_id=1, source_target_pairs={{0,24},{8,0},{16,8},{24,16},{1,25},{9,1},{17,9},{25,17},{2,26},{10... | collective-permute-start | bytes 9437192 | tf_op jit(solution)/shard_map/ppermute | solution.py:481
  358.7 137.1 %collective-permute-start = (f32[1536,512]{1,0:T(8,128)}, f32[1536,512]{1,0:T(8,128)}, u32[]{:S(2)}, u32[]{:S(2)}) collective-permute-start(f32[1536,512]{1,0:T(8,128)} %get-tuple-element.45), channel_id=1, source_target_pairs={{0,24},{8,0},{16,8},{24,16},{1,25},{9,1},{17,9},{25,17},{2,26},{10... | collective-permute-start | bytes 9437192 | tf_op jit(solution)/shard_map/ppermute | solution.py:481
  360.0 135.8 %collective-permute-start.1 = (f32[1536,512]{1,0:T(8,128)}, f32[1536,512]{1,0:T(8,128)}, u32[]{:S(2)}, u32[]{:S(2)}) collective-permute-start(f32[1536,512]{1,0:T(8,128)} %get-tuple-element.47), channel_id=1, source_target_pairs={{0,8},{8,16},{16,24},{24,0},{1,9},{9,17},{17,25},{25,1},{2,10},{10... | collective-permute-start | bytes 9437192 | tf_op jit(solution)/shard_map/ppermute | solution.py:481
  426.4 4.6 copy-start
  428.9 132.4 %collective-permute-start.3 = (f32[1536,512]{1,0:T(8,128)}, f32[1536,512]{1,0:T(8,128)S(1)}, u32[]{:S(2)}, u32[]{:S(2)}) collective-permute-start(f32[1536,512]{1,0:T(8,128)} %add.21), channel_id=1, source_target_pairs={{0,8},{8,16},{16,24},{24,0},{1,9},{9,17},{17,25},{25,1},{2,10},{10... | collective-permute-start | bytes 9437192 | tf_op jit(solution)/shard_map/ppermute | solution.py:481
  433.5 129.7 %collective-permute-start.5 = (f32[1536,512]{1,0:T(8,128)}, f32[1536,512]{1,0:T(8,128)}, u32[]{:S(2)}, u32[]{:S(2)}) collective-permute-start(f32[1536,512]{1,0:T(8,128)} %add.22), channel_id=1, source_target_pairs={{0,24},{8,0},{16,8},{24,16},{1,25},{9,1},{17,9},{25,17},{2,26},{10... | collective-permute-start | bytes 9437192 | tf_op jit(solution)/shard_map/ppermute | solution.py:481
  561.3 1.9 copy-start.2
Sparse Core Ops, SparseCore 0:
  14.8 119.8 all-gather.1

commit v7 on v6

--- a/solution.py
+++ b/solution.py
@@ -350,23 +350,11 @@
 
 
 def home_kernel(first, slot_ref, ret_ref, *refs):
-    refs, (ret, sems) = refs[:-2], refs[-2:]
     groups, size, width = ret_ref.shape
-    loads = [pltpu.make_async_copy(ret_ref.at[g], ret.at[g], sems.at[g]) for g in range(groups)]
-
-    @pl.when(pl.program_id(0) == 0)
-    def _():
-        for copy in loads:
-            copy.start()
-
+    acc = refs[0][...] if first else None
     outs = refs[1:] if first else refs
-    acc = refs[0][...] if first else None
     for g in range(groups):
-        @pl.when(pl.program_id(0) == 0)
-        def _(g=g):
-            loads[g].wait()
-
-        part = dot(pick_rows(slot_ref[g:g + 1, :], first, size), ret[g], 0, 0)
+        part = dot(pick_rows(slot_ref[g:g + 1, :], first, size), ret_ref[g], 0, 0)
         acc = part if acc is None else acc + part
     if len(outs) == 1:
         outs[0][...] = acc
@@ -386,10 +374,9 @@
         functools.partial(home_kernel, c * size),
         grid=(tokens // block,),
         out_shape=[jax.ShapeDtypeStruct((tokens, w), t) for w, t in outs],
-        in_specs=[pl.BlockSpec((groups, block), lambda i: (0, i)), pl.BlockSpec(memory_space=pl.ANY)] + [rows(width)] * len(extra),
+        in_specs=[pl.BlockSpec((groups, block), lambda i: (0, i)), pl.BlockSpec(memory_space=pltpu.VMEM)] + [rows(width)] * len(extra),
         out_specs=[rows(w) for w, _ in outs],
-        scratch_shapes=[pltpu.VMEM(ret.shape, BF16), pltpu.SemaphoreType.DMA((groups,))],
-        compiler_params=pltpu.CompilerParams(vmem_limit_bytes=58 * 1024 * 1024),
+        compiler_params=pltpu.CompilerParams(vmem_limit_bytes=48 * 1024 * 1024),
         cost_estimate=pl.CostEstimate(flops=2 * groups * size * tokens * width, bytes_accessed=groups * size * width * 2, transcendentals=0),
         name='home_sum',
     )(slot, ret, *extra)

time: 610 us -> 608 us (level)
  no operation moved by 1% of the time
where the time goes in v7:
time: 608 us; the launch traced here: 607 us
  Pallas kernels  281 us (46%)
  waiting for transfers between devices  269 us (44%)
  starting transfers between devices  37.5 us (6%)
  between operations  14.1 us (2%)
    pallas_call x4, Pallas kernels, run_experts(): pl.pallas_call(functools.partial(expert_kernel, chunk, first, steps, prev...  201 us
    ppermute x6, waiting for transfers between devices, layer(): lax.ppermute(a, 'ing', [(i, (i + d) % inner) for i in range(inner)])  187 us
    all_to_all x5, waiting for transfers between devices, layer(): swap = lambda a: lax.all_to_all(a, 'grp', 0, 0, tiled=True)  81.3 us
    pallas_call x2, Pallas kernels, home_sum(): pl.pallas_call(functools.partial(home_kernel, c * size), grid=(tokens //...  28.6 us
    all_to_all x5, starting transfers between devices, layer(): swap = lambda a: lax.all_to_all(a, 'grp', 0, 0, tiled=True)  28.1 us
    pallas_call x2, Pallas kernels, pack_rows(): pl.pallas_call(functools.partial(pack_kernel, c * size), grid=(groups,),...  26.9 us
  transfers between devices with their start and end apart: 12, of which 6 were waited for; matrix products, arithmetic and copies ran while one was open for 1% of the time, Pallas kernels for 43%

profile of v7, /device:TPU:97, one launch (start us, length us, event | category | flops | bytes accessed | tf_op | source)
XLA Modules:
  0.0 607.1 jit_solution(1802046832750181622)
XLA Ops:
  7.2 0.1 all-gather.2.cloned.1.call-start
  7.2 7.4 %make_tables.1 = (f32[8,1024]{1,0:T(8,128)}, f32[8,8,512]{2,1,0:T(8,128)}, bf16[1,1536,1024]{2,1,0:T(8,128)(2,1)}) custom-call(s32[8,1024]{1,0:T(8,128)} %bitcast.2, f32[8,1024]{1,0:T(8,128)} %bitcast.3, bf16[1,1024,512]{2,1,0:T(8,128)(2,1)} %refs_0_.1, bf16[1,1024,512]{2,1,0:T(8,128)(2,1)} %refs_1_.1, bf16[1,512,1024]{2,1,0:T(8,128)(2,1)} %refs_2_.1), custom_call_target="tpu_custom_call" | custom-call | flops 1073741824 | bytes 262144 | tf_op jit(solution)/shard_map/make_tables/pallas_call | solution.py:92
  14.7 6.0 all-to-all-start
  20.7 13.5 %pack_rows.2 = bf16[8,256,2048]{2,1,0:T(8,128)(2,1)} custom-call(f32[8,1024]{1,0:T(8,128)} %get-tuple-element.33.slot_ref, bf16[1024,1024]{1,0:T(8,128)(2,1)} %x_ref.3, bf16[1024,1024]{1,0:T(8,128)(2,1)} %dy_ref.3), custom_call_target="tpu_custom_call" | custom-call | flops 8589934592 | bytes 8388608 | tf_op jit(solution)/shard_map/pack_rows/pallas_call | solution.py:123
  34.2 0.7 copy-done.4
  34.9 5.0 all-to-all-start.2
  39.9 13.4 %pack_rows.3 = bf16[8,256,2048]{2,1,0:T(8,128)(2,1)} custom-call(f32[8,1024]{1,0:T(8,128)} %get-tuple-element.33.slot_ref, bf16[1024,1024]{1,0:T(8,128)(2,1)} %x_ref.3, bf16[1024,1024]{1,0:T(8,128)(2,1)} %dy_ref.3), custom_call_target="tpu_custom_call" | custom-call | flops 8589934592 | bytes 8388608 | tf_op jit(solution)/shard_map/pack_rows/pallas_call | solution.py:123
  53.3 80.2 %all-to-all-done.2.xd_ref = bf16[8,256,2048]{2,1,0:T(8,128)(2,1)} async-done(((bf16[8,256,2048]{2,1,0:T(8,128)(2,1)}), bf16[8,256,2048]{2,1,0:T(8,128)(2,1)}, u32[]{:S(2)}, u32[]{:S(2)}) %all-to-all-start.2) | async-done | bytes 8388640 | tf_op jit(solution)/shard_map/all_to_all | solution.py:453
  133.6 5.8 all-to-all-start.1
  139.4 0.5 and_select_fusion.order_ref
  139.9 92.2 %run_experts.4 = (bf16[8,256,2048]{2,1,0:T(8,128)(2,1)}, f32[4,1536,1024]{2,1,0:T(8,128)}) custom-call(s32[4]{0:T(128)} %and_select_fusion.order_ref, f32[8,8,512]{2,1,0:T(8,128)} %copy-done.4, bf16[8,256,2048]{2,1,0:T(8,128)(2,1)} %all-to-all-done.2.xd_ref, bf16[4,1536,1024]{2,1,0:T(8,128)(2,1)} %all-gather.2.cloned.1.call-done.w_ref), custom_call_target="tpu_custom_call" | custom-call | flops 47244640256 | bytes 16777216 | tf_op jit(solution)/shard_map/run_experts/pallas_call | solution.py:336
  232.1 1.1 all-to-all-done.1.xd_ref
  233.2 5.8 all-to-all-start.4
  239.0 27.0 %run_experts.5 = (f32[8,256,2048]{2,1,0:T(8,128)}, f32[1536,512]{1,0:T(8,128)}, f32[1536,512]{1,0:T(8,128)}) custom-call(s32[4]{0:T(128)} %and_select_fusion.order_ref, f32[8,8,512]{2,1,0:T(8,128)} %copy-done.4, bf16[8,256,2048]{2,1,0:T(8,128)(2,1)} %all-to-all-done.1.xd_ref, bf16[4,1536,1024]{2,1,0:T(8,128)(2,1)} %all-gather.2.cloned.1.call-done.w_ref, ...), custom_call_target="tpu_custom_call" | custom-call | flops 11811160064 | bytes 16777216 | tf_op jit(solution)/shard_map/run_experts/pallas_call | solution.py:336
  266.0 55.8 %run_experts.6 = (f32[8,256,2048]{2,1,0:T(8,128)}, f32[1536,512]{1,0:T(8,128)}, f32[1536,512]{1,0:T(8,128)}, f32[1536,512]{1,0:T(8,128)}, f32[1536,512]{1,0:T(8,128)}) custom-call(s32[4]{0:T(128)} %and_select_fusion.order_ref, f32[8,8,512]{2,1,0:T(8,128)} %copy-done.4, bf16[8,256,2048]{2,1,0:T(8,128)(2,1)} %all-to-all-done.1.xd_ref, ...), custom_call_target="tpu_custom_call" | custom-call | flops 23622320128 | bytes 16777216 | tf_op jit(solution)/shard_map/run_experts/pallas_call | solution.py:336
  321.7 26.3 %run_experts.7 = (bf16[8,256,2048]{2,1,0:T(8,128)(2,1)}, f32[1536,512]{1,0:T(8,128)}, f32[1536,512]{1,0:T(8,128)}) custom-call(s32[4]{0:T(128)} %and_select_fusion.order_ref, f32[8,8,512]{2,1,0:T(8,128)} %copy-done.4, bf16[8,256,2048]{2,1,0:T(8,128)(2,1)} %all-to-all-done.1.xd_ref, bf16[4,1536,1024]{2,1,0:T(8,128)(2,1)} %all-gather.2.cloned.1.call-done.w_ref, ...), custom_call_target="tpu_custom_call" | custom-call | flops 11811160064 | bytes 16777216 | tf_op jit(solution)/shard_map/run_experts/pallas_call | solution.py:336
  348.1 5.4 all-to-all-start.3
  353.5 5.2 collective-permute-start.2
  358.7 1.1 collective-permute-start
  359.9 0.3 collective-permute-start.1
  360.2 66.3 %collective-permute-done.2 = f32[1536,512]{1,0:T(8,128)S(1)} collective-permute-done((f32[1536,512]{1,0:T(8,128)}, f32[1536,512]{1,0:T(8,128)S(1)}, u32[]{:S(2)}, u32[]{:S(2)}) %collective-permute-start.2) | collective-permute-done | bytes 3145760 | tf_op jit(solution)/shard_map/ppermute | solution.py:468
  426.5 2.4 add.21
  429.0 2.2 collective-permute-start.3
  431.2 2.4 add.22
  433.6 0.5 collective-permute-start.5
  434.0 61.8 %collective-permute-done.b_ref = f32[1536,512]{1,0:T(8,128)} collective-permute-done((f32[1536,512]{1,0:T(8,128)}, f32[1536,512]{1,0:T(8,128)}, u32[]{:S(2)}, u32[]{:S(2)}) %collective-permute-start) | collective-permute-done | bytes 3145760 | tf_op jit(solution)/shard_map/ppermute | solution.py:468
  495.8 8.2 %pair_sums.1 = (f32[1536,512]{1,0:T(8,128)}, f32[1536,512]{1,0:T(8,128)}) custom-call(f32[1536,512]{1,0:T(8,128)} %get-tuple-element.44.a_ref, f32[1536,512]{1,0:T(8,128)} %collective-permute-done.b_ref, f32[1536,512]{1,0:T(8,128)} %get-tuple-element.46.c_ref, f32[1536,512]{1,0:T(8,128)} %collective-permute-done.1.d_ref), custom_call_target="tpu_custom_call" | custom-call | flops 1572864 | bytes 18874368 | tf_op jit(solution)/shard_map/pair_sums/pallas_call | solution.py:393
  504.1 57.3 %collective-permute-done.3.b_ref = f32[1536,512]{1,0:T(8,128)S(1)} collective-permute-done((f32[1536,512]{1,0:T(8,128)}, f32[1536,512]{1,0:T(8,128)S(1)}, u32[]{:S(2)}, u32[]{:S(2)}) %collective-permute-start.3) | collective-permute-done | bytes 3145760 | tf_op jit(solution)/shard_map/ppermute | solution.py:468
  561.3 1.9 collective-permute-done.5.d_ref
  563.3 8.4 %finish.1 = (f32[1,1024,512]{2,1,0:T(8,128)}, f32[1,1024,512]{2,1,0:T(8,128)}, f32[1,512,1024]{2,1,0:T(8,128)}) custom-call(f32[1536,512]{1,0:T(8,128)} %get-tuple-element.48.a_ref, f32[1536,512]{1,0:T(8,128)} %copy-done.3, f32[1536,512]{1,0:T(8,128)} %get-tuple-element.51.c_ref, f32[1536,512]{1,0:T(8,128)} %collective-permute-done.5.d_ref), custom_call_target="tpu_custom_call" | custom-call | flops 1572864 | bytes 18874368 | tf_op jit(solution)/shard_map/finish/pallas_call | solution.py:427
  571.7 14.2 %home_sum.2.refs_0_ = f32[1024,2048]{1,0:T(8,128)} custom-call(f32[8,1024]{1,0:T(8,128)S(1)} %copy-done, bf16[8,256,2048]{2,1,0:T(8,128)(2,1)} %all-to-all-done.4.ret_ref), custom_call_target="tpu_custom_call" | custom-call | flops 8589934592 | bytes 8388608 | tf_op jit(solution)/shard_map/home_sum/pallas_call | solution.py:373
  585.9 14.4 %home_sum.3 = (bf16[1024,1024]{1,0:T(8,128)(2,1)}, bf16[1024,1024]{1,0:T(8,128)(2,1)}) custom-call(f32[8,1024]{1,0:T(8,128)S(1)} %copy-done, bf16[8,256,2048]{2,1,0:T(8,128)(2,1)} %all-to-all-done.3.ret_ref, f32[1024,2048]{1,0:T(8,128)} %home_sum.2.refs_0_), custom_call_target="tpu_custom_call" | custom-call | flops 8589934592 | bytes 8388608 | tf_op jit(solution)/shard_map/home_sum/pallas_call | solution.py:373
  (19 shorter events, 0.1 us)
Async XLA Ops:
  7.2 132.7 %all-gather.2.cloned.1.call-start = ((), (), s32[]{:S(2)}) async-start(), calls=%async_computation.5 | async-start | bytes 15728640 | tf_op jit(solution)/shard_map/all_gather | solution.py:456
  14.7 19.5 %all-to-all-start = ((f32[8,8,512]{2,1,0:T(8,128)}), f32[8,8,512]{2,1,0:T(8,128)S(1)}, u32[]{:S(2)}, u32[]{:S(2)}) async-start(f32[8,8,512]{2,1,0:T(8,128)} %get-tuple-element.32), calls=%async_computation | async-start | bytes 262144 | tf_op jit(solution)/shard_map/all_to_all | solution.py:453
  34.2 0.7 copy-start.4
  34.9 98.7 %all-to-all-start.2 = ((bf16[8,256,2048]{2,1,0:T(8,128)(2,1)}), bf16[8,256,2048]{2,1,0:T(8,128)(2,1)}, u32[]{:S(2)}, u32[]{:S(2)}) async-start(bf16[8,256,2048]{2,1,0:T(8,128)(2,1)} %pack_rows.2), calls=%async_computation.2 | async-start | bytes 16777216 | tf_op jit(solution)/shard_map/all_to_all | solution.py:453
  53.3 86.1 %copy-start.5 = (s32[4]{0:T(128)S(1)}, s32[4]{0:T(128)}, u32[]{:S(2)}) copy-start(s32[4]{0:T(128)} %constant.22.clone) | copy-start | bytes 52
  133.6 99.7 %all-to-all-start.1 = ((bf16[8,256,2048]{2,1,0:T(8,128)(2,1)}), bf16[8,256,2048]{2,1,0:T(8,128)(2,1)}, u32[]{:S(2)}, u32[]{:S(2)}) async-start(bf16[8,256,2048]{2,1,0:T(8,128)(2,1)} %pack_rows.3), calls=%async_computation.1 | async-start | bytes 16777216 | tf_op jit(solution)/shard_map/all_to_all | solution.py:453
  233.2 114.9 %all-to-all-start.4 = ((bf16[8,256,2048]{2,1,0:T(8,128)(2,1)}), bf16[8,256,2048]{2,1,0:T(8,128)(2,1)}, u32[]{:S(2)}, u32[]{:S(2)}) async-start(bf16[8,256,2048]{2,1,0:T(8,128)(2,1)} %get-tuple-element.41), calls=%async_computation.4 | async-start | bytes 16777216 | tf_op jit(solution)/shard_map/all_to_all | solution.py:453
  348.1 78.4 %copy-start.2 = (f32[1536,512]{1,0:T(8,128)S(1)}, f32[1536,512]{1,0:T(8,128)}, u32[]{:S(2)}) copy-start(f32[1536,512]{1,0:T(8,128)} %get-tuple-element.49) | copy-start | bytes 9437188
  348.1 237.8 %all-to-all-start.3 = ((bf16[8,256,2048]{2,1,0:T(8,128)(2,1)}), bf16[8,256,2048]{2,1,0:T(8,128)(2,1)}, u32[]{:S(2)}, u32[]{:S(2)}) async-start(bf16[8,256,2048]{2,1,0:T(8,128)(2,1)} %get-tuple-element.40), calls=%async_computation.3 | async-start | bytes 16777216 | tf_op jit(solution)/shard_map/all_to_all | solution.py:453
  353.5 73.0 %collective-permute-start.2 = (f32[1536,512]{1,0:T(8,128)}, f32[1536,512]{1,0:T(8,128)S(1)}, u32[]{:S(2)}, u32[]{:S(2)}) collective-permute-start(f32[1536,512]{1,0:T(8,128)} %get-tuple-element.50), channel_id=1, source_target_pairs={{0,8},{8,16},{16,24},{24,0},{1,9},{9,17},{17,25},{25,1},{2,10},{10... | collective-permute-start | bytes 9437192 | tf_op jit(solution)/shard_map/ppermute | solution.py:468
  358.7 72.4 %collective-permute-start.4 = (f32[1536,512]{1,0:T(8,128)}, f32[1536,512]{1,0:T(8,128)S(1)}, u32[]{:S(2)}, u32[]{:S(2)}) collective-permute-start(f32[1536,512]{1,0:T(8,128)} %get-tuple-element.53), channel_id=1, source_target_pairs={{0,24},{8,0},{16,8},{24,16},{1,25},{9,1},{17,9},{25,17},{2,26},{10... | collective-permute-start | bytes 9437192 | tf_op jit(solution)/shard_map/ppermute | solution.py:468
  358.7 137.1 %collective-permute-start = (f32[1536,512]{1,0:T(8,128)}, f32[1536,512]{1,0:T(8,128)}, u32[]{:S(2)}, u32[]{:S(2)}) collective-permute-start(f32[1536,512]{1,0:T(8,128)} %get-tuple-element.45), channel_id=1, source_target_pairs={{0,24},{8,0},{16,8},{24,16},{1,25},{9,1},{17,9},{25,17},{2,26},{10... | collective-permute-start | bytes 9437192 | tf_op jit(solution)/shard_map/ppermute | solution.py:468
  359.9 136.0 %collective-permute-start.1 = (f32[1536,512]{1,0:T(8,128)}, f32[1536,512]{1,0:T(8,128)}, u32[]{:S(2)}, u32[]{:S(2)}) collective-permute-start(f32[1536,512]{1,0:T(8,128)} %get-tuple-element.47), channel_id=1, source_target_pairs={{0,8},{8,16},{16,24},{24,0},{1,9},{9,17},{17,25},{25,1},{2,10},{10... | collective-permute-start | bytes 9437192 | tf_op jit(solution)/shard_map/ppermute | solution.py:468
  426.5 4.7 copy-start.1
  429.0 132.4 %collective-permute-start.3 = (f32[1536,512]{1,0:T(8,128)}, f32[1536,512]{1,0:T(8,128)S(1)}, u32[]{:S(2)}, u32[]{:S(2)}) collective-permute-start(f32[1536,512]{1,0:T(8,128)} %add.21), channel_id=1, source_target_pairs={{0,8},{8,16},{16,24},{24,0},{1,9},{9,17},{17,25},{25,1},{2,10},{10... | collective-permute-start | bytes 9437192 | tf_op jit(solution)/shard_map/ppermute | solution.py:468
  433.6 129.7 %collective-permute-start.5 = (f32[1536,512]{1,0:T(8,128)}, f32[1536,512]{1,0:T(8,128)}, u32[]{:S(2)}, u32[]{:S(2)}) collective-permute-start(f32[1536,512]{1,0:T(8,128)} %add.22), channel_id=1, source_target_pairs={{0,24},{8,0},{16,8},{24,16},{1,25},{9,1},{17,9},{25,17},{2,26},{10... | collective-permute-start | bytes 9437192 | tf_op jit(solution)/shard_map/ppermute | solution.py:468
  561.3 1.9 copy-start.3
  563.3 8.4 %copy-start = (f32[8,1024]{1,0:T(8,128)S(1)}, f32[8,1024]{1,0:T(8,128)}, u32[]{:S(2)}) copy-start(f32[8,1024]{1,0:T(8,128)} %get-tuple-element.33.slot_ref) | copy-start | bytes 98308
Sparse Core Ops, SparseCore 0:
  14.8 119.8 all-gather.1
